TPU v7x, 256 devices: a whole 4x4x8 slice. The times are simulated.
256 devices in a mesh: rows: 64 (over z, y, core), cols: 4 (over x).
Axes of the slice: x: 4, y: 4, z: 8, core: 2. Of those that a mesh axis runs over, the one named last changes fastest.
Arguments:
- adjacency_tiles: bfloat16 [1536, 12, 128, 128], P(('rows', 'cols')), may hold values from 2.170139e-08 to 0.25
- col_block: int32 [1536, 12], P(('rows', 'cols')), may hold values from 0 to 1535, as said below
- label_prior: float32 [196608, 256], P(('rows', 'cols')), may hold values from 0.05 to 20.1
- seed_label: int32 [196608], P(('rows', 'cols')), may hold values from 0 to 255
- seed_mask: int32 [196608], P(('rows', 'cols')), may hold values 0 or 1
Outputs:
- labels: float32 [196608, 256], P(('rows', 'cols'))
Inputs may be any that keep to these rules, and one draw needn't show every extreme that they name: Row block b is held by device b // 6 of rows+cols, whose rows group is b // (6 * 4). col_block[b, 0] = b. For each device, all its tiles that reference blocks of another rows group reference one and the same block of that group, and each device references every rows group.
All inputs are finite; a program needn't handle non-finite values. No bound on the sum of `seed_mask` on one device may be relied on, other than what follows from the above.
Results may differ from a plain program's by a relative error of at most 0.00041.
Values may be sent and summed in bfloat16 or wider, within the bound.
No kernel may reach another device: no remote copies, remote signals or barrier semaphores. Data moves between devices by JAX's collectives and lax.ppermute only.
A program may use at most 64 MiB of HBM per device.

v0:
```python
import jax
import jax.numpy as jnp
from jax import lax
from jax.sharding import PartitionSpec as P

HOPS = 4


ALPHA = 0.85
SEED_BOOST = 8.0


def sent_to_all(value, axis):
    length = lax.axis_size(axis)
    return lax.all_to_all(
        jnp.broadcast_to(value[None], (length, *value.shape)), axis, 0, 0, tiled=True
    )


def joined_along(parts, dim):
    parts = jnp.moveaxis(parts, 0, dim)
    shape = parts.shape
    return parts.reshape(*shape[:dim], shape[dim] * shape[dim + 1], *shape[dim + 2 :])


def gather_directly(value, axis, dim):
    parts = sent_to_all(value, axis)
    return joined_along(parts, dim)


def prepare(label_prior, seed_label, seed_mask):
    classes = label_prior.shape[1]
    one_hot = (seed_label[:, None] == jnp.arange(classes, dtype=jnp.int32)[None, :]).astype(
        jnp.float32
    )
    anchor_raw = label_prior + SEED_BOOST * seed_mask[:, None].astype(jnp.float32) * one_hot
    return anchor_raw * (classes / jnp.sum(anchor_raw, axis=1, keepdims=True))


def ask_blocks(owner_group, within, own_group, n_rows):
    group_ids = jnp.arange(n_rows, dtype=jnp.int32)
    matched = owner_group.reshape(-1)[:, None] == group_ids[None, :]
    wanted = jnp.max(jnp.where(matched, within.reshape(-1)[:, None], 0), axis=0)
    wanted = jnp.where(group_ids == own_group, 0, wanted)
    return lax.all_to_all(
        wanted.reshape(n_rows, 1), "rows", split_axis=0, concat_axis=0, tiled=True
    )


def local(adjacency_tiles, col_block, label_prior, seed_label, seed_mask):
    blocks_dev = adjacency_tiles.shape[0]
    degree = adjacency_tiles.shape[1]
    block_rows = adjacency_tiles.shape[2]
    classes = label_prior.shape[1]
    n_rows = lax.axis_size("rows")
    n_cols = lax.axis_size("cols")
    group_size = n_cols * blocks_dev
    own_group = lax.axis_index("rows")
    owner_group = col_block // group_size
    within = col_block % group_size
    table_index = jnp.where(owner_group == own_group, within, group_size + owner_group).reshape(-1)
    anchor = prepare(label_prior, seed_label, seed_mask)
    labels = anchor
    for hop_index in range(HOPS):
        asked = ask_blocks(owner_group, within, own_group, n_rows)
        sent_blocks = labels.astype(jnp.bfloat16).reshape(blocks_dev, block_rows, classes)
        group_blocks = gather_directly(sent_blocks, "cols", 0)
        reply = group_blocks[asked[:, 0]]
        remote = lax.all_to_all(reply, "rows", split_axis=0, concat_axis=0, tiled=True)
        table = jnp.concatenate([group_blocks, remote], axis=0)
        operand = table[table_index].reshape(blocks_dev, degree, block_rows, classes)
        spread = jnp.einsum(
            "bkij,bkjc->bic", adjacency_tiles, operand, preferred_element_type=jnp.float32
        )
        spread = spread.reshape(blocks_dev * block_rows, classes)
        blended = ALPHA * spread + (1.0 - ALPHA) * anchor
        labels = blended * (classes / jnp.sum(blended, axis=1, keepdims=True))
    return labels


def solution(mesh):
    in_specs = (
        P(("rows", "cols"), None, None, None),
        P(("rows", "cols"), None),
        P(("rows", "cols"), None),
        P(("rows", "cols")),
        P(("rows", "cols")),
    )
    out_specs = P(("rows", "cols"), None)
    return jax.shard_map(local, mesh=mesh, in_specs=in_specs, out_specs=out_specs, check_vma=False)
```

profile of v0, /device:TPU:8, one launch (start us, length us, event | category | flops | bytes accessed | tf_op | source)
XLA Modules:
  0.0 612.2 jit_solution(2709465145339446009)
XLA Ops:
  0.0 0.9 add_select_fusion.2
  0.9 0.1 eq.37
  1.0 0.1 select_reduce_fusion
  1.1 0.7 copy.8
  1.9 12.1 %all-to-all-start.1 = ((s32[64,1,1]{2,1,0:T(1,128)}), s32[64,1,1]{2,1,0:T(1,128)S(1)}, u32[]{:S(2)}, u32[]{:S(2)}) async-start(s32[64,1,1]{2,1,0:T(1,128)} %copy.8), calls=%async_computation.1 | async-start | bytes 65536 | tf_op jit(solution)/shard_map/all_to_all | solution.py:45
  14.0 0.7 convert_multiply_fusion
  14.7 1.5 fusion.11
  16.2 1.5 multiply_convert_fusion.3
  17.7 4.8 all-to-all-done.1
  22.5 1.3 broadcast_in_dim.84
  23.8 4.3 all-to-all-start
  28.2 1.2 reduce
  29.4 19.8 %all-to-all-done = bf16[4,6,128,256]{3,2,1,0:T(8,128)(2,1)} async-done(((bf16[4,6,128,256]{3,2,1,0:T(8,128)(2,1)}), bf16[4,6,128,256]{3,2,1,0:T(8,128)(2,1)}, u32[]{:S(2)}, u32[]{:S(2)}) %all-to-all-start) | async-done | bytes 1572896 | tf_op jit(solution)/shard_map/all_to_all | solution.py:15
  49.3 4.1 gather_fusion
  53.4 6.5 %all-to-all-start.2 = ((bf16[64,128,256]{2,1,0:T(8,128)(2,1)}), bf16[64,128,256]{2,1,0:T(8,128)(2,1)}, u32[]{:S(2)}, u32[]{:S(2)}) async-start(bf16[64,128,256]{2,1,0:T(8,128)(2,1)} %gather_fusion), calls=%async_computation.2 | async-start | bytes 8388608 | tf_op jit(solution)/shard_map/all_to_all | solution.py:69
  60.0 96.1 %all-to-all-done.2 = bf16[64,128,256]{2,1,0:T(8,128)(2,1)} async-done(((bf16[64,128,256]{2,1,0:T(8,128)(2,1)}), bf16[64,128,256]{2,1,0:T(8,128)(2,1)}, u32[]{:S(2)}, u32[]{:S(2)}) %all-to-all-start.2) | async-done | bytes 4194336 | tf_op jit(solution)/shard_map/all_to_all | solution.py:69
  156.1 5.6 pad_maximum_fusion
  161.7 8.2 %gather_fusion.1 = bf16[72,128,256]{2,1,0:T(8,128)(2,1)} fusion(bf16[88,128,256]{2,1,0:T(8,128)(2,1)} %pad_maximum_fusion, s32[1024]{0:T(1024)S(1)} %pad_clamp_fusion), kind=kCustom, calls=%fused_computation.1 | custom fusion | bytes 9437472 | tf_op jit(solution)/shard_map/gather | solution.py:71
  169.9 3.3 fusion
  173.3 0.5 fusion.4
  173.8 0.5 multiply_convert_fusion.2
  174.3 0.2 broadcast_in_dim.91
  174.5 22.0 %all_to_all.52 = bf16[4,6,128,256]{3,2,1,0:T(8,128)(2,1)} all-to-all(bf16[4,6,128,256]{3,2,1,0:T(8,128)(2,1)S(1)} %broadcast_in_dim.91), channel_id=1, replica_groups=mesh['rows'=64,'cols'=4] {'cols'}, dimensions={0} | all-to-all | bytes 3145728 | tf_op jit(solution)/shard_map/all_to_all | solution.py:15
  196.5 4.1 gather_fusion.2
  200.6 104.1 %all_to_all.53 = bf16[64,128,256]{2,1,0:T(8,128)(2,1)S(1)} all-to-all(bf16[64,128,256]{2,1,0:T(8,128)(2,1)} %gather_fusion.2), channel_id=1, replica_groups=mesh['rows'=64,'cols'=4] {'rows'}, dimensions={0} | all-to-all | bytes 8388608 | tf_op jit(solution)/shard_map/all_to_all | solution.py:69
  304.7 3.0 pad_maximum_fusion.1
  307.7 8.2 %gather_fusion.3 = bf16[72,128,256]{2,1,0:T(8,128)(2,1)} fusion(bf16[88,128,256]{2,1,0:T(8,128)(2,1)} %pad_maximum_fusion.1, s32[1024]{0:T(1024)S(1)} %pad_clamp_fusion), kind=kCustom, calls=%fused_computation.3 | custom fusion | bytes 9437472 | tf_op jit(solution)/shard_map/gather | solution.py:71
  315.9 3.2 fusion.1
  319.1 0.5 fusion.5
  319.6 0.5 multiply_convert_fusion.1
  320.2 0.2 broadcast_in_dim.93
  320.3 22.7 %all_to_all.54 = bf16[4,6,128,256]{3,2,1,0:T(8,128)(2,1)} all-to-all(bf16[4,6,128,256]{3,2,1,0:T(8,128)(2,1)S(1)} %broadcast_in_dim.93), channel_id=1, replica_groups=mesh['rows'=64,'cols'=4] {'cols'}, dimensions={0} | all-to-all | bytes 3145728 | tf_op jit(solution)/shard_map/all_to_all | solution.py:15
  343.0 4.1 gather_fusion.4
  347.1 103.1 %all_to_all.55 = bf16[64,128,256]{2,1,0:T(8,128)(2,1)S(1)} all-to-all(bf16[64,128,256]{2,1,0:T(8,128)(2,1)} %gather_fusion.4), channel_id=1, replica_groups=mesh['rows'=64,'cols'=4] {'rows'}, dimensions={0} | all-to-all | bytes 8388608 | tf_op jit(solution)/shard_map/all_to_all | solution.py:69
  450.3 3.0 pad_maximum_fusion.2
  453.3 8.2 %gather_fusion.5 = bf16[72,128,256]{2,1,0:T(8,128)(2,1)} fusion(bf16[88,128,256]{2,1,0:T(8,128)(2,1)} %pad_maximum_fusion.2, s32[1024]{0:T(1024)S(1)} %pad_clamp_fusion), kind=kCustom, calls=%fused_computation.5 | custom fusion | bytes 9437472 | tf_op jit(solution)/shard_map/gather | solution.py:71
  461.4 3.2 fusion.2
  464.7 0.5 fusion.6
  465.2 0.5 multiply_convert_fusion
  465.7 0.2 broadcast_in_dim.95
  465.9 22.7 %all_to_all.56 = bf16[4,6,128,256]{3,2,1,0:T(8,128)(2,1)} all-to-all(bf16[4,6,128,256]{3,2,1,0:T(8,128)(2,1)S(1)} %broadcast_in_dim.95), channel_id=1, replica_groups=mesh['rows'=64,'cols'=4] {'cols'}, dimensions={0} | all-to-all | bytes 3145728 | tf_op jit(solution)/shard_map/all_to_all | solution.py:15
  488.6 4.1 gather_fusion.6
  492.7 103.1 %all_to_all.57 = bf16[64,128,256]{2,1,0:T(8,128)(2,1)S(1)} all-to-all(bf16[64,128,256]{2,1,0:T(8,128)(2,1)} %gather_fusion.6), channel_id=1, replica_groups=mesh['rows'=64,'cols'=4] {'rows'}, dimensions={0} | all-to-all | bytes 8388608 | tf_op jit(solution)/shard_map/all_to_all | solution.py:69
  595.9 3.0 pad_maximum_fusion.3
  598.9 8.2 %gather_fusion.7 = bf16[72,128,256]{2,1,0:T(8,128)(2,1)} fusion(bf16[88,128,256]{2,1,0:T(8,128)(2,1)} %pad_maximum_fusion.3, s32[1024]{0:T(1024)S(1)} %pad_clamp_fusion), kind=kCustom, calls=%fused_computation.7 | custom fusion | bytes 9437472 | tf_op jit(solution)/shard_map/gather | solution.py:71
  607.0 3.2 fusion.3
  610.3 0.5 fusion.7
  610.8 1.4 broadcast_multiply_fusion
  (24 shorter events, 0.2 us)
Async XLA Ops:
  0.0 169.9 %copy-start = (bf16[6,12,128,128]{3,2,1,0:T(8,128)(2,1)S(1)}, bf16[6,12,128,128]{3,2,1,0:T(8,128)(2,1)}, u32[]{:S(2)}) copy-start(bf16[6,12,128,128]{3,2,1,0:T(8,128)(2,1)} %param.5) | copy-start | bytes 7077892
  1.9 20.7 %all-to-all-start.1 = ((s32[64,1,1]{2,1,0:T(1,128)}), s32[64,1,1]{2,1,0:T(1,128)S(1)}, u32[]{:S(2)}, u32[]{:S(2)}) async-start(s32[64,1,1]{2,1,0:T(1,128)} %copy.8), calls=%async_computation.1 | async-start | bytes 65536 | tf_op jit(solution)/shard_map/all_to_all | solution.py:45
  23.8 25.4 %all-to-all-start = ((bf16[4,6,128,256]{3,2,1,0:T(8,128)(2,1)}), bf16[4,6,128,256]{3,2,1,0:T(8,128)(2,1)}, u32[]{:S(2)}, u32[]{:S(2)}) async-start(bf16[4,6,128,256]{3,2,1,0:T(8,128)(2,1)} %broadcast_in_dim.84), calls=%async_computation | async-start | bytes 3145728 | tf_op jit(solution)/shard_map/all_to_all | solution.py:15
  53.4 102.7 %all-to-all-start.2 = ((bf16[64,128,256]{2,1,0:T(8,128)(2,1)}), bf16[64,128,256]{2,1,0:T(8,128)(2,1)}, u32[]{:S(2)}, u32[]{:S(2)}) async-start(bf16[64,128,256]{2,1,0:T(8,128)(2,1)} %gather_fusion), calls=%async_computation.2 | async-start | bytes 8388608 | tf_op jit(solution)/shard_map/all_to_all | solution.py:69
  169.9 3.3 copy-start.1
  169.9 3.3 copy-start.5
  200.6 104.1 %copy-start.3 = (bf16[4,6,128,256]{3,2,1,0:T(8,128)(2,1)S(1)}, bf16[4,6,128,256]{3,2,1,0:T(8,128)(2,1)}, u32[]{:S(2)}) copy-start(bf16[4,6,128,256]{3,2,1,0:T(8,128)(2,1)} %all_to_all.52) | copy-start | bytes 4718596
  347.1 103.1 %copy-start.4 = (bf16[4,6,128,256]{3,2,1,0:T(8,128)(2,1)S(1)}, bf16[4,6,128,256]{3,2,1,0:T(8,128)(2,1)}, u32[]{:S(2)}) copy-start(bf16[4,6,128,256]{3,2,1,0:T(8,128)(2,1)} %all_to_all.54) | copy-start | bytes 4718596
  492.7 103.1 %copy-start.2 = (bf16[4,6,128,256]{3,2,1,0:T(8,128)(2,1)S(1)}, bf16[4,6,128,256]{3,2,1,0:T(8,128)(2,1)}, u32[]{:S(2)}) copy-start(bf16[4,6,128,256]{3,2,1,0:T(8,128)(2,1)} %all_to_all.56) | copy-start | bytes 4718596
where the time goes:
time: 613 us; the launch traced here: 612 us
  blocking collectives  378 us (62%)
  waiting for transfers between devices  121 us (20%)
  local copies, waits for them, and re-layouts  52.1 us (8%)
  other arithmetic  25.6 us (4%)
  starting transfers between devices  22.9 us (4%)
  matrix products  13 us (2%)
    all_to_all x3, blocking collectives, local(): lax.all_to_all(reply, 'rows', split_axis=0, concat_axis=0, tiled=True)  310 us
    all_to_all x1, waiting for transfers between devices, local(): lax.all_to_all(reply, 'rows', split_axis=0, concat_axis=0, tiled=True)  96.1 us
    all_to_all x3, blocking collectives, sent_to_all(): lax.all_to_all(jnp.broadcast_to(value[None], (length, *value.shape)), axi...  67.3 us
    gather x4, local copies, waits for them, and re-layouts, local(): table[table_index].reshape(blocks_dev, degree, block_rows, classes)  32.7 us
    all_to_all x1, waiting for transfers between devices, sent_to_all(): lax.all_to_all(jnp.broadcast_to(value[None], (length, *value.shape)), axi...  19.8 us
    gather x4, local copies, waits for them, and re-layouts, local(): reply = group_blocks[asked[:, 0]]  16.6 us
    concatenate x4, other arithmetic, local(): table = jnp.concatenate([group_blocks, remote], axis=0)  14.6 us
    dot_general x4, matrix products, local(): jnp.einsum('bkij,bkjc->bic', adjacency_tiles, operand, preferred_element_...  13 us
  transfers between devices with their start and end apart: 3, of which 3 were waited for; matrix products, arithmetic and copies ran while one was open for 1% of the time, Pallas kernels for 0%

commit v1 on v0

v1 whole, which is shorter than its diff:
```python
import functools

import jax
import jax.numpy as jnp
from jax import lax
from jax.experimental import pallas as pl
from jax.experimental.pallas import tpu as pltpu
from jax.sharding import PartitionSpec as P

HOPS = 4
PARTS = 2


ALPHA = 0.85
SEED_BOOST = 8.0

ANY = pl.BlockSpec(memory_space=pl.ANY)
VMEM = pl.BlockSpec(memory_space=pltpu.VMEM)
SMEM = pl.BlockSpec(memory_space=pltpu.SMEM)


def prepare(label_prior, seed_label, seed_mask):
    classes = label_prior.shape[1]
    one_hot = (seed_label[:, None] == jnp.arange(classes, dtype=jnp.int32)[None, :]).astype(
        jnp.float32
    )
    anchor_raw = label_prior + SEED_BOOST * seed_mask[:, None].astype(jnp.float32) * one_hot
    return anchor_raw * (classes / jnp.sum(anchor_raw, axis=1, keepdims=True))


def ask_blocks(owner_group, within, own_group, n_rows):
    group_ids = jnp.arange(n_rows, dtype=jnp.int32)
    matched = owner_group.reshape(-1)[:, None] == group_ids[None, :]
    wanted = jnp.max(jnp.where(matched, within.reshape(-1)[:, None], 0), axis=0)
    wanted = jnp.where(group_ids == own_group, 0, wanted)
    return lax.all_to_all(
        wanted.reshape(n_rows, 1), "rows", split_axis=0, concat_axis=0, tiled=True
    )


def reply_kernel(asked_ref, *refs, n_cols):
    parts, out_ref, table, in_sems, out_sem = refs[:n_cols], refs[n_cols], *refs[n_cols + 1 :]
    blocks_dev = parts[0].shape[0]
    n = out_ref.shape[0]
    loads = [
        pltpu.make_async_copy(p, table.at[pl.ds(i * blocks_dev, blocks_dev)], in_sems.at[i])
        for i, p in enumerate(parts)
    ]
    for c in loads:
        c.start()
    for c in loads:
        c.wait()

    @pl.loop(0, n)
    def _(i):
        pltpu.make_async_copy(table.at[asked_ref[i]], out_ref.at[i], out_sem).start()

    pltpu.make_async_copy(out_ref, out_ref, out_sem).wait()


def reply_blocks(asked, parts):
    blocks_dev, block, width = parts[0].shape
    n = asked.shape[0]
    n_cols = len(parts)
    size = block * width * 2
    return pl.pallas_call(
        functools.partial(reply_kernel, n_cols=n_cols),
        out_shape=jax.ShapeDtypeStruct((n, block, width), jnp.bfloat16),
        in_specs=[SMEM] + [ANY] * n_cols,
        out_specs=ANY,
        scratch_shapes=[
            pltpu.VMEM((n_cols * blocks_dev, block, width), jnp.bfloat16),
            pltpu.SemaphoreType.DMA((n_cols,)),
            pltpu.SemaphoreType.DMA,
        ],
        cost_estimate=pl.CostEstimate(
            flops=4_000_000, bytes_accessed=(n + n_cols * blocks_dev) * size, transcendentals=0
        ),
        name="reply",
    )(asked, *parts)


def spread_kernel(index_ref, tiles_ref, weight_ref, anchor_ref, *refs, n_src):
    sources, out_ref, table, sems = refs[:n_src], refs[n_src], *refs[n_src + 1 :]
    blocks_dev, degree, block, _ = tiles_ref.shape
    loads, at = [], 0
    for i, s in enumerate(sources):
        loads.append(pltpu.make_async_copy(s, table.at[pl.ds(at, s.shape[0])], sems.at[i]))
        at += s.shape[0]
    for c in loads:
        c.start()
    for c in loads:
        c.wait()

    @pl.loop(0, blocks_dev)
    def _(b):
        total = None
        for k in range(0, degree, 2):
            left = jnp.concatenate([tiles_ref[b, k], tiles_ref[b, k + 1]], axis=1)
            right = jnp.concatenate(
                [table[index_ref[b * degree + k]], table[index_ref[b * degree + k + 1]]], axis=0
            )
            term = jnp.dot(left, right, preferred_element_type=jnp.float32)
            total = term if total is None else total + term
        rows = pl.ds(pl.multiple_of(b * block, block), block)
        out_ref[rows, :] = (weight_ref[rows, :] * total + anchor_ref[rows, :]).astype(out_ref.dtype)


def spread_blocks(index, tiles, weight, anchor, sources, dtype):
    blocks_dev, degree, block, _ = tiles.shape
    width = anchor.shape[1]
    n_src = len(sources)
    total = sum(s.shape[0] for s in sources)
    return pl.pallas_call(
        functools.partial(spread_kernel, n_src=n_src),
        out_shape=jax.ShapeDtypeStruct((blocks_dev * block, width), dtype),
        in_specs=[SMEM, VMEM, VMEM, VMEM] + [ANY] * n_src,
        out_specs=VMEM,
        scratch_shapes=[
            pltpu.VMEM((total, block, width), jnp.bfloat16),
            pltpu.SemaphoreType.DMA((n_src,)),
        ],
        cost_estimate=pl.CostEstimate(
            flops=2 * blocks_dev * degree * block * block * width,
            bytes_accessed=total * block * width * 2 + tiles.size * 2,
            transcendentals=0,
        ),
        name="spread",
    )(index, tiles, weight, anchor, *sources)


def local(adjacency_tiles, col_block, label_prior, seed_label, seed_mask):
    blocks_dev, degree, block, _ = adjacency_tiles.shape
    classes = label_prior.shape[1]
    width = classes // PARTS
    n_rows = lax.axis_size("rows")
    n_cols = lax.axis_size("cols")
    group_size = n_cols * blocks_dev
    own_group = lax.axis_index("rows")
    own_col = lax.axis_index("cols")
    owner_group = col_block // group_size
    within = col_block % group_size

    def from_here(w):
        return (w // blocks_dev + n_cols - own_col) % n_cols * blocks_dev + w % blocks_dev

    index = jnp.where(
        owner_group == own_group, from_here(within), group_size + owner_group
    ).reshape(-1)
    asked = from_here(ask_blocks(owner_group, within, own_group, n_rows)[:, 0])
    anchor = prepare(label_prior, seed_label, seed_mask)

    row_sum = jnp.sum(adjacency_tiles.astype(jnp.float32), axis=(1, 3)).reshape(-1, 1)
    scale = 1.0 / (ALPHA * row_sum + (1.0 - ALPHA))
    weight = jnp.broadcast_to(ALPHA * scale, (blocks_dev * block, width))

    ranges = [slice(p * width, (p + 1) * width) for p in range(PARTS)]
    anchors = [(1.0 - ALPHA) * scale * anchor[:, r] for r in ranges]
    sent = [anchor[:, r].astype(jnp.bfloat16) for r in ranges]
    blended = [None] * PARTS
    for hop in range(HOPS):
        last = hop == HOPS - 1
        for p in range(PARTS):
            own = sent[p].reshape(blocks_dev, block, width)
            parts = [own] + [
                lax.ppermute(own, "cols", [((x + d) % n_cols, x) for x in range(n_cols)])
                for d in range(1, n_cols)
            ]
            reply = reply_blocks(asked, parts)
            remote = lax.all_to_all(reply, "rows", split_axis=0, concat_axis=0, tiled=True)
            blended[p] = spread_blocks(
                index, adjacency_tiles, weight, anchors[p], parts + [remote],
                jnp.float32 if last else jnp.bfloat16,
            )
        sent = blended
    labels = jnp.concatenate(blended, axis=1)
    return labels * (classes / jnp.sum(labels, axis=1, keepdims=True))


def solution(mesh):
    in_specs = (
        P(("rows", "cols"), None, None, None),
        P(("rows", "cols"), None),
        P(("rows", "cols"), None),
        P(("rows", "cols")),
        P(("rows", "cols")),
    )
    out_specs = P(("rows", "cols"), None)
    return jax.shard_map(local, mesh=mesh, in_specs=in_specs, out_specs=out_specs, check_vma=False)
```

time: 613 us -> 511 us (0.83)
  blocking collectives: 378 us -> 0 us
  waiting for transfers between devices: 121 us -> 322 us
  Pallas kernels: 0 us -> 75.2 us
  starting transfers between devices: 22.9 us -> 83.8 us
  local copies, waits for them, and re-layouts: 52.1 us -> 12.7 us
  matrix products: 13 us -> 0 us
  other arithmetic: 25.6 us -> 14.6 us
    all_to_all x6 -> x0, blocking collectives: 378 us -> none  [the longest x3 310 us: local(): lax.all_to_all(reply, 'rows', split_axis=0, concat_axis=0, tiled=True)]
    all_to_all x1 -> x8, waiting for transfers between devices: 96.1 us -> 241 us  [local(): lax.all_to_all(reply, 'rows', split_axis=0, concat_axis=0, tiled=True)]
    ppermute x0 -> x24, waiting for transfers between devices: none -> 81.5 us  [local(): lax.ppermute(own, 'cols', [((x + d) % n_cols, x) for x in range(n_cols)])]
    pallas_call x0 -> x16, Pallas kernels: none -> 75.2 us  [the longest x8 49 us: spread_blocks(): pl.pallas_call(functools.partial(spread_kernel, n_src=n_src), out_shape=j...]
    gather x8 -> x0, local copies, waits for them, and re-layouts: 49.3 us -> none  [the longest x4 32.7 us: local(): table[table_index].reshape(blocks_dev, degree, block_rows, classes)]
    all_to_all x1 -> x8, starting transfers between devices: 6.46 us -> 49.3 us  [local(): lax.all_to_all(reply, 'rows', split_axis=0, concat_axis=0, tiled=True)]
    ppermute x0 -> x24, starting transfers between devices: none -> 22.4 us  [local(): lax.ppermute(own, 'cols', [((x + d) % n_cols, x) for x in range(n_cols)])]
    all_to_all x1 -> x0, waiting for transfers between devices: 19.8 us -> none  [sent_to_all(): lax.all_to_all(jnp.broadcast_to(value[None], (length, *value.shape)), axi...]
  transfers between devices with their start and end apart: 3 -> 33, of which waited for: 3 -> 32; matrix products, arithmetic and copies ran while one was open for 1% -> 2% of each run, Pallas kernels for 0% -> 13%
where the time goes in v1:
time: 511 us; the launch traced here: 509 us
  waiting for transfers between devices  322 us (63%)
  starting transfers between devices  83.8 us (16%)
  Pallas kernels  75.2 us (15%)
  other arithmetic  14.6 us (3%)
  local copies, waits for them, and re-layouts  12.7 us (2%)
    all_to_all x8, waiting for transfers between devices, local(): lax.all_to_all(reply, 'rows', split_axis=0, concat_axis=0, tiled=True)  241 us
    ppermute x24, waiting for transfers between devices, local(): lax.ppermute(own, 'cols', [((x + d) % n_cols, x) for x in range(n_cols)])  81.5 us
    all_to_all x8, starting transfers between devices, local(): lax.all_to_all(reply, 'rows', split_axis=0, concat_axis=0, tiled=True)  49.3 us
    pallas_call x8, Pallas kernels, spread_blocks(): pl.pallas_call(functools.partial(spread_kernel, n_src=n_src), out_shape=j...  49 us
    pallas_call x8, Pallas kernels, reply_blocks(): pl.pallas_call(functools.partial(reply_kernel, n_cols=n_cols), out_shape=...  26.2 us
    ppermute x24, starting transfers between devices, local(): lax.ppermute(own, 'cols', [((x + d) % n_cols, x) for x in range(n_cols)])  22.4 us
    all_to_all x1, starting transfers between devices, ask_blocks(): lax.all_to_all(wanted.reshape(n_rows, 1), 'rows', split_axis=0, concat_ax...  12.1 us
  transfers between devices with their start and end apart: 33, of which 32 were waited for; matrix products, arithmetic and copies ran while one was open for 2% of the time, Pallas kernels for 13%

profile of v1, /device:TPU:8, one launch (start us, length us, event | category | flops | bytes accessed | tf_op | source)
XLA Modules:
  0.0 509.1 jit_solution(13441484856213578812)
XLA Ops:
  1.7 12.1 %all-to-all-start = ((s32[64,1,1]{2,1,0:T(1,128)}), s32[64,1,1]{2,1,0:T(1,128)S(1)}, u32[]{:S(2)}, u32[]{:S(2)}) async-start(s32[64,1,1]{2,1,0:T(1,128)} %copy.8), calls=%async_computation | async-start | bytes 65536 | tf_op jit(solution)/shard_map/all_to_all | solution.py:36
  29.8 3.0 collective-permute-done.2.refs_3_
  33.5 3.3 reply.8
  36.8 10.5 %all-to-all-start.1 = ((bf16[64,128,128]{2,1,0:T(8,128)(2,1)}), bf16[64,128,128]{2,1,0:T(8,128)(2,1)}, u32[]{:S(2)}, u32[]{:S(2)}) async-start(bf16[64,128,128]{2,1,0:T(8,128)(2,1)} %reply.8), calls=%async_computation.1 | async-start | bytes 4194304 | tf_op jit(solution)/shard_map/all_to_all | solution.py:170
  49.6 5.5 %collective-permute-done.12.refs_1_ = bf16[6,128,128]{2,1,0:T(8,128)(2,1)S(1)} collective-permute-done((bf16[6,128,128]{2,1,0:T(8,128)(2,1)S(1)}, bf16[6,128,128]{2,1,0:T(8,128)(2,1)S(1)}, u32[]{:S(2)}, u32[]{:S(2)}) %collective-permute-start.12) | collective-permute-done | bytes 196640 | tf_op jit(solution)/shard_map/ppermute | solution.py:166
  57.5 3.0 collective-permute-done.14.refs_3_
  61.2 3.3 reply.12
  64.5 34.0 %all-to-all-done.1.refs_4_ = bf16[64,128,128]{2,1,0:T(8,128)(2,1)} async-done(((bf16[64,128,128]{2,1,0:T(8,128)(2,1)}), bf16[64,128,128]{2,1,0:T(8,128)(2,1)}, u32[]{:S(2)}, u32[]{:S(2)}) %all-to-all-start.1) | async-done | bytes 2097184 | tf_op jit(solution)/shard_map/all_to_all | solution.py:170
  98.5 5.6 %all-to-all-start.5 = ((bf16[64,128,128]{2,1,0:T(8,128)(2,1)}), bf16[64,128,128]{2,1,0:T(8,128)(2,1)}, u32[]{:S(2)}, u32[]{:S(2)}) async-start(bf16[64,128,128]{2,1,0:T(8,128)(2,1)} %reply.12), calls=%async_computation.5 | async-start | bytes 4194304 | tf_op jit(solution)/shard_map/all_to_all | solution.py:170
  107.1 6.1 %spread.8 = bf16[768,128]{1,0:T(8,128)(2,1)} custom-call(s32[72]{0:T(128)} %reshape.100.index_ref, bf16[6,12,128,128]{3,2,1,0:T(8,128)(2,1)} %tiles_ref.15, f32[768,128]{1,0:T(8,128)} %broadcast_in_dim.31.weight_ref, f32[768,128]{1,0:T(8,128)} %get-tuple-element.7.anchor_ref, bf16[6,128,128]{2,1,0:T(8,128)(2,1)} %bitcast.53, bf16[6,128,128]{2,1,0:T(8,128)(2,1)} %copy-done.7, ...), custom_call_target="tpu_custom_call" | custom-call | flops 301989888 | bytes 5242880 | tf_op jit(solution)/shard_map/spread/pallas_call | solution.py:114
  115.5 5.8 %collective-permute-done.3.refs_1_ = bf16[6,128,128]{2,1,0:T(8,128)(2,1)S(1)} collective-permute-done((bf16[6,128,128]{2,1,0:T(8,128)(2,1)}, bf16[6,128,128]{2,1,0:T(8,128)(2,1)S(1)}, u32[]{:S(2)}, u32[]{:S(2)}) %collective-permute-start.3) | collective-permute-done | bytes 196640 | tf_op jit(solution)/shard_map/ppermute | solution.py:166
  123.6 3.0 collective-permute-done.5.refs_3_
  127.3 3.3 reply.9
  130.6 24.6 %all-to-all-done.5.refs_4_ = bf16[64,128,128]{2,1,0:T(8,128)(2,1)} async-done(((bf16[64,128,128]{2,1,0:T(8,128)(2,1)}), bf16[64,128,128]{2,1,0:T(8,128)(2,1)}, u32[]{:S(2)}, u32[]{:S(2)}) %all-to-all-start.5) | async-done | bytes 2097184 | tf_op jit(solution)/shard_map/all_to_all | solution.py:170
  155.3 5.4 %all-to-all-start.2 = ((bf16[64,128,128]{2,1,0:T(8,128)(2,1)}), bf16[64,128,128]{2,1,0:T(8,128)(2,1)S(1)}, u32[]{:S(2)}, u32[]{:S(2)}) async-start(bf16[64,128,128]{2,1,0:T(8,128)(2,1)} %reply.9), calls=%async_computation.2 | async-start | bytes 4194304 | tf_op jit(solution)/shard_map/all_to_all | solution.py:170
  160.7 6.1 %spread.12 = bf16[768,128]{1,0:T(8,128)(2,1)} custom-call(s32[72]{0:T(128)} %reshape.100.index_ref, bf16[6,12,128,128]{3,2,1,0:T(8,128)(2,1)} %tiles_ref.15, f32[768,128]{1,0:T(8,128)} %broadcast_in_dim.31.weight_ref, f32[768,128]{1,0:T(8,128)} %get-tuple-element.8.anchor_ref, bf16[6,128,128]{2,1,0:T(8,128)(2,1)} %bitcast.48, ...), custom_call_target="tpu_custom_call" | custom-call | flops 301989888 | bytes 5242880 | tf_op jit(solution)/shard_map/spread/pallas_call | solution.py:114
  169.1 5.8 %collective-permute-done.15.refs_1_ = bf16[6,128,128]{2,1,0:T(8,128)(2,1)S(1)} collective-permute-done((bf16[6,128,128]{2,1,0:T(8,128)(2,1)}, bf16[6,128,128]{2,1,0:T(8,128)(2,1)S(1)}, u32[]{:S(2)}, u32[]{:S(2)}) %collective-permute-start.15) | collective-permute-done | bytes 196640 | tf_op jit(solution)/shard_map/ppermute | solution.py:166
  177.2 3.0 collective-permute-done.17.refs_3_
  180.9 3.3 reply.13
  184.2 27.7 %all-to-all-done.2.refs_4_ = bf16[64,128,128]{2,1,0:T(8,128)(2,1)S(1)} async-done(((bf16[64,128,128]{2,1,0:T(8,128)(2,1)}), bf16[64,128,128]{2,1,0:T(8,128)(2,1)S(1)}, u32[]{:S(2)}, u32[]{:S(2)}) %all-to-all-start.2) | async-done | bytes 2097184 | tf_op jit(solution)/shard_map/all_to_all | solution.py:170
  213.3 5.6 %all-to-all-start.6 = ((bf16[64,128,128]{2,1,0:T(8,128)(2,1)}), bf16[64,128,128]{2,1,0:T(8,128)(2,1)}, u32[]{:S(2)}, u32[]{:S(2)}) async-start(bf16[64,128,128]{2,1,0:T(8,128)(2,1)} %reply.13), calls=%async_computation.6 | async-start | bytes 4194304 | tf_op jit(solution)/shard_map/all_to_all | solution.py:170
  218.9 6.1 %spread.9 = bf16[768,128]{1,0:T(8,128)(2,1)} custom-call(s32[72]{0:T(128)} %reshape.100.index_ref, bf16[6,12,128,128]{3,2,1,0:T(8,128)(2,1)} %tiles_ref.15, f32[768,128]{1,0:T(8,128)} %broadcast_in_dim.31.weight_ref, f32[768,128]{1,0:T(8,128)} %get-tuple-element.7.anchor_ref, bf16[6,128,128]{2,1,0:T(8,128)(2,1)} %bitcast.23, ...), custom_call_target="tpu_custom_call" | custom-call | flops 301989888 | bytes 5242880 | tf_op jit(solution)/shard_map/spread/pallas_call | solution.py:114
  227.3 5.8 %collective-permute-done.6.refs_1_ = bf16[6,128,128]{2,1,0:T(8,128)(2,1)S(1)} collective-permute-done((bf16[6,128,128]{2,1,0:T(8,128)(2,1)}, bf16[6,128,128]{2,1,0:T(8,128)(2,1)S(1)}, u32[]{:S(2)}, u32[]{:S(2)}) %collective-permute-start.6) | collective-permute-done | bytes 196640 | tf_op jit(solution)/shard_map/ppermute | solution.py:166
  235.4 3.0 collective-permute-done.8.refs_3_
  239.1 3.3 reply.10
  242.4 27.7 %all-to-all-done.6.refs_4_ = bf16[64,128,128]{2,1,0:T(8,128)(2,1)} async-done(((bf16[64,128,128]{2,1,0:T(8,128)(2,1)}), bf16[64,128,128]{2,1,0:T(8,128)(2,1)}, u32[]{:S(2)}, u32[]{:S(2)}) %all-to-all-start.6) | async-done | bytes 2097184 | tf_op jit(solution)/shard_map/all_to_all | solution.py:170
  270.1 5.4 %all-to-all-start.3 = ((bf16[64,128,128]{2,1,0:T(8,128)(2,1)}), bf16[64,128,128]{2,1,0:T(8,128)(2,1)S(1)}, u32[]{:S(2)}, u32[]{:S(2)}) async-start(bf16[64,128,128]{2,1,0:T(8,128)(2,1)} %reply.10), calls=%async_computation.3 | async-start | bytes 4194304 | tf_op jit(solution)/shard_map/all_to_all | solution.py:170
  275.5 6.1 %spread.13 = bf16[768,128]{1,0:T(8,128)(2,1)} custom-call(s32[72]{0:T(128)} %reshape.100.index_ref, bf16[6,12,128,128]{3,2,1,0:T(8,128)(2,1)} %tiles_ref.15, f32[768,128]{1,0:T(8,128)} %broadcast_in_dim.31.weight_ref, f32[768,128]{1,0:T(8,128)} %get-tuple-element.8.anchor_ref, bf16[6,128,128]{2,1,0:T(8,128)(2,1)} %bitcast.28, ...), custom_call_target="tpu_custom_call" | custom-call | flops 301989888 | bytes 5242880 | tf_op jit(solution)/shard_map/spread/pallas_call | solution.py:114
  283.9 5.8 %collective-permute-done.18.refs_1_ = bf16[6,128,128]{2,1,0:T(8,128)(2,1)S(1)} collective-permute-done((bf16[6,128,128]{2,1,0:T(8,128)(2,1)}, bf16[6,128,128]{2,1,0:T(8,128)(2,1)S(1)}, u32[]{:S(2)}, u32[]{:S(2)}) %collective-permute-start.18) | collective-permute-done | bytes 196640 | tf_op jit(solution)/shard_map/ppermute | solution.py:166
  292.0 3.0 collective-permute-done.20.refs_3_
  295.7 3.3 reply.14
  299.0 27.8 %all-to-all-done.3.refs_4_ = bf16[64,128,128]{2,1,0:T(8,128)(2,1)S(1)} async-done(((bf16[64,128,128]{2,1,0:T(8,128)(2,1)}), bf16[64,128,128]{2,1,0:T(8,128)(2,1)S(1)}, u32[]{:S(2)}, u32[]{:S(2)}) %all-to-all-start.3) | async-done | bytes 2097184 | tf_op jit(solution)/shard_map/all_to_all | solution.py:170
  328.1 5.6 %all-to-all-start.7 = ((bf16[64,128,128]{2,1,0:T(8,128)(2,1)}), bf16[64,128,128]{2,1,0:T(8,128)(2,1)}, u32[]{:S(2)}, u32[]{:S(2)}) async-start(bf16[64,128,128]{2,1,0:T(8,128)(2,1)} %reply.14), calls=%async_computation.7 | async-start | bytes 4194304 | tf_op jit(solution)/shard_map/all_to_all | solution.py:170
  333.7 6.1 %spread.10 = bf16[768,128]{1,0:T(8,128)(2,1)} custom-call(s32[72]{0:T(128)} %reshape.100.index_ref, bf16[6,12,128,128]{3,2,1,0:T(8,128)(2,1)} %tiles_ref.15, f32[768,128]{1,0:T(8,128)} %broadcast_in_dim.31.weight_ref, f32[768,128]{1,0:T(8,128)} %get-tuple-element.7.anchor_ref, bf16[6,128,128]{2,1,0:T(8,128)(2,1)} %bitcast.33, ...), custom_call_target="tpu_custom_call" | custom-call | flops 301989888 | bytes 5242880 | tf_op jit(solution)/shard_map/spread/pallas_call | solution.py:114
  344.0 5.5 %collective-permute-done.10.refs_2_ = bf16[6,128,128]{2,1,0:T(8,128)(2,1)S(1)} collective-permute-done((bf16[6,128,128]{2,1,0:T(8,128)(2,1)}, bf16[6,128,128]{2,1,0:T(8,128)(2,1)S(1)}, u32[]{:S(2)}, u32[]{:S(2)}) %collective-permute-start.10) | collective-permute-done | bytes 196640 | tf_op jit(solution)/shard_map/ppermute | solution.py:166
  349.5 3.3 collective-permute-done.11.refs_3_
  354.2 3.3 reply.11
  357.4 27.4 %all-to-all-done.7.refs_4_ = bf16[64,128,128]{2,1,0:T(8,128)(2,1)} async-done(((bf16[64,128,128]{2,1,0:T(8,128)(2,1)}), bf16[64,128,128]{2,1,0:T(8,128)(2,1)}, u32[]{:S(2)}, u32[]{:S(2)}) %all-to-all-start.7) | async-done | bytes 2097184 | tf_op jit(solution)/shard_map/all_to_all | solution.py:170
  384.9 5.4 %all-to-all-start.4 = ((bf16[64,128,128]{2,1,0:T(8,128)(2,1)}), bf16[64,128,128]{2,1,0:T(8,128)(2,1)S(1)}, u32[]{:S(2)}, u32[]{:S(2)}) async-start(bf16[64,128,128]{2,1,0:T(8,128)(2,1)} %reply.11), calls=%async_computation.4 | async-start | bytes 4194304 | tf_op jit(solution)/shard_map/all_to_all | solution.py:170
  390.3 6.1 %spread.14 = bf16[768,128]{1,0:T(8,128)(2,1)} custom-call(s32[72]{0:T(128)} %reshape.100.index_ref, bf16[6,12,128,128]{3,2,1,0:T(8,128)(2,1)} %tiles_ref.15, f32[768,128]{1,0:T(8,128)} %broadcast_in_dim.31.weight_ref, f32[768,128]{1,0:T(8,128)} %get-tuple-element.8.anchor_ref, bf16[6,128,128]{2,1,0:T(8,128)(2,1)} %bitcast.38, ...), custom_call_target="tpu_custom_call" | custom-call | flops 301989888 | bytes 5242880 | tf_op jit(solution)/shard_map/spread/pallas_call | solution.py:114
  398.7 5.8 %collective-permute-done.21.refs_1_ = bf16[6,128,128]{2,1,0:T(8,128)(2,1)S(1)} collective-permute-done((bf16[6,128,128]{2,1,0:T(8,128)(2,1)}, bf16[6,128,128]{2,1,0:T(8,128)(2,1)S(1)}, u32[]{:S(2)}, u32[]{:S(2)}) %collective-permute-start.21) | collective-permute-done | bytes 196640 | tf_op jit(solution)/shard_map/ppermute | solution.py:166
  406.8 3.0 collective-permute-done.23.refs_3_
  410.5 3.3 reply.15
  413.8 27.7 %all-to-all-done.4.refs_4_ = bf16[64,128,128]{2,1,0:T(8,128)(2,1)S(1)} async-done(((bf16[64,128,128]{2,1,0:T(8,128)(2,1)}), bf16[64,128,128]{2,1,0:T(8,128)(2,1)S(1)}, u32[]{:S(2)}, u32[]{:S(2)}) %all-to-all-start.4) | async-done | bytes 2097184 | tf_op jit(solution)/shard_map/all_to_all | solution.py:170
  442.9 5.6 %all-to-all-start.8 = ((bf16[64,128,128]{2,1,0:T(8,128)(2,1)}), bf16[64,128,128]{2,1,0:T(8,128)(2,1)}, u32[]{:S(2)}, u32[]{:S(2)}) async-start(bf16[64,128,128]{2,1,0:T(8,128)(2,1)} %reply.15), calls=%async_computation.8 | async-start | bytes 4194304 | tf_op jit(solution)/shard_map/all_to_all | solution.py:170
  448.5 6.2 %spread.11 = f32[768,128]{1,0:T(8,128)} custom-call(s32[72]{0:T(128)} %reshape.100.index_ref, bf16[6,12,128,128]{3,2,1,0:T(8,128)(2,1)} %tiles_ref.15, f32[768,128]{1,0:T(8,128)} %broadcast_in_dim.31.weight_ref, f32[768,128]{1,0:T(8,128)} %get-tuple-element.7.anchor_ref, bf16[6,128,128]{2,1,0:T(8,128)(2,1)} %bitcast.18, bf16[6,128,128]{2,1,0:T(8,128)(2,1)} %copy-done.23, ...), custom_call_target="tpu_custom_call" | custom-call | flops 301989888 | bytes 5242880 | tf_op jit(solution)/shard_map/spread/pallas_call | solution.py:114
  455.9 43.8 %all-to-all-done.8.refs_4_ = bf16[64,128,128]{2,1,0:T(8,128)(2,1)} async-done(((bf16[64,128,128]{2,1,0:T(8,128)(2,1)}), bf16[64,128,128]{2,1,0:T(8,128)(2,1)}, u32[]{:S(2)}, u32[]{:S(2)}) %all-to-all-start.8) | async-done | bytes 2097184 | tf_op jit(solution)/shard_map/all_to_all | solution.py:170
  499.7 6.1 %spread.15 = f32[768,128]{1,0:T(8,128)} custom-call(s32[72]{0:T(128)} %reshape.100.index_ref, bf16[6,12,128,128]{3,2,1,0:T(8,128)(2,1)} %tiles_ref.15, f32[768,128]{1,0:T(8,128)} %broadcast_in_dim.31.weight_ref, f32[768,128]{1,0:T(8,128)} %get-tuple-element.8.anchor_ref, bf16[6,128,128]{2,1,0:T(8,128)(2,1)} %bitcast.43, bf16[6,128,128]{2,1,0:T(8,128)(2,1)} %copy-done.28, ...), custom_call_target="tpu_custom_call" | custom-call | flops 301989888 | bytes 5242880 | tf_op jit(solution)/shard_map/spread/pallas_call | solution.py:114
  (119 shorter events, 67.0 us)
Async XLA Ops:
  1.7 20.7 %all-to-all-start = ((s32[64,1,1]{2,1,0:T(1,128)}), s32[64,1,1]{2,1,0:T(1,128)S(1)}, u32[]{:S(2)}, u32[]{:S(2)}) async-start(s32[64,1,1]{2,1,0:T(1,128)} %copy.8), calls=%async_computation | async-start | bytes 65536 | tf_op jit(solution)/shard_map/all_to_all | solution.py:36
  17.6 15.2 %copy-start.6 = (bf16[768,128]{1,0:T(8,128)(2,1)}, bf16[768,128]{1,0:T(8,128)(2,1)S(1)}, u32[]{:S(2)}) copy-start(bf16[768,128]{1,0:T(8,128)(2,1)S(1)} %get-tuple-element.9) | copy-start | bytes 589828
  17.7 31.2 %copy-start.5 = (bf16[768,128]{1,0:T(8,128)(2,1)}, bf16[768,128]{1,0:T(8,128)(2,1)S(1)}, u32[]{:S(2)}) copy-start(bf16[768,128]{1,0:T(8,128)(2,1)S(1)} %get-tuple-element.10) | copy-start | bytes 589828
  17.7 11.5 %collective-permute-start = (bf16[6,128,128]{2,1,0:T(8,128)(2,1)S(1)}, bf16[6,128,128]{2,1,0:T(8,128)(2,1)S(1)}, u32[]{:S(2)}, u32[]{:S(2)}) collective-permute-start(bf16[6,128,128]{2,1,0:T(8,128)(2,1)S(1)} %bitcast.49), channel_id=1, source_target_pairs={{1,0},{2,1},{3,2},{0,3},{5,4},{6,5},{7,6},{4,7},{9,8},{10,9},{11,1... | collective-permute-start | bytes 589832 | tf_op jit(solution)/shard_map/ppermute | solution.py:166
  20.5 9.3 %collective-permute-start.1 = (bf16[6,128,128]{2,1,0:T(8,128)(2,1)S(1)}, bf16[6,128,128]{2,1,0:T(8,128)(2,1)S(1)}, u32[]{:S(2)}, u32[]{:S(2)}) collective-permute-start(bf16[6,128,128]{2,1,0:T(8,128)(2,1)S(1)} %bitcast.50), channel_id=1, source_target_pairs={{2,0},{3,1},{0,2},{1,3},{6,4},{7,5},{4,6},{5,7},{10,8},{11,9},{8,1... | collective-permute-start | bytes 589832 | tf_op jit(solution)/shard_map/ppermute | solution.py:166
  21.3 11.6 %collective-permute-start.2 = (bf16[6,128,128]{2,1,0:T(8,128)(2,1)S(1)}, bf16[6,128,128]{2,1,0:T(8,128)(2,1)S(1)}, u32[]{:S(2)}, u32[]{:S(2)}) collective-permute-start(bf16[6,128,128]{2,1,0:T(8,128)(2,1)S(1)} %bitcast.51), channel_id=1, source_target_pairs={{3,0},{0,1},{1,2},{2,3},{7,4},{4,5},{5,6},{6,7},{11,8},{8,9},{9,10... | collective-permute-start | bytes 589832 | tf_op jit(solution)/shard_map/ppermute | solution.py:166
  29.2 3.7 copy-start.7
  29.8 3.0 copy-start.8
  36.8 61.7 %all-to-all-start.1 = ((bf16[64,128,128]{2,1,0:T(8,128)(2,1)}), bf16[64,128,128]{2,1,0:T(8,128)(2,1)}, u32[]{:S(2)}, u32[]{:S(2)}) async-start(bf16[64,128,128]{2,1,0:T(8,128)(2,1)} %reply.8), calls=%async_computation.1 | async-start | bytes 4194304 | tf_op jit(solution)/shard_map/all_to_all | solution.py:170
  47.3 7.8 %collective-permute-start.12 = (bf16[6,128,128]{2,1,0:T(8,128)(2,1)S(1)}, bf16[6,128,128]{2,1,0:T(8,128)(2,1)S(1)}, u32[]{:S(2)}, u32[]{:S(2)}) collective-permute-start(bf16[6,128,128]{2,1,0:T(8,128)(2,1)S(1)} %bitcast.44), channel_id=1, source_target_pairs={{1,0},{2,1},{3,2},{0,3},{5,4},{6,5},{7,6},{4,7},{9,8},{10,9},{11,1... | collective-permute-start | bytes 589832 | tf_op jit(solution)/shard_map/ppermute | solution.py:166
  48.2 9.3 %collective-permute-start.13 = (bf16[6,128,128]{2,1,0:T(8,128)(2,1)S(1)}, bf16[6,128,128]{2,1,0:T(8,128)(2,1)S(1)}, u32[]{:S(2)}, u32[]{:S(2)}) collective-permute-start(bf16[6,128,128]{2,1,0:T(8,128)(2,1)S(1)} %bitcast.45), channel_id=1, source_target_pairs={{2,0},{3,1},{0,2},{1,3},{6,4},{7,5},{4,6},{5,7},{10,8},{11,9},{8,1... | collective-permute-start | bytes 589832 | tf_op jit(solution)/shard_map/ppermute | solution.py:166
  48.8 11.7 %collective-permute-start.14 = (bf16[6,128,128]{2,1,0:T(8,128)(2,1)S(1)}, bf16[6,128,128]{2,1,0:T(8,128)(2,1)S(1)}, u32[]{:S(2)}, u32[]{:S(2)}) collective-permute-start(bf16[6,128,128]{2,1,0:T(8,128)(2,1)S(1)} %bitcast.46), channel_id=1, source_target_pairs={{3,0},{0,1},{1,2},{2,3},{7,4},{4,5},{5,6},{6,7},{11,8},{8,9},{9,10... | collective-permute-start | bytes 589832 | tf_op jit(solution)/shard_map/ppermute | solution.py:166
  55.2 5.3 %copy-start.9 = (bf16[6,128,128]{2,1,0:T(8,128)(2,1)}, bf16[6,128,128]{2,1,0:T(8,128)(2,1)S(1)}, u32[]{:S(2)}) copy-start(bf16[6,128,128]{2,1,0:T(8,128)(2,1)S(1)} %collective-permute-done.12.refs_1_) | copy-start | bytes 589828
  57.5 3.0 copy-start.11
  64.5 40.2 %copy-start = (bf16[6,12,128,128]{3,2,1,0:T(8,128)(2,1)S(1)}, bf16[6,12,128,128]{3,2,1,0:T(8,128)(2,1)}, u32[]{:S(2)}) copy-start(bf16[6,12,128,128]{3,2,1,0:T(8,128)(2,1)} %tiles_ref.15) | copy-start | bytes 7077892
  98.5 56.8 %all-to-all-start.5 = ((bf16[64,128,128]{2,1,0:T(8,128)(2,1)}), bf16[64,128,128]{2,1,0:T(8,128)(2,1)}, u32[]{:S(2)}, u32[]{:S(2)}) async-start(bf16[64,128,128]{2,1,0:T(8,128)(2,1)} %reply.12), calls=%async_computation.5 | async-start | bytes 4194304 | tf_op jit(solution)/shard_map/all_to_all | solution.py:170
  113.2 8.1 %collective-permute-start.3 = (bf16[6,128,128]{2,1,0:T(8,128)(2,1)}, bf16[6,128,128]{2,1,0:T(8,128)(2,1)S(1)}, u32[]{:S(2)}, u32[]{:S(2)}) collective-permute-start(bf16[6,128,128]{2,1,0:T(8,128)(2,1)} %bitcast.19), channel_id=1, source_target_pairs={{1,0},{2,1},{3,2},{0,3},{5,4},{6,5},{7,6},{4,7},{9,8},{10,9},{11,1... | collective-permute-start | bytes 589832 | tf_op jit(solution)/shard_map/ppermute | solution.py:166
  114.1 9.5 %collective-permute-start.4 = (bf16[6,128,128]{2,1,0:T(8,128)(2,1)}, bf16[6,128,128]{2,1,0:T(8,128)(2,1)S(1)}, u32[]{:S(2)}, u32[]{:S(2)}) collective-permute-start(bf16[6,128,128]{2,1,0:T(8,128)(2,1)} %bitcast.20), channel_id=1, source_target_pairs={{2,0},{3,1},{0,2},{1,3},{6,4},{7,5},{4,6},{5,7},{10,8},{11,9},{8,1... | collective-permute-start | bytes 589832 | tf_op jit(solution)/shard_map/ppermute | solution.py:166
  114.7 11.9 %collective-permute-start.5 = (bf16[6,128,128]{2,1,0:T(8,128)(2,1)}, bf16[6,128,128]{2,1,0:T(8,128)(2,1)S(1)}, u32[]{:S(2)}, u32[]{:S(2)}) collective-permute-start(bf16[6,128,128]{2,1,0:T(8,128)(2,1)} %bitcast.21), channel_id=1, source_target_pairs={{3,0},{0,1},{1,2},{2,3},{7,4},{4,5},{5,6},{6,7},{11,8},{8,9},{9,10... | collective-permute-start | bytes 589832 | tf_op jit(solution)/shard_map/ppermute | solution.py:166
  121.3 5.3 %copy-start.14 = (bf16[6,128,128]{2,1,0:T(8,128)(2,1)}, bf16[6,128,128]{2,1,0:T(8,128)(2,1)S(1)}, u32[]{:S(2)}) copy-start(bf16[6,128,128]{2,1,0:T(8,128)(2,1)S(1)} %collective-permute-done.3.refs_1_) | copy-start | bytes 589828
  155.3 56.7 %all-to-all-start.2 = ((bf16[64,128,128]{2,1,0:T(8,128)(2,1)}), bf16[64,128,128]{2,1,0:T(8,128)(2,1)S(1)}, u32[]{:S(2)}, u32[]{:S(2)}) async-start(bf16[64,128,128]{2,1,0:T(8,128)(2,1)} %reply.9), calls=%async_computation.2 | async-start | bytes 4194304 | tf_op jit(solution)/shard_map/all_to_all | solution.py:170
  166.8 8.1 %collective-permute-start.15 = (bf16[6,128,128]{2,1,0:T(8,128)(2,1)}, bf16[6,128,128]{2,1,0:T(8,128)(2,1)S(1)}, u32[]{:S(2)}, u32[]{:S(2)}) collective-permute-start(bf16[6,128,128]{2,1,0:T(8,128)(2,1)} %bitcast.24), channel_id=1, source_target_pairs={{1,0},{2,1},{3,2},{0,3},{5,4},{6,5},{7,6},{4,7},{9,8},{10,9},{11,1... | collective-permute-start | bytes 589832 | tf_op jit(solution)/shard_map/ppermute | solution.py:166
  167.7 9.5 %collective-permute-start.16 = (bf16[6,128,128]{2,1,0:T(8,128)(2,1)}, bf16[6,128,128]{2,1,0:T(8,128)(2,1)S(1)}, u32[]{:S(2)}, u32[]{:S(2)}) collective-permute-start(bf16[6,128,128]{2,1,0:T(8,128)(2,1)} %bitcast.25), channel_id=1, source_target_pairs={{2,0},{3,1},{0,2},{1,3},{6,4},{7,5},{4,6},{5,7},{10,8},{11,9},{8,1... | collective-permute-start | bytes 589832 | tf_op jit(solution)/shard_map/ppermute | solution.py:166
  168.3 11.9 %collective-permute-start.17 = (bf16[6,128,128]{2,1,0:T(8,128)(2,1)}, bf16[6,128,128]{2,1,0:T(8,128)(2,1)S(1)}, u32[]{:S(2)}, u32[]{:S(2)}) collective-permute-start(bf16[6,128,128]{2,1,0:T(8,128)(2,1)} %bitcast.26), channel_id=1, source_target_pairs={{3,0},{0,1},{1,2},{2,3},{7,4},{4,5},{5,6},{6,7},{11,8},{8,9},{9,10... | collective-permute-start | bytes 589832 | tf_op jit(solution)/shard_map/ppermute | solution.py:166
  174.9 5.3 %copy-start.15 = (bf16[6,128,128]{2,1,0:T(8,128)(2,1)}, bf16[6,128,128]{2,1,0:T(8,128)(2,1)S(1)}, u32[]{:S(2)}) copy-start(bf16[6,128,128]{2,1,0:T(8,128)(2,1)S(1)} %collective-permute-done.15.refs_1_) | copy-start | bytes 589828
  177.2 3.0 copy-start.20
  213.3 56.8 %all-to-all-start.6 = ((bf16[64,128,128]{2,1,0:T(8,128)(2,1)}), bf16[64,128,128]{2,1,0:T(8,128)(2,1)}, u32[]{:S(2)}, u32[]{:S(2)}) async-start(bf16[64,128,128]{2,1,0:T(8,128)(2,1)} %reply.13), calls=%async_computation.6 | async-start | bytes 4194304 | tf_op jit(solution)/shard_map/all_to_all | solution.py:170
  225.0 8.1 %collective-permute-start.6 = (bf16[6,128,128]{2,1,0:T(8,128)(2,1)}, bf16[6,128,128]{2,1,0:T(8,128)(2,1)S(1)}, u32[]{:S(2)}, u32[]{:S(2)}) collective-permute-start(bf16[6,128,128]{2,1,0:T(8,128)(2,1)} %bitcast.29), channel_id=1, source_target_pairs={{1,0},{2,1},{3,2},{0,3},{5,4},{6,5},{7,6},{4,7},{9,8},{10,9},{11,1... | collective-permute-start | bytes 589832 | tf_op jit(solution)/shard_map/ppermute | solution.py:166
  225.9 9.5 %collective-permute-start.7 = (bf16[6,128,128]{2,1,0:T(8,128)(2,1)}, bf16[6,128,128]{2,1,0:T(8,128)(2,1)S(1)}, u32[]{:S(2)}, u32[]{:S(2)}) collective-permute-start(bf16[6,128,128]{2,1,0:T(8,128)(2,1)} %bitcast.30), channel_id=1, source_target_pairs={{2,0},{3,1},{0,2},{1,3},{6,4},{7,5},{4,6},{5,7},{10,8},{11,9},{8,1... | collective-permute-start | bytes 589832 | tf_op jit(solution)/shard_map/ppermute | solution.py:166
  226.5 11.9 %collective-permute-start.8 = (bf16[6,128,128]{2,1,0:T(8,128)(2,1)}, bf16[6,128,128]{2,1,0:T(8,128)(2,1)S(1)}, u32[]{:S(2)}, u32[]{:S(2)}) collective-permute-start(bf16[6,128,128]{2,1,0:T(8,128)(2,1)} %bitcast.31), channel_id=1, source_target_pairs={{3,0},{0,1},{1,2},{2,3},{7,4},{4,5},{5,6},{6,7},{11,8},{8,9},{9,10... | collective-permute-start | bytes 589832 | tf_op jit(solution)/shard_map/ppermute | solution.py:166
  233.1 5.4 %copy-start.16 = (bf16[6,128,128]{2,1,0:T(8,128)(2,1)}, bf16[6,128,128]{2,1,0:T(8,128)(2,1)S(1)}, u32[]{:S(2)}) copy-start(bf16[6,128,128]{2,1,0:T(8,128)(2,1)S(1)} %collective-permute-done.6.refs_1_) | copy-start | bytes 589828
  270.1 56.7 %all-to-all-start.3 = ((bf16[64,128,128]{2,1,0:T(8,128)(2,1)}), bf16[64,128,128]{2,1,0:T(8,128)(2,1)S(1)}, u32[]{:S(2)}, u32[]{:S(2)}) async-start(bf16[64,128,128]{2,1,0:T(8,128)(2,1)} %reply.10), calls=%async_computation.3 | async-start | bytes 4194304 | tf_op jit(solution)/shard_map/all_to_all | solution.py:170
  281.6 8.1 %collective-permute-start.18 = (bf16[6,128,128]{2,1,0:T(8,128)(2,1)}, bf16[6,128,128]{2,1,0:T(8,128)(2,1)S(1)}, u32[]{:S(2)}, u32[]{:S(2)}) collective-permute-start(bf16[6,128,128]{2,1,0:T(8,128)(2,1)} %bitcast.34), channel_id=1, source_target_pairs={{1,0},{2,1},{3,2},{0,3},{5,4},{6,5},{7,6},{4,7},{9,8},{10,9},{11,1... | collective-permute-start | bytes 589832 | tf_op jit(solution)/shard_map/ppermute | solution.py:166
  282.5 9.5 %collective-permute-start.19 = (bf16[6,128,128]{2,1,0:T(8,128)(2,1)}, bf16[6,128,128]{2,1,0:T(8,128)(2,1)S(1)}, u32[]{:S(2)}, u32[]{:S(2)}) collective-permute-start(bf16[6,128,128]{2,1,0:T(8,128)(2,1)} %bitcast.35), channel_id=1, source_target_pairs={{2,0},{3,1},{0,2},{1,3},{6,4},{7,5},{4,6},{5,7},{10,8},{11,9},{8,1... | collective-permute-start | bytes 589832 | tf_op jit(solution)/shard_map/ppermute | solution.py:166
  283.1 11.9 %collective-permute-start.20 = (bf16[6,128,128]{2,1,0:T(8,128)(2,1)}, bf16[6,128,128]{2,1,0:T(8,128)(2,1)S(1)}, u32[]{:S(2)}, u32[]{:S(2)}) collective-permute-start(bf16[6,128,128]{2,1,0:T(8,128)(2,1)} %bitcast.36), channel_id=1, source_target_pairs={{3,0},{0,1},{1,2},{2,3},{7,4},{4,5},{5,6},{6,7},{11,8},{8,9},{9,10... | collective-permute-start | bytes 589832 | tf_op jit(solution)/shard_map/ppermute | solution.py:166
  289.7 5.3 %copy-start.17 = (bf16[6,128,128]{2,1,0:T(8,128)(2,1)}, bf16[6,128,128]{2,1,0:T(8,128)(2,1)S(1)}, u32[]{:S(2)}) copy-start(bf16[6,128,128]{2,1,0:T(8,128)(2,1)S(1)} %collective-permute-done.18.refs_1_) | copy-start | bytes 589828
  328.1 56.8 %all-to-all-start.7 = ((bf16[64,128,128]{2,1,0:T(8,128)(2,1)}), bf16[64,128,128]{2,1,0:T(8,128)(2,1)}, u32[]{:S(2)}, u32[]{:S(2)}) async-start(bf16[64,128,128]{2,1,0:T(8,128)(2,1)} %reply.14), calls=%async_computation.7 | async-start | bytes 4194304 | tf_op jit(solution)/shard_map/all_to_all | solution.py:170
  339.9 9.6 %collective-permute-start.10 = (bf16[6,128,128]{2,1,0:T(8,128)(2,1)}, bf16[6,128,128]{2,1,0:T(8,128)(2,1)S(1)}, u32[]{:S(2)}, u32[]{:S(2)}) collective-permute-start(bf16[6,128,128]{2,1,0:T(8,128)(2,1)} %bitcast.14), channel_id=1, source_target_pairs={{2,0},{3,1},{0,2},{1,3},{6,4},{7,5},{4,6},{5,7},{10,8},{11,9},{8,1... | collective-permute-start | bytes 589832 | tf_op jit(solution)/shard_map/ppermute | solution.py:166
  340.7 12.1 %collective-permute-start.11 = (bf16[6,128,128]{2,1,0:T(8,128)(2,1)}, bf16[6,128,128]{2,1,0:T(8,128)(2,1)S(1)}, u32[]{:S(2)}, u32[]{:S(2)}) collective-permute-start(bf16[6,128,128]{2,1,0:T(8,128)(2,1)} %bitcast.15), channel_id=1, source_target_pairs={{3,0},{0,1},{1,2},{2,3},{7,4},{4,5},{5,6},{6,7},{11,8},{8,9},{9,10... | collective-permute-start | bytes 589832 | tf_op jit(solution)/shard_map/ppermute | solution.py:166
  341.6 11.2 %collective-permute-start.9 = (bf16[6,128,128]{2,1,0:T(8,128)(2,1)}, bf16[6,128,128]{2,1,0:T(8,128)(2,1)S(1)}, u32[]{:S(2)}, u32[]{:S(2)}) collective-permute-start(bf16[6,128,128]{2,1,0:T(8,128)(2,1)} %bitcast.16), channel_id=1, source_target_pairs={{1,0},{2,1},{3,2},{0,3},{5,4},{6,5},{7,6},{4,7},{9,8},{10,9},{11,1... | collective-permute-start | bytes 589832 | tf_op jit(solution)/shard_map/ppermute | solution.py:166
  349.5 3.3 copy-start.13
  384.9 56.7 %all-to-all-start.4 = ((bf16[64,128,128]{2,1,0:T(8,128)(2,1)}), bf16[64,128,128]{2,1,0:T(8,128)(2,1)S(1)}, u32[]{:S(2)}, u32[]{:S(2)}) async-start(bf16[64,128,128]{2,1,0:T(8,128)(2,1)} %reply.11), calls=%async_computation.4 | async-start | bytes 4194304 | tf_op jit(solution)/shard_map/all_to_all | solution.py:170
  396.4 8.1 %collective-permute-start.21 = (bf16[6,128,128]{2,1,0:T(8,128)(2,1)}, bf16[6,128,128]{2,1,0:T(8,128)(2,1)S(1)}, u32[]{:S(2)}, u32[]{:S(2)}) collective-permute-start(bf16[6,128,128]{2,1,0:T(8,128)(2,1)} %bitcast.39), channel_id=1, source_target_pairs={{1,0},{2,1},{3,2},{0,3},{5,4},{6,5},{7,6},{4,7},{9,8},{10,9},{11,1... | collective-permute-start | bytes 589832 | tf_op jit(solution)/shard_map/ppermute | solution.py:166
  397.3 9.5 %collective-permute-start.22 = (bf16[6,128,128]{2,1,0:T(8,128)(2,1)}, bf16[6,128,128]{2,1,0:T(8,128)(2,1)S(1)}, u32[]{:S(2)}, u32[]{:S(2)}) collective-permute-start(bf16[6,128,128]{2,1,0:T(8,128)(2,1)} %bitcast.40), channel_id=1, source_target_pairs={{2,0},{3,1},{0,2},{1,3},{6,4},{7,5},{4,6},{5,7},{10,8},{11,9},{8,1... | collective-permute-start | bytes 589832 | tf_op jit(solution)/shard_map/ppermute | solution.py:166
  397.9 11.9 %collective-permute-start.23 = (bf16[6,128,128]{2,1,0:T(8,128)(2,1)}, bf16[6,128,128]{2,1,0:T(8,128)(2,1)S(1)}, u32[]{:S(2)}, u32[]{:S(2)}) collective-permute-start(bf16[6,128,128]{2,1,0:T(8,128)(2,1)} %bitcast.41), channel_id=1, source_target_pairs={{3,0},{0,1},{1,2},{2,3},{7,4},{4,5},{5,6},{6,7},{11,8},{8,9},{9,10... | collective-permute-start | bytes 589832 | tf_op jit(solution)/shard_map/ppermute | solution.py:166
  404.5 5.3 %copy-start.28 = (bf16[6,128,128]{2,1,0:T(8,128)(2,1)}, bf16[6,128,128]{2,1,0:T(8,128)(2,1)S(1)}, u32[]{:S(2)}) copy-start(bf16[6,128,128]{2,1,0:T(8,128)(2,1)S(1)} %collective-permute-done.21.refs_1_) | copy-start | bytes 589828
  442.9 56.8 %all-to-all-start.8 = ((bf16[64,128,128]{2,1,0:T(8,128)(2,1)}), bf16[64,128,128]{2,1,0:T(8,128)(2,1)}, u32[]{:S(2)}, u32[]{:S(2)}) async-start(bf16[64,128,128]{2,1,0:T(8,128)(2,1)} %reply.15), calls=%async_computation.8 | async-start | bytes 4194304 | tf_op jit(solution)/shard_map/all_to_all | solution.py:170
  455.9 51.1 %copy-start.4 = (f32[768,128]{1,0:T(8,128)S(1)}, f32[768,128]{1,0:T(8,128)}, u32[]{:S(2)}) copy-start(f32[768,128]{1,0:T(8,128)} %spread.11) | copy-start | bytes 1179652
  (16 other events, 22.3 us)

commit v2 on v1

v2 whole, which is shorter than its diff:
```python
import functools

import jax
import jax.numpy as jnp
from jax import lax
from jax.experimental import pallas as pl
from jax.experimental.pallas import tpu as pltpu
from jax.sharding import Mesh
from jax.sharding import PartitionSpec as P

HOPS = 4
PARTS = 2
AXES = ("zy", "core", "x")
GROUP = ("zy", "core")


ALPHA = 0.85
SEED_BOOST = 8.0

ANY = pl.BlockSpec(memory_space=pl.ANY)
VMEM = pl.BlockSpec(memory_space=pltpu.VMEM)
SMEM = pl.BlockSpec(memory_space=pltpu.SMEM)
HBM = pl.BlockSpec(memory_space=pltpu.HBM)


def prepare(label_prior, seed_label, seed_mask):
    classes = label_prior.shape[1]
    one_hot = (seed_label[:, None] == jnp.arange(classes, dtype=jnp.int32)[None, :]).astype(
        jnp.float32
    )
    anchor_raw = label_prior + SEED_BOOST * seed_mask[:, None].astype(jnp.float32) * one_hot
    return anchor_raw * (classes / jnp.sum(anchor_raw, axis=1, keepdims=True))


def ask_blocks(owner_group, place, own_group, n_rows):
    group_ids = jnp.arange(n_rows, dtype=jnp.int32)
    matched = owner_group.reshape(-1)[:, None] == group_ids[None, :]
    wanted = jnp.max(jnp.where(matched, place.reshape(-1)[:, None], 0), axis=0)
    wanted = jnp.where(group_ids == own_group, 0, wanted)
    return lax.all_to_all(wanted.reshape(n_rows, 1), GROUP, 0, 0, tiled=True)[:, 0]


def reply_kernel(asked_ref, *refs, n_cols):
    parts, out_ref, table, in_sems, out_sem = refs[:n_cols], refs[n_cols], *refs[n_cols + 1 :]
    blocks_dev = parts[0].shape[0]
    n = out_ref.shape[0]
    loads = [
        pltpu.make_async_copy(p, table.at[pl.ds(i * blocks_dev, blocks_dev)], in_sems.at[i])
        for i, p in enumerate(parts)
    ]
    for c in loads:
        c.start()
    for c in loads:
        c.wait()

    @pl.loop(0, n)
    def _(i):
        pltpu.make_async_copy(table.at[asked_ref[i]], out_ref.at[i], out_sem).start()

    pltpu.make_async_copy(out_ref, out_ref, out_sem).wait()


def reply_blocks(asked, parts):
    blocks_dev, block, width = parts[0].shape
    n = asked.shape[0]
    n_cols = len(parts)
    size = block * width * 2
    return pl.pallas_call(
        functools.partial(reply_kernel, n_cols=n_cols),
        out_shape=jax.ShapeDtypeStruct((n, block, width), jnp.bfloat16),
        in_specs=[SMEM] + [ANY] * n_cols,
        out_specs=ANY,
        scratch_shapes=[
            pltpu.VMEM((n_cols * blocks_dev, block, width), jnp.bfloat16),
            pltpu.SemaphoreType.DMA((n_cols,)),
            pltpu.SemaphoreType.DMA,
        ],
        cost_estimate=pl.CostEstimate(
            flops=4_000_000, bytes_accessed=(n + n_cols * blocks_dev) * size, transcendentals=0
        ),
        name="reply",
    )(asked, *parts)


def spread_kernel(index_ref, core_ref, tiles_ref, weight_ref, anchor_ref, *refs, n_src, final):
    sources, same_ref, other_ref = refs[:n_src], refs[n_src], refs[n_src + 1]
    first_ref = refs[n_src + 2] if final else None
    out_ref, table, sems = refs[-3:]
    blocks_dev, degree, block, _ = tiles_ref.shape
    width = anchor_ref.shape[1]
    loads, at = [], 0
    for i, s in enumerate([*sources, same_ref.at[:, core_ref[0]], other_ref.at[:, core_ref[0]]]):
        loads.append(pltpu.make_async_copy(s, table.at[pl.ds(at, s.shape[0])], sems.at[i]))
        at += s.shape[0]
    for c in loads:
        c.start()
    for c in loads:
        c.wait()

    @pl.loop(0, blocks_dev)
    def _(b):
        left = jnp.concatenate([tiles_ref[b, k] for k in range(degree)], axis=1)
        right = jnp.concatenate(
            [table[index_ref[b * degree + k]] for k in range(degree)], axis=0
        )
        total = jnp.dot(left, right, preferred_element_type=jnp.float32)
        rows = pl.ds(pl.multiple_of(b * block, block), block)
        blended = weight_ref[rows, :] * total + anchor_ref[rows, :]
        if not final:
            out_ref[rows, :] = blended.astype(out_ref.dtype)
        else:
            first = first_ref[rows, :]
            classes = 2 * width
            factor = classes / jnp.sum(first + blended, axis=1, keepdims=True)
            out_ref[rows, :width] = first * factor
            out_ref[rows, width:] = blended * factor


def spread_blocks(index, core, tiles, weight, anchor, pieces, same, other, dtype, first=None):
    blocks_dev, degree, block, _ = tiles.shape
    width = anchor.shape[1]
    final = first is not None
    n_src = len(pieces)
    total = sum(s.shape[0] for s in pieces) + same.shape[0] + other.shape[0]
    return pl.pallas_call(
        functools.partial(spread_kernel, n_src=n_src, final=final),
        out_shape=jax.ShapeDtypeStruct((blocks_dev * block, width * (2 if final else 1)), dtype),
        in_specs=[SMEM, SMEM, VMEM, VMEM, VMEM] + [ANY] * n_src + [HBM, HBM] + [VMEM] * final,
        out_specs=VMEM,
        scratch_shapes=[
            pltpu.VMEM((total, block, width), jnp.bfloat16),
            pltpu.SemaphoreType.DMA((n_src + 2,)),
        ],
        cost_estimate=pl.CostEstimate(
            flops=2 * blocks_dev * degree * block * block * width,
            bytes_accessed=total * block * width * 2 + tiles.size * 2,
            transcendentals=0,
        ),
        name="spread",
    )(index, core, tiles, weight, anchor, *pieces, same, other, *([first] if final else []))


def local(adjacency_tiles, col_block, label_prior, seed_label, seed_mask):
    blocks_dev, degree, block, _ = adjacency_tiles.shape
    classes = label_prior.shape[1]
    width = classes // PARTS
    n_rows = lax.axis_size(GROUP)
    n_cols = lax.axis_size("x")
    n_chips = lax.axis_size("zy")
    group_size = n_cols * blocks_dev
    own_group = lax.axis_index(GROUP)
    own_col = lax.axis_index("x")
    own_core = lax.axis_index("core")
    owner_group = col_block // group_size
    within = col_block % group_size

    place = (within // blocks_dev + n_cols - own_col) % n_cols * blocks_dev + within % blocks_dev
    chip, core = owner_group // 2, owner_group % 2
    slot = group_size + chip + jnp.where(core == own_core, 0, n_chips)
    index = jnp.where(owner_group == own_group, place, slot).reshape(-1)
    asked = ask_blocks(owner_group, place, own_group, n_rows)
    anchor = prepare(label_prior, seed_label, seed_mask)

    row_sum = jnp.sum(adjacency_tiles.astype(jnp.float32), axis=(1, 3)).reshape(-1, 1)
    scale = 1.0 / (ALPHA * row_sum + (1.0 - ALPHA))
    weight = jnp.broadcast_to(ALPHA * scale, (blocks_dev * block, width))

    ranges = [slice(p * width, (p + 1) * width) for p in range(PARTS)]
    anchors = [(1.0 - ALPHA) * scale * anchor[:, r] for r in ranges]
    blended = [anchor[:, r].astype(jnp.bfloat16) for r in ranges]
    for hop in range(HOPS):
        last = hop == HOPS - 1
        for p in range(PARTS):
            own = blended[p].reshape(blocks_dev, block, width)
            pieces = [own] + [
                lax.ppermute(own, "x", [((x + d) % n_cols, x) for x in range(n_cols)])
                for d in range(1, n_cols)
            ]
            reply = reply_blocks(asked, pieces).reshape(n_chips, 2, block, width)
            same = lax.all_to_all(reply, "zy", 0, 0, tiled=True)
            other = lax.ppermute(same, "core", [(0, 1), (1, 0)])
            blended[p] = spread_blocks(
                index, own_core.reshape(1), adjacency_tiles, weight, anchors[p], pieces,
                same, other,
                jnp.float32 if last else jnp.bfloat16,
                blended[0] if last and p == 1 else None,
            )
    return blended[1]


def solution(mesh):
    n_rows, n_cols = mesh.devices.shape
    fine = Mesh(mesh.devices.reshape(n_rows // 2, 2, n_cols), AXES)
    in_specs = (
        P(AXES, None, None, None),
        P(AXES, None),
        P(AXES, None),
        P(AXES),
        P(AXES),
    )
    out_specs = P(AXES, None)
    return jax.shard_map(local, mesh=fine, in_specs=in_specs, out_specs=out_specs, check_vma=False)
```

time: 511 us -> 487 us (0.953)
  waiting for transfers between devices: 322 us -> 289 us
  blocking collectives: 0 us -> 20.5 us
  other arithmetic: 14.6 us -> 7.11 us
    all_to_all x9 -> x8, waiting for transfers between devices: 241 us -> 189 us  [local(): same = lax.all_to_all(reply, 'zy', 0, 0, tiled=True)]
    all_to_all x0 -> x1, blocking collectives: none -> 20.5 us  [ask_blocks(): lax.all_to_all(wanted.reshape(n_rows, 1), GROUP, 0, 0, tiled=True)[:, 0]]
    ppermute x24 -> x32, waiting for transfers between devices: 81.5 us -> 99.4 us  [the longest x24 74.9 us: local(): lax.ppermute(own, 'x', [((x + d) % n_cols, x) for x in range(n_cols)])]
    all_to_all x9 -> x8, starting transfers between devices: 61.4 us -> 49.6 us  [local(): same = lax.all_to_all(reply, 'zy', 0, 0, tiled=True)]
    ppermute x24 -> x32, starting transfers between devices: 22.4 us -> 33.1 us  [the longest x24 32.3 us: local(): lax.ppermute(own, 'x', [((x + d) % n_cols, x) for x in range(n_cols)])]
  transfers between devices with their start and end apart: 33 -> 40, of which waited for: 32 -> 35; matrix products, arithmetic and copies ran while one was open for 2% -> 1% of each run, Pallas kernels for 13% -> 13%
where the time goes in v2:
time: 487 us; the launch traced here: 484 us
  waiting for transfers between devices  289 us (59%)
  starting transfers between devices  82.7 us (17%)
  Pallas kernels  75.3 us (15%)
  blocking collectives  20.5 us (4%)
  local copies, waits for them, and re-layouts  8.66 us (2%)
  other arithmetic  7.11 us (1%)
    all_to_all x8, waiting for transfers between devices, local(): same = lax.all_to_all(reply, 'zy', 0, 0, tiled=True)  189 us
    ppermute x24, waiting for transfers between devices, local(): lax.ppermute(own, 'x', [((x + d) % n_cols, x) for x in range(n_cols)])  74.9 us
    all_to_all x8, starting transfers between devices, local(): same = lax.all_to_all(reply, 'zy', 0, 0, tiled=True)  49.6 us
    pallas_call x8, Pallas kernels, spread_blocks(): pl.pallas_call(functools.partial(spread_kernel, n_src=n_src, final=final)...  49.2 us
    ppermute x24, starting transfers between devices, local(): lax.ppermute(own, 'x', [((x + d) % n_cols, x) for x in range(n_cols)])  32.3 us
    pallas_call x8, Pallas kernels, reply_blocks(): pl.pallas_call(functools.partial(reply_kernel, n_cols=n_cols), out_shape=...  26.2 us
    ppermute x8, waiting for transfers between devices, local(): other = lax.ppermute(same, 'core', [(0, 1), (1, 0)])  24.5 us
    all_to_all x1, blocking collectives, ask_blocks(): lax.all_to_all(wanted.reshape(n_rows, 1), GROUP, 0, 0, tiled=True)[:, 0]  20.5 us
  transfers between devices with their start and end apart: 40, of which 35 were waited for; matrix products, arithmetic and copies ran while one was open for 1% of the time, Pallas kernels for 13%

profile of v2, /device:TPU:8, one launch (start us, length us, event | category | flops | bytes accessed | tf_op | source)
XLA Modules:
  0.0 483.6 jit_solution(2700412021423652812)
XLA Ops:
  8.8 20.5 %all_to_all.46 = s32[64,1,1]{2,1,0:T(1,128)S(1)} all-to-all(s32[64,1,1]{2,1,0:T(1,128)S(1)} %copy.8), channel_id=1, replica_groups=mesh['zy'=32,'core'=2,'x'=4] {'zy','core'}, dimensions={0} | all-to-all | bytes 512 | tf_op jit(solution)/shard_map/all_to_all | solution.py:40
  32.5 3.3 reply.12
  35.8 5.1 %all-to-all-start.5 = ((bf16[32,2,128,128]{3,2,1,0:T(8,128)(2,1)}), bf16[32,2,128,128]{3,2,1,0:T(8,128)(2,1)S(1)}, u32[]{:S(2)}, u32[]{:S(2)}) async-start(bf16[32,2,128,128]{3,2,1,0:T(8,128)(2,1)} %bitcast.29), calls=%async_computation.5 | async-start | bytes 4194304 | tf_op jit(solution)/shard_map/all_to_all | solution.py:180
  44.9 6.6 %collective-permute-done.refs_1_ = bf16[6,128,128]{2,1,0:T(8,128)(2,1)S(1)} collective-permute-done((bf16[6,128,128]{2,1,0:T(8,128)(2,1)S(1)}, bf16[6,128,128]{2,1,0:T(8,128)(2,1)S(1)}, u32[]{:S(2)}, u32[]{:S(2)}) %collective-permute-start) | collective-permute-done | bytes 196640 | tf_op jit(solution)/shard_map/ppermute | solution.py:176
  55.2 3.3 reply.8
  58.5 32.0 %all-to-all-done.5.refs_4_ = bf16[32,2,128,128]{3,2,1,0:T(8,128)(2,1)S(1)} async-done(((bf16[32,2,128,128]{3,2,1,0:T(8,128)(2,1)}), bf16[32,2,128,128]{3,2,1,0:T(8,128)(2,1)S(1)}, u32[]{:S(2)}, u32[]{:S(2)}) %all-to-all-start.5) | async-done | bytes 2097184 | tf_op jit(solution)/shard_map/all_to_all | solution.py:180
  91.9 7.1 %all-to-all-start.1 = ((bf16[32,2,128,128]{3,2,1,0:T(8,128)(2,1)}), bf16[32,2,128,128]{3,2,1,0:T(8,128)(2,1)}, u32[]{:S(2)}, u32[]{:S(2)}) async-start(bf16[32,2,128,128]{3,2,1,0:T(8,128)(2,1)} %bitcast.23), calls=%async_computation.1 | async-start | bytes 4194304 | tf_op jit(solution)/shard_map/all_to_all | solution.py:180
  104.4 6.0 %spread.11 = bf16[768,128]{1,0:T(8,128)(2,1)} custom-call(s32[72]{0:T(128)} %reshape.120.index_ref, s32[1]{0:T(128)} %bitcast.core_ref, bf16[6,12,128,128]{3,2,1,0:T(8,128)(2,1)} %tiles_ref.15, f32[768,128]{1,0:T(8,128)} %broadcast_in_dim.35.weight_ref, f32[768,128]{1,0:T(8,128)} %get-tuple-element.7.anchor_ref, bf16[6,128,128]{2,1,0:T(8,128)(2,1)} %bitcast.40, ...), custom_call_target="tpu_custom_call" | custom-call | flops 301989888 | bytes 5242880 | tf_op jit(solution)/shard_map/spread/pallas_call | solution.py:125
  114.4 7.5 %collective-permute-done.20.refs_1_ = bf16[6,128,128]{2,1,0:T(8,128)(2,1)S(1)} collective-permute-done((bf16[6,128,128]{2,1,0:T(8,128)(2,1)}, bf16[6,128,128]{2,1,0:T(8,128)(2,1)S(1)}, u32[]{:S(2)}, u32[]{:S(2)}) %collective-permute-start.20) | collective-permute-done | bytes 196640 | tf_op jit(solution)/shard_map/ppermute | solution.py:176
  122.4 3.1 collective-permute-done.22.refs_3_
  126.2 3.3 reply.13
  129.5 18.1 %all-to-all-done.1.refs_4_ = bf16[32,2,128,128]{3,2,1,0:T(8,128)(2,1)} async-done(((bf16[32,2,128,128]{3,2,1,0:T(8,128)(2,1)}), bf16[32,2,128,128]{3,2,1,0:T(8,128)(2,1)}, u32[]{:S(2)}, u32[]{:S(2)}) %all-to-all-start.1) | async-done | bytes 2097184 | tf_op jit(solution)/shard_map/all_to_all | solution.py:180
  147.6 6.7 %all-to-all-start.6 = ((bf16[32,2,128,128]{3,2,1,0:T(8,128)(2,1)}), bf16[32,2,128,128]{3,2,1,0:T(8,128)(2,1)S(1)}, u32[]{:S(2)}, u32[]{:S(2)}) async-start(bf16[32,2,128,128]{3,2,1,0:T(8,128)(2,1)} %bitcast.24), calls=%async_computation.6 | async-start | bytes 4194304 | tf_op jit(solution)/shard_map/all_to_all | solution.py:180
  154.6 4.5 collective-permute-done.3.refs_5_
  159.1 6.0 %spread.8 = bf16[768,128]{1,0:T(8,128)(2,1)} custom-call(s32[72]{0:T(128)} %reshape.120.index_ref, s32[1]{0:T(128)} %bitcast.core_ref, bf16[6,12,128,128]{3,2,1,0:T(8,128)(2,1)} %tiles_ref.15, f32[768,128]{1,0:T(8,128)} %broadcast_in_dim.35.weight_ref, f32[768,128]{1,0:T(8,128)} %get-tuple-element.8.anchor_ref, bf16[6,128,128]{2,1,0:T(8,128)(2,1)} %bitcast.35, ...), custom_call_target="tpu_custom_call" | custom-call | flops 301989888 | bytes 5242880 | tf_op jit(solution)/shard_map/spread/pallas_call | solution.py:125
  169.1 7.5 %collective-permute-done.4.refs_1_ = bf16[6,128,128]{2,1,0:T(8,128)(2,1)S(1)} collective-permute-done((bf16[6,128,128]{2,1,0:T(8,128)(2,1)}, bf16[6,128,128]{2,1,0:T(8,128)(2,1)S(1)}, u32[]{:S(2)}, u32[]{:S(2)}) %collective-permute-start.4) | collective-permute-done | bytes 196640 | tf_op jit(solution)/shard_map/ppermute | solution.py:176
  180.8 3.3 reply.9
  184.1 19.3 %all-to-all-done.6.refs_4_ = bf16[32,2,128,128]{3,2,1,0:T(8,128)(2,1)S(1)} async-done(((bf16[32,2,128,128]{3,2,1,0:T(8,128)(2,1)}), bf16[32,2,128,128]{3,2,1,0:T(8,128)(2,1)S(1)}, u32[]{:S(2)}, u32[]{:S(2)}) %all-to-all-start.6) | async-done | bytes 2097184 | tf_op jit(solution)/shard_map/all_to_all | solution.py:180
  203.4 5.6 %all-to-all-start.2 = ((bf16[32,2,128,128]{3,2,1,0:T(8,128)(2,1)}), bf16[32,2,128,128]{3,2,1,0:T(8,128)(2,1)}, u32[]{:S(2)}, u32[]{:S(2)}) async-start(bf16[32,2,128,128]{3,2,1,0:T(8,128)(2,1)} %bitcast.26), calls=%async_computation.2 | async-start | bytes 4194304 | tf_op jit(solution)/shard_map/all_to_all | solution.py:180
  209.1 4.3 collective-permute-done.23.refs_5_
  213.4 6.0 %spread.12 = bf16[768,128]{1,0:T(8,128)(2,1)} custom-call(s32[72]{0:T(128)} %reshape.120.index_ref, s32[1]{0:T(128)} %bitcast.core_ref, bf16[6,12,128,128]{3,2,1,0:T(8,128)(2,1)} %tiles_ref.15, f32[768,128]{1,0:T(8,128)} %broadcast_in_dim.35.weight_ref, f32[768,128]{1,0:T(8,128)} %get-tuple-element.7.anchor_ref, bf16[6,128,128]{2,1,0:T(8,128)(2,1)} %bitcast.50, ...), custom_call_target="tpu_custom_call" | custom-call | flops 301989888 | bytes 5242880 | tf_op jit(solution)/shard_map/spread/pallas_call | solution.py:125
  223.4 7.5 %collective-permute-done.24.refs_1_ = bf16[6,128,128]{2,1,0:T(8,128)(2,1)S(1)} collective-permute-done((bf16[6,128,128]{2,1,0:T(8,128)(2,1)}, bf16[6,128,128]{2,1,0:T(8,128)(2,1)S(1)}, u32[]{:S(2)}, u32[]{:S(2)}) %collective-permute-start.24) | collective-permute-done | bytes 196640 | tf_op jit(solution)/shard_map/ppermute | solution.py:176
  231.4 3.1 collective-permute-done.26.refs_3_
  235.2 3.3 reply.14
  238.4 18.1 %all-to-all-done.2.refs_4_ = bf16[32,2,128,128]{3,2,1,0:T(8,128)(2,1)} async-done(((bf16[32,2,128,128]{3,2,1,0:T(8,128)(2,1)}), bf16[32,2,128,128]{3,2,1,0:T(8,128)(2,1)}, u32[]{:S(2)}, u32[]{:S(2)}) %all-to-all-start.2) | async-done | bytes 2097184 | tf_op jit(solution)/shard_map/all_to_all | solution.py:180
  256.5 6.3 %all-to-all-start.7 = ((bf16[32,2,128,128]{3,2,1,0:T(8,128)(2,1)}), bf16[32,2,128,128]{3,2,1,0:T(8,128)(2,1)S(1)}, u32[]{:S(2)}, u32[]{:S(2)}) async-start(bf16[32,2,128,128]{3,2,1,0:T(8,128)(2,1)} %bitcast.27), calls=%async_computation.7 | async-start | bytes 4194304 | tf_op jit(solution)/shard_map/all_to_all | solution.py:180
  262.9 4.5 collective-permute-done.7.refs_5_
  267.4 6.0 %spread.9 = bf16[768,128]{1,0:T(8,128)(2,1)} custom-call(s32[72]{0:T(128)} %reshape.120.index_ref, s32[1]{0:T(128)} %bitcast.core_ref, bf16[6,12,128,128]{3,2,1,0:T(8,128)(2,1)} %tiles_ref.15, f32[768,128]{1,0:T(8,128)} %broadcast_in_dim.35.weight_ref, f32[768,128]{1,0:T(8,128)} %get-tuple-element.8.anchor_ref, bf16[6,128,128]{2,1,0:T(8,128)(2,1)} %bitcast.55, ...), custom_call_target="tpu_custom_call" | custom-call | flops 301989888 | bytes 5242880 | tf_op jit(solution)/shard_map/spread/pallas_call | solution.py:125
  277.5 4.7 collective-permute-done.10.refs_3_
  283.3 3.4 collective-permute-done.9.refs_2_
  287.3 3.3 reply.10
  290.6 19.4 %all-to-all-done.7.refs_4_ = bf16[32,2,128,128]{3,2,1,0:T(8,128)(2,1)S(1)} async-done(((bf16[32,2,128,128]{3,2,1,0:T(8,128)(2,1)}), bf16[32,2,128,128]{3,2,1,0:T(8,128)(2,1)S(1)}, u32[]{:S(2)}, u32[]{:S(2)}) %all-to-all-start.7) | async-done | bytes 2097184 | tf_op jit(solution)/shard_map/all_to_all | solution.py:180
  310.0 6.3 %all-to-all-start.3 = ((bf16[32,2,128,128]{3,2,1,0:T(8,128)(2,1)}), bf16[32,2,128,128]{3,2,1,0:T(8,128)(2,1)}, u32[]{:S(2)}, u32[]{:S(2)}) async-start(bf16[32,2,128,128]{3,2,1,0:T(8,128)(2,1)} %bitcast.28), calls=%async_computation.3 | async-start | bytes 4194304 | tf_op jit(solution)/shard_map/all_to_all | solution.py:180
  316.4 4.3 collective-permute-done.27.refs_5_
  320.7 6.0 %spread.13 = bf16[768,128]{1,0:T(8,128)(2,1)} custom-call(s32[72]{0:T(128)} %reshape.120.index_ref, s32[1]{0:T(128)} %bitcast.core_ref, bf16[6,12,128,128]{3,2,1,0:T(8,128)(2,1)} %tiles_ref.15, f32[768,128]{1,0:T(8,128)} %broadcast_in_dim.35.weight_ref, f32[768,128]{1,0:T(8,128)} %get-tuple-element.7.anchor_ref, bf16[6,128,128]{2,1,0:T(8,128)(2,1)} %bitcast.60, ...), custom_call_target="tpu_custom_call" | custom-call | flops 301989888 | bytes 5242880 | tf_op jit(solution)/shard_map/spread/pallas_call | solution.py:125
  330.7 7.5 %collective-permute-done.28.refs_1_ = bf16[6,128,128]{2,1,0:T(8,128)(2,1)S(1)} collective-permute-done((bf16[6,128,128]{2,1,0:T(8,128)(2,1)}, bf16[6,128,128]{2,1,0:T(8,128)(2,1)S(1)}, u32[]{:S(2)}, u32[]{:S(2)}) %collective-permute-start.28) | collective-permute-done | bytes 196640 | tf_op jit(solution)/shard_map/ppermute | solution.py:176
  342.4 3.3 reply.15
  345.7 17.8 %all-to-all-done.3.refs_4_ = bf16[32,2,128,128]{3,2,1,0:T(8,128)(2,1)} async-done(((bf16[32,2,128,128]{3,2,1,0:T(8,128)(2,1)}), bf16[32,2,128,128]{3,2,1,0:T(8,128)(2,1)}, u32[]{:S(2)}, u32[]{:S(2)}) %all-to-all-start.3) | async-done | bytes 2097184 | tf_op jit(solution)/shard_map/all_to_all | solution.py:180
  363.5 6.3 %all-to-all-start.8 = ((bf16[32,2,128,128]{3,2,1,0:T(8,128)(2,1)}), bf16[32,2,128,128]{3,2,1,0:T(8,128)(2,1)S(1)}, u32[]{:S(2)}, u32[]{:S(2)}) async-start(bf16[32,2,128,128]{3,2,1,0:T(8,128)(2,1)} %bitcast.25), calls=%async_computation.8 | async-start | bytes 4194304 | tf_op jit(solution)/shard_map/all_to_all | solution.py:180
  369.9 4.5 collective-permute-done.11.refs_5_
  374.4 6.0 %spread.10 = bf16[768,128]{1,0:T(8,128)(2,1)} custom-call(s32[72]{0:T(128)} %reshape.120.index_ref, s32[1]{0:T(128)} %bitcast.core_ref, bf16[6,12,128,128]{3,2,1,0:T(8,128)(2,1)} %tiles_ref.15, f32[768,128]{1,0:T(8,128)} %broadcast_in_dim.35.weight_ref, f32[768,128]{1,0:T(8,128)} %get-tuple-element.8.anchor_ref, bf16[6,128,128]{2,1,0:T(8,128)(2,1)} %bitcast.65, ...), custom_call_target="tpu_custom_call" | custom-call | flops 301989888 | bytes 5242880 | tf_op jit(solution)/shard_map/spread/pallas_call | solution.py:125
  384.4 7.5 %collective-permute-done.12.refs_1_ = bf16[6,128,128]{2,1,0:T(8,128)(2,1)S(1)} collective-permute-done((bf16[6,128,128]{2,1,0:T(8,128)(2,1)}, bf16[6,128,128]{2,1,0:T(8,128)(2,1)S(1)}, u32[]{:S(2)}, u32[]{:S(2)}) %collective-permute-start.12) | collective-permute-done | bytes 196640 | tf_op jit(solution)/shard_map/ppermute | solution.py:176
  396.1 3.3 reply.11
  399.4 17.6 %all-to-all-done.8.refs_4_ = bf16[32,2,128,128]{3,2,1,0:T(8,128)(2,1)S(1)} async-done(((bf16[32,2,128,128]{3,2,1,0:T(8,128)(2,1)}), bf16[32,2,128,128]{3,2,1,0:T(8,128)(2,1)S(1)}, u32[]{:S(2)}, u32[]{:S(2)}) %all-to-all-start.8) | async-done | bytes 2097184 | tf_op jit(solution)/shard_map/all_to_all | solution.py:180
  416.9 6.3 %all-to-all-start.4 = ((bf16[32,2,128,128]{3,2,1,0:T(8,128)(2,1)}), bf16[32,2,128,128]{3,2,1,0:T(8,128)(2,1)}, u32[]{:S(2)}, u32[]{:S(2)}) async-start(bf16[32,2,128,128]{3,2,1,0:T(8,128)(2,1)} %bitcast.30), calls=%async_computation.4 | async-start | bytes 4194304 | tf_op jit(solution)/shard_map/all_to_all | solution.py:180
  423.4 47.1 %all-to-all-done.4.refs_4_ = bf16[32,2,128,128]{3,2,1,0:T(8,128)(2,1)} async-done(((bf16[32,2,128,128]{3,2,1,0:T(8,128)(2,1)}), bf16[32,2,128,128]{3,2,1,0:T(8,128)(2,1)}, u32[]{:S(2)}, u32[]{:S(2)}) %all-to-all-start.4) | async-done | bytes 2097184 | tf_op jit(solution)/shard_map/all_to_all | solution.py:180
  470.5 6.1 %spread.14.refs_6_ = f32[768,128]{1,0:T(8,128)} custom-call(s32[72]{0:T(128)} %reshape.120.index_ref, s32[1]{0:T(128)} %bitcast.core_ref, bf16[6,12,128,128]{3,2,1,0:T(8,128)(2,1)} %tiles_ref.15, f32[768,128]{1,0:T(8,128)} %broadcast_in_dim.35.weight_ref, f32[768,128]{1,0:T(8,128)} %get-tuple-element.7.anchor_ref, bf16[6,128,128]{2,1,0:T(8,128)(2,1)} %bitcast.45, ...), custom_call_target="tpu_custom_call" | custom-call | flops 301989888 | bytes 5242880 | tf_op jit(solution)/shard_map/spread/pallas_call | solution.py:125
  476.6 6.9 %spread.15 = f32[768,256]{1,0:T(8,128)} custom-call(s32[72]{0:T(128)} %reshape.120.index_ref, s32[1]{0:T(128)} %bitcast.core_ref, bf16[6,12,128,128]{3,2,1,0:T(8,128)(2,1)} %tiles_ref.15, f32[768,128]{1,0:T(8,128)} %broadcast_in_dim.35.weight_ref, f32[768,128]{1,0:T(8,128)} %get-tuple-element.8.anchor_ref, bf16[6,128,128]{2,1,0:T(8,128)(2,1)} %bitcast.70, ...), custom_call_target="tpu_custom_call" | custom-call | flops 301989888 | bytes 5242880 | tf_op jit(solution)/shard_map/spread/pallas_call | solution.py:125
  (128 shorter events, 68.0 us)
Async XLA Ops:
  0.0 8.4 %copy-start.30 = (s32[6,12]{1,0:T(8,128)S(1)}, s32[6,12]{1,0:T(8,128)}, u32[]{:S(2)}) copy-start(s32[6,12]{1,0:T(8,128)} %param.6) | copy-start | bytes 868
  3.8 27.3 %copy-start.6 = (bf16[768,128]{1,0:T(8,128)(2,1)}, bf16[768,128]{1,0:T(8,128)(2,1)S(1)}, u32[]{:S(2)}) copy-start(bf16[768,128]{1,0:T(8,128)(2,1)S(1)} %get-tuple-element.9) | copy-start | bytes 589828
  3.8 41.0 %copy-start.5 = (bf16[768,128]{1,0:T(8,128)(2,1)}, bf16[768,128]{1,0:T(8,128)(2,1)S(1)}, u32[]{:S(2)}) copy-start(bf16[768,128]{1,0:T(8,128)(2,1)S(1)} %get-tuple-element.10) | copy-start | bytes 589828
  3.8 27.2 %collective-permute-start.16 = (bf16[6,128,128]{2,1,0:T(8,128)(2,1)S(1)}, bf16[6,128,128]{2,1,0:T(8,128)(2,1)S(1)}, u32[]{:S(2)}, u32[]{:S(2)}) collective-permute-start(bf16[6,128,128]{2,1,0:T(8,128)(2,1)S(1)} %bitcast.36), channel_id=1, source_target_pairs={{1,0},{2,1},{3,2},{0,3},{5,4},{6,5},{7,6},{4,7},{9,8},{10,9},{11,1... | collective-permute-start | bytes 589832 | tf_op jit(solution)/shard_map/ppermute | solution.py:176
  6.7 24.4 %collective-permute-start.17 = (bf16[6,128,128]{2,1,0:T(8,128)(2,1)S(1)}, bf16[6,128,128]{2,1,0:T(8,128)(2,1)S(1)}, u32[]{:S(2)}, u32[]{:S(2)}) collective-permute-start(bf16[6,128,128]{2,1,0:T(8,128)(2,1)S(1)} %bitcast.37), channel_id=1, source_target_pairs={{2,0},{3,1},{0,2},{1,3},{6,4},{7,5},{4,6},{5,7},{10,8},{11,9},{8,1... | collective-permute-start | bytes 589832 | tf_op jit(solution)/shard_map/ppermute | solution.py:176
  7.5 23.6 %collective-permute-start.18 = (bf16[6,128,128]{2,1,0:T(8,128)(2,1)S(1)}, bf16[6,128,128]{2,1,0:T(8,128)(2,1)S(1)}, u32[]{:S(2)}, u32[]{:S(2)}) collective-permute-start(bf16[6,128,128]{2,1,0:T(8,128)(2,1)S(1)} %bitcast.38), channel_id=1, source_target_pairs={{3,0},{0,1},{1,2},{2,3},{7,4},{4,5},{5,6},{6,7},{11,8},{8,9},{9,10... | collective-permute-start | bytes 589832 | tf_op jit(solution)/shard_map/ppermute | solution.py:176
  35.8 54.7 %all-to-all-start.5 = ((bf16[32,2,128,128]{3,2,1,0:T(8,128)(2,1)}), bf16[32,2,128,128]{3,2,1,0:T(8,128)(2,1)S(1)}, u32[]{:S(2)}, u32[]{:S(2)}) async-start(bf16[32,2,128,128]{3,2,1,0:T(8,128)(2,1)} %bitcast.29), calls=%async_computation.5 | async-start | bytes 4194304 | tf_op jit(solution)/shard_map/all_to_all | solution.py:180
  40.9 10.6 %collective-permute-start = (bf16[6,128,128]{2,1,0:T(8,128)(2,1)S(1)}, bf16[6,128,128]{2,1,0:T(8,128)(2,1)S(1)}, u32[]{:S(2)}, u32[]{:S(2)}) collective-permute-start(bf16[6,128,128]{2,1,0:T(8,128)(2,1)S(1)} %bitcast.31), channel_id=1, source_target_pairs={{1,0},{2,1},{3,2},{0,3},{5,4},{6,5},{7,6},{4,7},{9,8},{10,9},{11,1... | collective-permute-start | bytes 589832 | tf_op jit(solution)/shard_map/ppermute | solution.py:176
  43.3 9.3 %collective-permute-start.1 = (bf16[6,128,128]{2,1,0:T(8,128)(2,1)S(1)}, bf16[6,128,128]{2,1,0:T(8,128)(2,1)S(1)}, u32[]{:S(2)}, u32[]{:S(2)}) collective-permute-start(bf16[6,128,128]{2,1,0:T(8,128)(2,1)S(1)} %bitcast.32), channel_id=1, source_target_pairs={{2,0},{3,1},{0,2},{1,3},{6,4},{7,5},{4,6},{5,7},{10,8},{11,9},{8,1... | collective-permute-start | bytes 589832 | tf_op jit(solution)/shard_map/ppermute | solution.py:176
  44.9 10.4 %collective-permute-start.2 = (bf16[6,128,128]{2,1,0:T(8,128)(2,1)S(1)}, bf16[6,128,128]{2,1,0:T(8,128)(2,1)}, u32[]{:S(2)}, u32[]{:S(2)}) collective-permute-start(bf16[6,128,128]{2,1,0:T(8,128)(2,1)S(1)} %bitcast.33), channel_id=1, source_target_pairs={{3,0},{0,1},{1,2},{2,3},{7,4},{4,5},{5,6},{6,7},{11,8},{8,9},{9,10... | collective-permute-start | bytes 589832 | tf_op jit(solution)/shard_map/ppermute | solution.py:176
  91.9 7.7 %copy-start = (bf16[6,12,128,128]{3,2,1,0:T(8,128)(2,1)S(1)}, bf16[6,12,128,128]{3,2,1,0:T(8,128)(2,1)}, u32[]{:S(2)}) copy-start(bf16[6,12,128,128]{3,2,1,0:T(8,128)(2,1)} %tiles_ref.15) | copy-start | bytes 7077892
  91.9 55.7 %all-to-all-start.1 = ((bf16[32,2,128,128]{3,2,1,0:T(8,128)(2,1)}), bf16[32,2,128,128]{3,2,1,0:T(8,128)(2,1)}, u32[]{:S(2)}, u32[]{:S(2)}) async-start(bf16[32,2,128,128]{3,2,1,0:T(8,128)(2,1)} %bitcast.23), calls=%async_computation.1 | async-start | bytes 4194304 | tf_op jit(solution)/shard_map/all_to_all | solution.py:180
  98.9 4.6 collective-permute-start.19
  110.5 11.5 %collective-permute-start.20 = (bf16[6,128,128]{2,1,0:T(8,128)(2,1)}, bf16[6,128,128]{2,1,0:T(8,128)(2,1)S(1)}, u32[]{:S(2)}, u32[]{:S(2)}) collective-permute-start(bf16[6,128,128]{2,1,0:T(8,128)(2,1)} %bitcast.46), channel_id=1, source_target_pairs={{1,0},{2,1},{3,2},{0,3},{5,4},{6,5},{7,6},{4,7},{9,8},{10,9},{11,1... | collective-permute-start | bytes 589832 | tf_op jit(solution)/shard_map/ppermute | solution.py:176
  112.9 9.5 %collective-permute-start.21 = (bf16[6,128,128]{2,1,0:T(8,128)(2,1)}, bf16[6,128,128]{2,1,0:T(8,128)(2,1)S(1)}, u32[]{:S(2)}, u32[]{:S(2)}) collective-permute-start(bf16[6,128,128]{2,1,0:T(8,128)(2,1)} %bitcast.47), channel_id=1, source_target_pairs={{2,0},{3,1},{0,2},{1,3},{6,4},{7,5},{4,6},{5,7},{10,8},{11,9},{8,1... | collective-permute-start | bytes 589832 | tf_op jit(solution)/shard_map/ppermute | solution.py:176
  114.4 11.1 %collective-permute-start.22 = (bf16[6,128,128]{2,1,0:T(8,128)(2,1)}, bf16[6,128,128]{2,1,0:T(8,128)(2,1)S(1)}, u32[]{:S(2)}, u32[]{:S(2)}) collective-permute-start(bf16[6,128,128]{2,1,0:T(8,128)(2,1)} %bitcast.48), channel_id=1, source_target_pairs={{3,0},{0,1},{1,2},{2,3},{7,4},{4,5},{5,6},{6,7},{11,8},{8,9},{9,10... | collective-permute-start | bytes 589832 | tf_op jit(solution)/shard_map/ppermute | solution.py:176
  147.6 55.8 %all-to-all-start.6 = ((bf16[32,2,128,128]{3,2,1,0:T(8,128)(2,1)}), bf16[32,2,128,128]{3,2,1,0:T(8,128)(2,1)S(1)}, u32[]{:S(2)}, u32[]{:S(2)}) async-start(bf16[32,2,128,128]{3,2,1,0:T(8,128)(2,1)} %bitcast.24), calls=%async_computation.6 | async-start | bytes 4194304 | tf_op jit(solution)/shard_map/all_to_all | solution.py:180
  154.3 4.8 collective-permute-start.3
  165.1 11.5 %collective-permute-start.4 = (bf16[6,128,128]{2,1,0:T(8,128)(2,1)}, bf16[6,128,128]{2,1,0:T(8,128)(2,1)S(1)}, u32[]{:S(2)}, u32[]{:S(2)}) collective-permute-start(bf16[6,128,128]{2,1,0:T(8,128)(2,1)} %bitcast.51), channel_id=1, source_target_pairs={{1,0},{2,1},{3,2},{0,3},{5,4},{6,5},{7,6},{4,7},{9,8},{10,9},{11,1... | collective-permute-start | bytes 589832 | tf_op jit(solution)/shard_map/ppermute | solution.py:176
  167.5 9.5 %collective-permute-start.5 = (bf16[6,128,128]{2,1,0:T(8,128)(2,1)}, bf16[6,128,128]{2,1,0:T(8,128)(2,1)S(1)}, u32[]{:S(2)}, u32[]{:S(2)}) collective-permute-start(bf16[6,128,128]{2,1,0:T(8,128)(2,1)} %bitcast.52), channel_id=1, source_target_pairs={{2,0},{3,1},{0,2},{1,3},{6,4},{7,5},{4,6},{5,7},{10,8},{11,9},{8,1... | collective-permute-start | bytes 589832 | tf_op jit(solution)/shard_map/ppermute | solution.py:176
  169.0 11.1 %collective-permute-start.6 = (bf16[6,128,128]{2,1,0:T(8,128)(2,1)}, bf16[6,128,128]{2,1,0:T(8,128)(2,1)S(1)}, u32[]{:S(2)}, u32[]{:S(2)}) collective-permute-start(bf16[6,128,128]{2,1,0:T(8,128)(2,1)} %bitcast.53), channel_id=1, source_target_pairs={{3,0},{0,1},{1,2},{2,3},{7,4},{4,5},{5,6},{6,7},{11,8},{8,9},{9,10... | collective-permute-start | bytes 589832 | tf_op jit(solution)/shard_map/ppermute | solution.py:176
  203.4 5.6 %copy-start.3 = (bf16[32,2,128,128]{3,2,1,0:T(8,128)(2,1)}, bf16[32,2,128,128]{3,2,1,0:T(8,128)(2,1)S(1)}, u32[]{:S(2)}) copy-start(bf16[32,2,128,128]{3,2,1,0:T(8,128)(2,1)S(1)} %all-to-all-done.6.refs_4_) | copy-start | bytes 6291460
  203.4 53.1 %all-to-all-start.2 = ((bf16[32,2,128,128]{3,2,1,0:T(8,128)(2,1)}), bf16[32,2,128,128]{3,2,1,0:T(8,128)(2,1)}, u32[]{:S(2)}, u32[]{:S(2)}) async-start(bf16[32,2,128,128]{3,2,1,0:T(8,128)(2,1)} %bitcast.26), calls=%async_computation.2 | async-start | bytes 4194304 | tf_op jit(solution)/shard_map/all_to_all | solution.py:180
  209.0 4.4 collective-permute-start.23
  219.5 11.5 %collective-permute-start.24 = (bf16[6,128,128]{2,1,0:T(8,128)(2,1)}, bf16[6,128,128]{2,1,0:T(8,128)(2,1)S(1)}, u32[]{:S(2)}, u32[]{:S(2)}) collective-permute-start(bf16[6,128,128]{2,1,0:T(8,128)(2,1)} %bitcast.56), channel_id=1, source_target_pairs={{1,0},{2,1},{3,2},{0,3},{5,4},{6,5},{7,6},{4,7},{9,8},{10,9},{11,1... | collective-permute-start | bytes 589832 | tf_op jit(solution)/shard_map/ppermute | solution.py:176
  221.9 9.5 %collective-permute-start.25 = (bf16[6,128,128]{2,1,0:T(8,128)(2,1)}, bf16[6,128,128]{2,1,0:T(8,128)(2,1)S(1)}, u32[]{:S(2)}, u32[]{:S(2)}) collective-permute-start(bf16[6,128,128]{2,1,0:T(8,128)(2,1)} %bitcast.57), channel_id=1, source_target_pairs={{2,0},{3,1},{0,2},{1,3},{6,4},{7,5},{4,6},{5,7},{10,8},{11,9},{8,1... | collective-permute-start | bytes 589832 | tf_op jit(solution)/shard_map/ppermute | solution.py:176
  223.4 11.1 %collective-permute-start.26 = (bf16[6,128,128]{2,1,0:T(8,128)(2,1)}, bf16[6,128,128]{2,1,0:T(8,128)(2,1)S(1)}, u32[]{:S(2)}, u32[]{:S(2)}) collective-permute-start(bf16[6,128,128]{2,1,0:T(8,128)(2,1)} %bitcast.58), channel_id=1, source_target_pairs={{3,0},{0,1},{1,2},{2,3},{7,4},{4,5},{5,6},{6,7},{11,8},{8,9},{9,10... | collective-permute-start | bytes 589832 | tf_op jit(solution)/shard_map/ppermute | solution.py:176
  256.5 53.4 %all-to-all-start.7 = ((bf16[32,2,128,128]{3,2,1,0:T(8,128)(2,1)}), bf16[32,2,128,128]{3,2,1,0:T(8,128)(2,1)S(1)}, u32[]{:S(2)}, u32[]{:S(2)}) async-start(bf16[32,2,128,128]{3,2,1,0:T(8,128)(2,1)} %bitcast.27), calls=%async_computation.7 | async-start | bytes 4194304 | tf_op jit(solution)/shard_map/all_to_all | solution.py:180
  262.8 4.6 collective-permute-start.7
  273.4 8.7 %collective-permute-start.10 = (bf16[6,128,128]{2,1,0:T(8,128)(2,1)}, bf16[6,128,128]{2,1,0:T(8,128)(2,1)S(1)}, u32[]{:S(2)}, u32[]{:S(2)}) collective-permute-start(bf16[6,128,128]{2,1,0:T(8,128)(2,1)} %bitcast.61), channel_id=1, source_target_pairs={{3,0},{0,1},{1,2},{2,3},{7,4},{4,5},{5,6},{6,7},{11,8},{8,9},{9,10... | collective-permute-start | bytes 589832 | tf_op jit(solution)/shard_map/ppermute | solution.py:176
  275.3 8.0 %collective-permute-start.8 = (bf16[6,128,128]{2,1,0:T(8,128)(2,1)}, bf16[6,128,128]{2,1,0:T(8,128)(2,1)S(1)}, u32[]{:S(2)}, u32[]{:S(2)}) collective-permute-start(bf16[6,128,128]{2,1,0:T(8,128)(2,1)} %bitcast.62), channel_id=1, source_target_pairs={{1,0},{2,1},{3,2},{0,3},{5,4},{6,5},{7,6},{4,7},{9,8},{10,9},{11,1... | collective-permute-start | bytes 589832 | tf_op jit(solution)/shard_map/ppermute | solution.py:176
  276.7 9.9 %collective-permute-start.9 = (bf16[6,128,128]{2,1,0:T(8,128)(2,1)}, bf16[6,128,128]{2,1,0:T(8,128)(2,1)S(1)}, u32[]{:S(2)}, u32[]{:S(2)}) collective-permute-start(bf16[6,128,128]{2,1,0:T(8,128)(2,1)} %bitcast.63), channel_id=1, source_target_pairs={{2,0},{3,1},{0,2},{1,3},{6,4},{7,5},{4,6},{5,7},{10,8},{11,9},{8,1... | collective-permute-start | bytes 589832 | tf_op jit(solution)/shard_map/ppermute | solution.py:176
  282.1 4.5 copy-start.18
  310.0 6.3 %copy-start.4 = (bf16[32,2,128,128]{3,2,1,0:T(8,128)(2,1)}, bf16[32,2,128,128]{3,2,1,0:T(8,128)(2,1)S(1)}, u32[]{:S(2)}) copy-start(bf16[32,2,128,128]{3,2,1,0:T(8,128)(2,1)S(1)} %all-to-all-done.7.refs_4_) | copy-start | bytes 6291460
  310.0 53.5 %all-to-all-start.3 = ((bf16[32,2,128,128]{3,2,1,0:T(8,128)(2,1)}), bf16[32,2,128,128]{3,2,1,0:T(8,128)(2,1)}, u32[]{:S(2)}, u32[]{:S(2)}) async-start(bf16[32,2,128,128]{3,2,1,0:T(8,128)(2,1)} %bitcast.28), calls=%async_computation.3 | async-start | bytes 4194304 | tf_op jit(solution)/shard_map/all_to_all | solution.py:180
  316.3 4.4 collective-permute-start.27
  326.7 11.5 %collective-permute-start.28 = (bf16[6,128,128]{2,1,0:T(8,128)(2,1)}, bf16[6,128,128]{2,1,0:T(8,128)(2,1)S(1)}, u32[]{:S(2)}, u32[]{:S(2)}) collective-permute-start(bf16[6,128,128]{2,1,0:T(8,128)(2,1)} %bitcast.41), channel_id=1, source_target_pairs={{1,0},{2,1},{3,2},{0,3},{5,4},{6,5},{7,6},{4,7},{9,8},{10,9},{11,1... | collective-permute-start | bytes 589832 | tf_op jit(solution)/shard_map/ppermute | solution.py:176
  329.2 9.5 %collective-permute-start.29 = (bf16[6,128,128]{2,1,0:T(8,128)(2,1)}, bf16[6,128,128]{2,1,0:T(8,128)(2,1)S(1)}, u32[]{:S(2)}, u32[]{:S(2)}) collective-permute-start(bf16[6,128,128]{2,1,0:T(8,128)(2,1)} %bitcast.42), channel_id=1, source_target_pairs={{2,0},{3,1},{0,2},{1,3},{6,4},{7,5},{4,6},{5,7},{10,8},{11,9},{8,1... | collective-permute-start | bytes 589832 | tf_op jit(solution)/shard_map/ppermute | solution.py:176
  330.7 11.1 %collective-permute-start.30 = (bf16[6,128,128]{2,1,0:T(8,128)(2,1)}, bf16[6,128,128]{2,1,0:T(8,128)(2,1)S(1)}, u32[]{:S(2)}, u32[]{:S(2)}) collective-permute-start(bf16[6,128,128]{2,1,0:T(8,128)(2,1)} %bitcast.43), channel_id=1, source_target_pairs={{3,0},{0,1},{1,2},{2,3},{7,4},{4,5},{5,6},{6,7},{11,8},{8,9},{9,10... | collective-permute-start | bytes 589832 | tf_op jit(solution)/shard_map/ppermute | solution.py:176
  363.5 53.4 %all-to-all-start.8 = ((bf16[32,2,128,128]{3,2,1,0:T(8,128)(2,1)}), bf16[32,2,128,128]{3,2,1,0:T(8,128)(2,1)S(1)}, u32[]{:S(2)}, u32[]{:S(2)}) async-start(bf16[32,2,128,128]{3,2,1,0:T(8,128)(2,1)} %bitcast.25), calls=%async_computation.8 | async-start | bytes 4194304 | tf_op jit(solution)/shard_map/all_to_all | solution.py:180
  369.8 4.6 collective-permute-start.11
  380.4 11.5 %collective-permute-start.12 = (bf16[6,128,128]{2,1,0:T(8,128)(2,1)}, bf16[6,128,128]{2,1,0:T(8,128)(2,1)S(1)}, u32[]{:S(2)}, u32[]{:S(2)}) collective-permute-start(bf16[6,128,128]{2,1,0:T(8,128)(2,1)} %bitcast.66), channel_id=1, source_target_pairs={{1,0},{2,1},{3,2},{0,3},{5,4},{6,5},{7,6},{4,7},{9,8},{10,9},{11,1... | collective-permute-start | bytes 589832 | tf_op jit(solution)/shard_map/ppermute | solution.py:176
  382.8 9.5 %collective-permute-start.13 = (bf16[6,128,128]{2,1,0:T(8,128)(2,1)}, bf16[6,128,128]{2,1,0:T(8,128)(2,1)S(1)}, u32[]{:S(2)}, u32[]{:S(2)}) collective-permute-start(bf16[6,128,128]{2,1,0:T(8,128)(2,1)} %bitcast.67), channel_id=1, source_target_pairs={{2,0},{3,1},{0,2},{1,3},{6,4},{7,5},{4,6},{5,7},{10,8},{11,9},{8,1... | collective-permute-start | bytes 589832 | tf_op jit(solution)/shard_map/ppermute | solution.py:176
  384.3 11.1 %collective-permute-start.14 = (bf16[6,128,128]{2,1,0:T(8,128)(2,1)}, bf16[6,128,128]{2,1,0:T(8,128)(2,1)S(1)}, u32[]{:S(2)}, u32[]{:S(2)}) collective-permute-start(bf16[6,128,128]{2,1,0:T(8,128)(2,1)} %bitcast.68), channel_id=1, source_target_pairs={{3,0},{0,1},{1,2},{2,3},{7,4},{4,5},{5,6},{6,7},{11,8},{8,9},{9,10... | collective-permute-start | bytes 589832 | tf_op jit(solution)/shard_map/ppermute | solution.py:176
  416.9 6.3 %copy-start.1 = (bf16[32,2,128,128]{3,2,1,0:T(8,128)(2,1)}, bf16[32,2,128,128]{3,2,1,0:T(8,128)(2,1)S(1)}, u32[]{:S(2)}) copy-start(bf16[32,2,128,128]{3,2,1,0:T(8,128)(2,1)S(1)} %all-to-all-done.8.refs_4_) | copy-start | bytes 6291460
  416.9 53.5 %all-to-all-start.4 = ((bf16[32,2,128,128]{3,2,1,0:T(8,128)(2,1)}), bf16[32,2,128,128]{3,2,1,0:T(8,128)(2,1)}, u32[]{:S(2)}, u32[]{:S(2)}) async-start(bf16[32,2,128,128]{3,2,1,0:T(8,128)(2,1)} %bitcast.30), calls=%async_computation.4 | async-start | bytes 4194304 | tf_op jit(solution)/shard_map/all_to_all | solution.py:180
  423.3 47.2 %collective-permute-start.31 = (bf16[32,2,128,128]{3,2,1,0:T(8,128)(2,1)S(1)}, bf16[32,2,128,128]{3,2,1,0:T(8,128)(2,1)}, u32[]{:S(2)}, u32[]{:S(2)}) collective-permute-start(bf16[32,2,128,128]{3,2,1,0:T(8,128)(2,1)S(1)} %all-to-all-done.8.refs_4_), channel_id=1, source_target_pairs={{0,4},{4,0},{1,5},{5,1},{2,6},{6,2},{3,7},{7,3},{8,12},{12,8},{9,1... | collective-permute-start | bytes 6291464 | tf_op jit(solution)/shard_map/ppermute | solution.py:181
  470.5 6.1 %collective-permute-start.15 = (bf16[32,2,128,128]{3,2,1,0:T(8,128)(2,1)}, bf16[32,2,128,128]{3,2,1,0:T(8,128)(2,1)}, u32[]{:S(2)}, u32[]{:S(2)}) collective-permute-start(bf16[32,2,128,128]{3,2,1,0:T(8,128)(2,1)} %all-to-all-done.4.refs_4_), channel_id=1, source_target_pairs={{0,4},{4,0},{1,5},{5,1},{2,6},{6,2},{3,7},{7,3},{8,12},{12,8},{9,1... | collective-permute-start | bytes 6291464 | tf_op jit(solution)/shard_map/ppermute | solution.py:181
  (23 other events, 50.4 us)

commit v3 on v2

v3 whole, which is shorter than its diff:
```python
import functools

import jax
import jax.numpy as jnp
from jax import lax
from jax.experimental import pallas as pl
from jax.experimental.pallas import tpu as pltpu
from jax.sharding import Mesh
from jax.sharding import PartitionSpec as P

HOPS = 4
PARTS = 2
AXES = ("zy", "core", "x")
GROUP = ("zy", "core")
LANES = 128


ALPHA = 0.85
SEED_BOOST = 8.0

ANY = pl.BlockSpec(memory_space=pl.ANY)
VMEM = pl.BlockSpec(memory_space=pltpu.VMEM)
SMEM = pl.BlockSpec(memory_space=pltpu.SMEM)
HBM = pl.BlockSpec(memory_space=pltpu.HBM)


def ask_blocks(owner_group, place, own_group, n_rows):
    group_ids = jnp.arange(n_rows, dtype=jnp.int32)
    matched = owner_group.reshape(-1)[:, None] == group_ids[None, :]
    wanted = jnp.max(jnp.where(matched, place.reshape(-1)[:, None], 0), axis=0)
    wanted = jnp.where(group_ids == own_group, 0, wanted).reshape(n_rows // 2, 2)
    own_core = lax.axis_index("core")
    other = lax.ppermute(wanted, "core", [(0, 1), (1, 0)])
    lane = jnp.arange(LANES, dtype=jnp.int32)[None, :]
    mine = jnp.where(own_core == 0, wanted[:, :1], wanted[:, 1:])
    others = jnp.where(own_core == 0, other[:, :1], other[:, 1:])
    rows = jnp.where(lane % 2 == own_core, mine, others)
    return lax.all_to_all(rows, "zy", 0, 0, tiled=True)


def prepare_kernel(prior_ref, label_ref, mask_ref, anchor_ref, *sent_refs):
    nodes, classes = prior_ref.shape
    width = sent_refs[0].shape[1]

    @pl.loop(0, nodes // LANES)
    def _(b):
        rows = pl.ds(pl.multiple_of(b * LANES, LANES), LANES)
        label = jnp.broadcast_to(label_ref[rows][None, :], (LANES, LANES)).T
        boost = SEED_BOOST * jnp.broadcast_to(
            mask_ref[rows][None, :].astype(jnp.float32), (LANES, LANES)
        ).T
        lane = lax.broadcasted_iota(jnp.int32, (LANES, LANES), 1)
        raw = [
            prior_ref[rows, at : at + LANES] + jnp.where(label == lane + at, boost, 0.0)
            for at in range(0, classes, LANES)
        ]
        raw = jnp.concatenate(raw, axis=1)
        anchor = raw * (classes / jnp.sum(raw, axis=1, keepdims=True))
        anchor_ref[rows, :] = anchor
        for i, s in enumerate(sent_refs):
            s[rows, :] = anchor[:, i * width : (i + 1) * width].astype(jnp.bfloat16)


def prepare(label_prior, seed_label, seed_mask):
    nodes, classes = label_prior.shape
    sent = jax.ShapeDtypeStruct((nodes, classes // PARTS), jnp.bfloat16)
    anchor, *sent = pl.pallas_call(
        prepare_kernel,
        out_shape=[jax.ShapeDtypeStruct((nodes, classes), jnp.float32)] + [sent] * PARTS,
        in_specs=[VMEM, VMEM, VMEM],
        out_specs=[VMEM] * (1 + PARTS),
        cost_estimate=pl.CostEstimate(
            flops=8 * nodes * classes, bytes_accessed=10 * nodes * classes, transcendentals=0
        ),
        name="prepare",
    )(label_prior, seed_label, seed_mask)
    return anchor, sent


def reply_kernel(asked_ref, *refs, n_cols):
    parts, out_ref, table, in_sems, out_sem = refs[:n_cols], refs[n_cols], *refs[n_cols + 1 :]
    blocks_dev = parts[0].shape[0]
    n = out_ref.shape[0]
    loads = [
        pltpu.make_async_copy(p, table.at[pl.ds(i * blocks_dev, blocks_dev)], in_sems.at[i])
        for i, p in enumerate(parts)
    ]
    for c in loads:
        c.start()
    for c in loads:
        c.wait()

    @pl.loop(0, n // 2)
    def _(chip):
        for core in range(2):
            pltpu.make_async_copy(
                table.at[asked_ref[chip, core]], out_ref.at[2 * chip + core], out_sem
            ).start()

    pltpu.make_async_copy(out_ref, out_ref, out_sem).wait()


def reply_blocks(asked, parts):
    blocks_dev, block, width = parts[0].shape
    n = 2 * asked.shape[0]
    n_cols = len(parts)
    size = block * width * 2
    return pl.pallas_call(
        functools.partial(reply_kernel, n_cols=n_cols),
        out_shape=jax.ShapeDtypeStruct((n, block, width), jnp.bfloat16),
        in_specs=[SMEM] + [HBM] * n_cols,
        out_specs=ANY,
        scratch_shapes=[
            pltpu.VMEM((n_cols * blocks_dev, block, width), jnp.bfloat16),
            pltpu.SemaphoreType.DMA((n_cols,)),
            pltpu.SemaphoreType.DMA,
        ],
        cost_estimate=pl.CostEstimate(
            flops=4_000_000, bytes_accessed=(n + n_cols * blocks_dev) * size, transcendentals=0
        ),
        name="reply",
    )(asked, *parts)


def spread_kernel(index_ref, core_ref, tiles_ref, weight_ref, anchor_ref, *refs, n_src, final):
    sources = [s if len(s.shape) == 3 else s.at[:, core_ref[0]] for s in refs[:n_src]]
    first_ref = refs[n_src] if final else None
    out_ref, table, sems = refs[-3:]
    blocks_dev, degree, block, _ = tiles_ref.shape
    width = anchor_ref.shape[1]
    loads, at = [], 0
    for i, s in enumerate(sources):
        loads.append(pltpu.make_async_copy(s, table.at[pl.ds(at, s.shape[0])], sems.at[i]))
        at += s.shape[0]
    for c in loads:
        c.start()
    for c in loads:
        c.wait()

    def row_block(b):
        left = jnp.concatenate([tiles_ref[b, k] for k in range(degree)], axis=1)
        right = jnp.concatenate(
            [table[index_ref[b * degree + k]] for k in range(degree)], axis=0
        )
        total = jnp.dot(left, right, preferred_element_type=jnp.float32)
        rows = pl.ds(b * block if final else pl.multiple_of(b * block, block), block)
        blended = weight_ref[rows, :] * total + anchor_ref[rows, :]
        if not final:
            out_ref[rows, :] = blended.astype(out_ref.dtype)
        else:
            first = first_ref[rows, :]
            classes = 2 * width
            factor = classes / jnp.sum(first + blended, axis=1, keepdims=True)
            out_ref[rows, :width] = first * factor
            out_ref[rows, width:] = blended * factor

    if final:
        for b in range(blocks_dev):
            row_block(b)
    else:
        pl.loop(0, blocks_dev)(row_block)


def spread_blocks(index, core, tiles, weight, anchor, sources, dtype, first=None):
    blocks_dev, degree, block, _ = tiles.shape
    width = anchor.shape[1]
    final = first is not None
    n_src = len(sources)
    total = sum(s.shape[0] for s in sources)
    places = [ANY if len(s.shape) == 3 else HBM for s in sources]
    return pl.pallas_call(
        functools.partial(spread_kernel, n_src=n_src, final=final),
        out_shape=jax.ShapeDtypeStruct((blocks_dev * block, width * (2 if final else 1)), dtype),
        in_specs=[SMEM, SMEM, VMEM, VMEM, VMEM] + places + [VMEM] * final,
        out_specs=VMEM,
        scratch_shapes=[
            pltpu.VMEM((total, block, width), jnp.bfloat16),
            pltpu.SemaphoreType.DMA((n_src,)),
        ],
        cost_estimate=pl.CostEstimate(
            flops=2 * blocks_dev * degree * block * block * width,
            bytes_accessed=total * block * width * 2 + tiles.size * 2,
            transcendentals=0,
        ),
        name="spread",
    )(index, core, tiles, weight, anchor, *sources, *([first] if final else []))


def local(adjacency_tiles, col_block, label_prior, seed_label, seed_mask):
    blocks_dev, _, block, _ = adjacency_tiles.shape
    classes = label_prior.shape[1]
    width = classes // PARTS
    n_rows = lax.axis_size(GROUP)
    n_cols = lax.axis_size("x")
    n_chips = lax.axis_size("zy")
    group_size = n_cols * blocks_dev
    own_group = lax.axis_index(GROUP)
    own_col = lax.axis_index("x")
    own_core = lax.axis_index("core")
    owner_group = col_block // group_size
    within = col_block % group_size

    place = (within // blocks_dev + n_cols - own_col) % n_cols * blocks_dev + within % blocks_dev
    chip, core = owner_group // 2, owner_group % 2
    slot = group_size + chip + jnp.where(core == own_core, 0, n_chips)
    index = jnp.where(owner_group == own_group, place, slot).reshape(-1)
    index_last = jnp.where(owner_group == own_group, place, group_size + owner_group).reshape(-1)
    asked = ask_blocks(owner_group, place, own_group, n_rows)
    anchor, blended = prepare(label_prior, seed_label, seed_mask)

    row_sum = jnp.sum(adjacency_tiles.astype(jnp.float32), axis=(1, 3)).reshape(-1, 1)
    scale = 1.0 / (ALPHA * row_sum + (1.0 - ALPHA))
    weight = jnp.broadcast_to(ALPHA * scale, (blocks_dev * block, width))

    ranges = [slice(p * width, (p + 1) * width) for p in range(PARTS)]
    anchors = [(1.0 - ALPHA) * scale * anchor[:, r] for r in ranges]
    for hop in range(HOPS):
        last = hop == HOPS - 1
        for p in range(PARTS):
            own = blended[p].reshape(blocks_dev, block, width)
            pieces = [own] + [
                lax.ppermute(own, "x", [((x + d) % n_cols, x) for x in range(n_cols)])
                for d in range(1, n_cols)
            ]
            reply = reply_blocks(asked, pieces)
            if last and p == PARTS - 1:
                remote = [lax.all_to_all(reply, GROUP, 0, 0, tiled=True)]
            else:
                reply = reply.reshape(n_chips, 2, block, width)
                same = lax.all_to_all(reply, "zy", 0, 0, tiled=True)
                remote = [same, lax.ppermute(same, "core", [(0, 1), (1, 0)])]
            blended[p] = spread_blocks(
                index_last if len(remote) == 1 else index,
                own_core.reshape(1), adjacency_tiles, weight, anchors[p], pieces + remote,
                jnp.float32 if last else jnp.bfloat16,
                blended[0] if last and p == PARTS - 1 else None,
            )
    return blended[1]


def solution(mesh):
    n_rows, n_cols = mesh.devices.shape
    fine = Mesh(mesh.devices.reshape(n_rows // 2, 2, n_cols), AXES)
    in_specs = (
        P(AXES, None, None, None),
        P(AXES, None),
        P(AXES, None),
        P(AXES),
        P(AXES),
    )
    out_specs = P(AXES, None)

    return jax.shard_map(local, mesh=fine, in_specs=in_specs, out_specs=out_specs, check_vma=False)
```

time: 487 us -> 480 us (0.986)
  waiting for transfers between devices: 289 us -> 281 us
    all_to_all x8 -> x7, waiting for transfers between devices: 189 us -> 139 us  [local(): same = lax.all_to_all(reply, 'zy', 0, 0, tiled=True)]
    all_to_all x0 -> x1, waiting for transfers between devices: none -> 40.6 us  [local(): remote = [lax.all_to_all(reply, GROUP, 0, 0, tiled=True)]]
    all_to_all x8 -> x7, starting transfers between devices: 49.6 us -> 41.7 us  [local(): same = lax.all_to_all(reply, 'zy', 0, 0, tiled=True)]
    all_to_all x0 -> x1, starting transfers between devices: none -> 6.85 us  [local(): remote = [lax.all_to_all(reply, GROUP, 0, 0, tiled=True)]]
  transfers between devices with their start and end apart: 40 -> 40, of which waited for: 35 -> 36; matrix products, arithmetic and copies ran while one was open for 1% -> 1% of each run, Pallas kernels for 13% -> 14%
where the time goes in v3:
time: 480 us; the launch traced here: 477 us
  waiting for transfers between devices  281 us (59%)
  starting transfers between devices  83.1 us (17%)
  Pallas kernels  79.6 us (17%)
  blocking collectives  20 us (4%)
  local copies, waits for them, and re-layouts  10.1 us (2%)
    all_to_all x7, waiting for transfers between devices, local(): same = lax.all_to_all(reply, 'zy', 0, 0, tiled=True)  139 us
    ppermute x24, waiting for transfers between devices, local(): lax.ppermute(own, 'x', [((x + d) % n_cols, x) for x in range(n_cols)])  72.4 us
    pallas_call x8, Pallas kernels, spread_blocks(): pl.pallas_call(functools.partial(spread_kernel, n_src=n_src, final=final)...  48.1 us
    all_to_all x7, starting transfers between devices, local(): same = lax.all_to_all(reply, 'zy', 0, 0, tiled=True)  41.7 us
    all_to_all x1, waiting for transfers between devices, local(): remote = [lax.all_to_all(reply, GROUP, 0, 0, tiled=True)]  40.6 us
    ppermute x24, starting transfers between devices, local(): lax.ppermute(own, 'x', [((x + d) % n_cols, x) for x in range(n_cols)])  33.5 us
    pallas_call x8, Pallas kernels, reply_blocks(): pl.pallas_call(functools.partial(reply_kernel, n_cols=n_cols), out_shape=...  28.2 us
    ppermute x7, waiting for transfers between devices, local(): remote = [same, lax.ppermute(same, 'core', [(0, 1), (1, 0)])]  27.9 us
  transfers between devices with their start and end apart: 40, of which 36 were waited for; matrix products, arithmetic and copies ran while one was open for 1% of the time, Pallas kernels for 14%

profile of v3, /device:TPU:8, one launch (start us, length us, event | category | flops | bytes accessed | tf_op | source)
XLA Modules:
  0.0 477.0 jit_solution(8579447043919237889)
XLA Ops:
  0.0 3.3 prepare.1
  10.5 20.0 %all_to_all.48 = s32[32,1,128]{2,1,0:T(1,128)} all-to-all(s32[32,1,128]{2,1,0:T(1,128)S(1)} %broadcast_select_fusion), channel_id=1, replica_groups=mesh['zy'=32,'core'=2,'x'=4] {'zy'}, dimensions={0} | all-to-all | bytes 32768 | tf_op jit(solution)/shard_map/all_to_all | solution.py:38
  31.3 3.5 reply.12
  34.8 5.2 %all-to-all-start.5 = ((bf16[32,2,128,128]{3,2,1,0:T(8,128)(2,1)}), bf16[32,2,128,128]{3,2,1,0:T(8,128)(2,1)S(1)}, u32[]{:S(2)}, u32[]{:S(2)}) async-start(bf16[32,2,128,128]{3,2,1,0:T(8,128)(2,1)} %bitcast.27), calls=%async_computation.5 | async-start | bytes 4194304 | tf_op jit(solution)/shard_map/all_to_all | solution.py:230
  44.0 5.7 %collective-permute-done.refs_1_ = bf16[6,128,128]{2,1,0:T(8,128)(2,1)S(1)} collective-permute-done((bf16[6,128,128]{2,1,0:T(8,128)(2,1)S(1)}, bf16[6,128,128]{2,1,0:T(8,128)(2,1)S(1)}, u32[]{:S(2)}, u32[]{:S(2)}) %collective-permute-start) | collective-permute-done | bytes 196640 | tf_op jit(solution)/shard_map/ppermute | solution.py:222
  54.0 3.5 reply.8
  57.6 32.5 %all-to-all-done.5.refs_4_ = bf16[32,2,128,128]{3,2,1,0:T(8,128)(2,1)S(1)} async-done(((bf16[32,2,128,128]{3,2,1,0:T(8,128)(2,1)}), bf16[32,2,128,128]{3,2,1,0:T(8,128)(2,1)S(1)}, u32[]{:S(2)}, u32[]{:S(2)}) %all-to-all-start.5) | async-done | bytes 2097184 | tf_op jit(solution)/shard_map/all_to_all | solution.py:230
  91.4 5.8 %all-to-all-start.1 = ((bf16[32,2,128,128]{3,2,1,0:T(8,128)(2,1)}), bf16[32,2,128,128]{3,2,1,0:T(8,128)(2,1)}, u32[]{:S(2)}, u32[]{:S(2)}) async-start(bf16[32,2,128,128]{3,2,1,0:T(8,128)(2,1)} %bitcast.21), calls=%async_computation.1 | async-start | bytes 4194304 | tf_op jit(solution)/shard_map/all_to_all | solution.py:230
  102.7 6.0 %spread.11 = bf16[768,128]{1,0:T(8,128)(2,1)} custom-call(s32[72]{0:T(128)} %reshape.185.index_ref, s32[1]{0:T(128)} %bitcast.core_ref, bf16[6,12,128,128]{3,2,1,0:T(8,128)(2,1)} %tiles_ref.15, f32[768,128]{1,0:T(8,128)} %broadcast_in_dim.55.weight_ref, f32[768,128]{1,0:T(8,128)} %get-tuple-element.13.anchor_ref, bf16[6,128,128]{2,1,0:T(8,128)(2,1)} %bitcast.75, ...), custom_call_target="tpu_custom_call" | custom-call | flops 301989888 | bytes 5242880 | tf_op jit(solution)/shard_map/spread/pallas_call | solution.py:171
  112.7 7.5 %collective-permute-done.20.refs_1_ = bf16[6,128,128]{2,1,0:T(8,128)(2,1)S(1)} collective-permute-done((bf16[6,128,128]{2,1,0:T(8,128)(2,1)}, bf16[6,128,128]{2,1,0:T(8,128)(2,1)S(1)}, u32[]{:S(2)}, u32[]{:S(2)}) %collective-permute-start.20) | collective-permute-done | bytes 196640 | tf_op jit(solution)/shard_map/ppermute | solution.py:222
  124.4 3.5 reply.13
  128.0 18.3 %all-to-all-done.1.refs_4_ = bf16[32,2,128,128]{3,2,1,0:T(8,128)(2,1)} async-done(((bf16[32,2,128,128]{3,2,1,0:T(8,128)(2,1)}), bf16[32,2,128,128]{3,2,1,0:T(8,128)(2,1)}, u32[]{:S(2)}, u32[]{:S(2)}) %all-to-all-start.1) | async-done | bytes 2097184 | tf_op jit(solution)/shard_map/all_to_all | solution.py:230
  146.2 5.6 %all-to-all-start.6 = ((bf16[32,2,128,128]{3,2,1,0:T(8,128)(2,1)}), bf16[32,2,128,128]{3,2,1,0:T(8,128)(2,1)S(1)}, u32[]{:S(2)}, u32[]{:S(2)}) async-start(bf16[32,2,128,128]{3,2,1,0:T(8,128)(2,1)} %bitcast.22), calls=%async_computation.6 | async-start | bytes 4194304 | tf_op jit(solution)/shard_map/all_to_all | solution.py:230
  151.9 4.5 collective-permute-done.4.refs_5_
  156.4 6.0 %spread.8 = bf16[768,128]{1,0:T(8,128)(2,1)} custom-call(s32[72]{0:T(128)} %reshape.185.index_ref, s32[1]{0:T(128)} %bitcast.core_ref, bf16[6,12,128,128]{3,2,1,0:T(8,128)(2,1)} %tiles_ref.15, f32[768,128]{1,0:T(8,128)} %broadcast_in_dim.55.weight_ref, f32[768,128]{1,0:T(8,128)} %get-tuple-element.14.anchor_ref, bf16[6,128,128]{2,1,0:T(8,128)(2,1)} %bitcast.67, ...), custom_call_target="tpu_custom_call" | custom-call | flops 301989888 | bytes 5242880 | tf_op jit(solution)/shard_map/spread/pallas_call | solution.py:171
  166.6 7.5 %collective-permute-done.5.refs_1_ = bf16[6,128,128]{2,1,0:T(8,128)(2,1)S(1)} collective-permute-done((bf16[6,128,128]{2,1,0:T(8,128)(2,1)}, bf16[6,128,128]{2,1,0:T(8,128)(2,1)S(1)}, u32[]{:S(2)}, u32[]{:S(2)}) %collective-permute-start.5) | collective-permute-done | bytes 196640 | tf_op jit(solution)/shard_map/ppermute | solution.py:222
  178.3 3.5 reply.9
  181.9 17.3 %all-to-all-done.6.refs_4_ = bf16[32,2,128,128]{3,2,1,0:T(8,128)(2,1)S(1)} async-done(((bf16[32,2,128,128]{3,2,1,0:T(8,128)(2,1)}), bf16[32,2,128,128]{3,2,1,0:T(8,128)(2,1)S(1)}, u32[]{:S(2)}, u32[]{:S(2)}) %all-to-all-start.6) | async-done | bytes 2097184 | tf_op jit(solution)/shard_map/all_to_all | solution.py:230
  199.2 6.3 %all-to-all-start.2 = ((bf16[32,2,128,128]{3,2,1,0:T(8,128)(2,1)}), bf16[32,2,128,128]{3,2,1,0:T(8,128)(2,1)}, u32[]{:S(2)}, u32[]{:S(2)}) async-start(bf16[32,2,128,128]{3,2,1,0:T(8,128)(2,1)} %bitcast.24), calls=%async_computation.2 | async-start | bytes 4194304 | tf_op jit(solution)/shard_map/all_to_all | solution.py:230
  205.6 4.3 collective-permute-done.23.refs_5_
  209.9 6.0 %spread.12 = bf16[768,128]{1,0:T(8,128)(2,1)} custom-call(s32[72]{0:T(128)} %reshape.185.index_ref, s32[1]{0:T(128)} %bitcast.core_ref, bf16[6,12,128,128]{3,2,1,0:T(8,128)(2,1)} %tiles_ref.15, f32[768,128]{1,0:T(8,128)} %broadcast_in_dim.55.weight_ref, f32[768,128]{1,0:T(8,128)} %get-tuple-element.13.anchor_ref, bf16[6,128,128]{2,1,0:T(8,128)(2,1)} %bitcast.37, ...), custom_call_target="tpu_custom_call" | custom-call | flops 301989888 | bytes 5242880 | tf_op jit(solution)/shard_map/spread/pallas_call | solution.py:171
  219.9 7.5 %collective-permute-done.24.refs_1_ = bf16[6,128,128]{2,1,0:T(8,128)(2,1)S(1)} collective-permute-done((bf16[6,128,128]{2,1,0:T(8,128)(2,1)}, bf16[6,128,128]{2,1,0:T(8,128)(2,1)S(1)}, u32[]{:S(2)}, u32[]{:S(2)}) %collective-permute-start.24) | collective-permute-done | bytes 196640 | tf_op jit(solution)/shard_map/ppermute | solution.py:222
  231.7 3.5 reply.14
  235.2 17.5 %all-to-all-done.2.refs_4_ = bf16[32,2,128,128]{3,2,1,0:T(8,128)(2,1)} async-done(((bf16[32,2,128,128]{3,2,1,0:T(8,128)(2,1)}), bf16[32,2,128,128]{3,2,1,0:T(8,128)(2,1)}, u32[]{:S(2)}, u32[]{:S(2)}) %all-to-all-start.2) | async-done | bytes 2097184 | tf_op jit(solution)/shard_map/all_to_all | solution.py:230
  252.7 6.3 %all-to-all-start.7 = ((bf16[32,2,128,128]{3,2,1,0:T(8,128)(2,1)}), bf16[32,2,128,128]{3,2,1,0:T(8,128)(2,1)S(1)}, u32[]{:S(2)}, u32[]{:S(2)}) async-start(bf16[32,2,128,128]{3,2,1,0:T(8,128)(2,1)} %bitcast.25), calls=%async_computation.7 | async-start | bytes 4194304 | tf_op jit(solution)/shard_map/all_to_all | solution.py:230
  259.1 4.5 collective-permute-done.8.refs_5_
  263.6 6.0 %spread.9 = bf16[768,128]{1,0:T(8,128)(2,1)} custom-call(s32[72]{0:T(128)} %reshape.185.index_ref, s32[1]{0:T(128)} %bitcast.core_ref, bf16[6,12,128,128]{3,2,1,0:T(8,128)(2,1)} %tiles_ref.15, f32[768,128]{1,0:T(8,128)} %broadcast_in_dim.55.weight_ref, f32[768,128]{1,0:T(8,128)} %get-tuple-element.14.anchor_ref, bf16[6,128,128]{2,1,0:T(8,128)(2,1)} %bitcast.42, ...), custom_call_target="tpu_custom_call" | custom-call | flops 301989888 | bytes 5242880 | tf_op jit(solution)/shard_map/spread/pallas_call | solution.py:171
  274.8 4.4 collective-permute-done.10.refs_2_
  279.2 3.3 collective-permute-done.11.refs_3_
  283.9 3.5 reply.10
  287.5 18.7 %all-to-all-done.7.refs_4_ = bf16[32,2,128,128]{3,2,1,0:T(8,128)(2,1)S(1)} async-done(((bf16[32,2,128,128]{3,2,1,0:T(8,128)(2,1)}), bf16[32,2,128,128]{3,2,1,0:T(8,128)(2,1)S(1)}, u32[]{:S(2)}, u32[]{:S(2)}) %all-to-all-start.7) | async-done | bytes 2097184 | tf_op jit(solution)/shard_map/all_to_all | solution.py:230
  306.2 6.3 %all-to-all-start.3 = ((bf16[32,2,128,128]{3,2,1,0:T(8,128)(2,1)}), bf16[32,2,128,128]{3,2,1,0:T(8,128)(2,1)}, u32[]{:S(2)}, u32[]{:S(2)}) async-start(bf16[32,2,128,128]{3,2,1,0:T(8,128)(2,1)} %bitcast.26), calls=%async_computation.3 | async-start | bytes 4194304 | tf_op jit(solution)/shard_map/all_to_all | solution.py:230
  312.6 4.3 collective-permute-done.27.refs_5_
  316.9 6.0 %spread.13 = bf16[768,128]{1,0:T(8,128)(2,1)} custom-call(s32[72]{0:T(128)} %reshape.185.index_ref, s32[1]{0:T(128)} %bitcast.core_ref, bf16[6,12,128,128]{3,2,1,0:T(8,128)(2,1)} %tiles_ref.15, f32[768,128]{1,0:T(8,128)} %broadcast_in_dim.55.weight_ref, f32[768,128]{1,0:T(8,128)} %get-tuple-element.13.anchor_ref, bf16[6,128,128]{2,1,0:T(8,128)(2,1)} %bitcast.47, ...), custom_call_target="tpu_custom_call" | custom-call | flops 301989888 | bytes 5242880 | tf_op jit(solution)/shard_map/spread/pallas_call | solution.py:171
  326.9 7.5 %collective-permute-done.28.refs_1_ = bf16[6,128,128]{2,1,0:T(8,128)(2,1)S(1)} collective-permute-done((bf16[6,128,128]{2,1,0:T(8,128)(2,1)}, bf16[6,128,128]{2,1,0:T(8,128)(2,1)S(1)}, u32[]{:S(2)}, u32[]{:S(2)}) %collective-permute-start.28) | collective-permute-done | bytes 196640 | tf_op jit(solution)/shard_map/ppermute | solution.py:222
  338.6 3.5 reply.15
  342.2 17.5 %all-to-all-done.3.refs_4_ = bf16[32,2,128,128]{3,2,1,0:T(8,128)(2,1)} async-done(((bf16[32,2,128,128]{3,2,1,0:T(8,128)(2,1)}), bf16[32,2,128,128]{3,2,1,0:T(8,128)(2,1)}, u32[]{:S(2)}, u32[]{:S(2)}) %all-to-all-start.3) | async-done | bytes 2097184 | tf_op jit(solution)/shard_map/all_to_all | solution.py:230
  359.7 6.3 %all-to-all-start.8 = ((bf16[32,2,128,128]{3,2,1,0:T(8,128)(2,1)}), bf16[32,2,128,128]{3,2,1,0:T(8,128)(2,1)S(1)}, u32[]{:S(2)}, u32[]{:S(2)}) async-start(bf16[32,2,128,128]{3,2,1,0:T(8,128)(2,1)} %bitcast.23), calls=%async_computation.8 | async-start | bytes 4194304 | tf_op jit(solution)/shard_map/all_to_all | solution.py:230
  366.3 4.5 collective-permute-done.12.refs_5_
  370.8 6.0 %spread.10 = bf16[768,128]{1,0:T(8,128)(2,1)} custom-call(s32[72]{0:T(128)} %reshape.185.index_ref, s32[1]{0:T(128)} %bitcast.core_ref, bf16[6,12,128,128]{3,2,1,0:T(8,128)(2,1)} %tiles_ref.15, f32[768,128]{1,0:T(8,128)} %broadcast_in_dim.55.weight_ref, f32[768,128]{1,0:T(8,128)} %get-tuple-element.14.anchor_ref, bf16[6,128,128]{2,1,0:T(8,128)(2,1)} %bitcast.52, ...), custom_call_target="tpu_custom_call" | custom-call | flops 301989888 | bytes 5242880 | tf_op jit(solution)/shard_map/spread/pallas_call | solution.py:171
  380.7 7.5 %collective-permute-done.13.refs_1_ = bf16[6,128,128]{2,1,0:T(8,128)(2,1)S(1)} collective-permute-done((bf16[6,128,128]{2,1,0:T(8,128)(2,1)}, bf16[6,128,128]{2,1,0:T(8,128)(2,1)S(1)}, u32[]{:S(2)}, u32[]{:S(2)}) %collective-permute-start.13) | collective-permute-done | bytes 196640 | tf_op jit(solution)/shard_map/ppermute | solution.py:222
  392.5 3.5 reply.11
  396.0 17.1 %all-to-all-done.8.refs_4_ = bf16[32,2,128,128]{3,2,1,0:T(8,128)(2,1)S(1)} async-done(((bf16[32,2,128,128]{3,2,1,0:T(8,128)(2,1)}), bf16[32,2,128,128]{3,2,1,0:T(8,128)(2,1)S(1)}, u32[]{:S(2)}, u32[]{:S(2)}) %all-to-all-start.8) | async-done | bytes 2097184 | tf_op jit(solution)/shard_map/all_to_all | solution.py:230
  413.1 6.8 %all-to-all-start.4 = ((bf16[64,128,128]{2,1,0:T(8,128)(2,1)}), bf16[64,128,128]{2,1,0:T(8,128)(2,1)}, u32[]{:S(2)}, u32[]{:S(2)}) async-start(bf16[64,128,128]{2,1,0:T(8,128)(2,1)} %reply.11), calls=%async_computation.4 | async-start | bytes 4194304 | tf_op jit(solution)/shard_map/all_to_all | solution.py:227
  420.9 3.5 collective-permute-done.31.refs_5_
  424.4 6.1 %spread.14.refs_5_ = f32[768,128]{1,0:T(8,128)} custom-call(s32[72]{0:T(128)} %reshape.185.index_ref, s32[1]{0:T(128)} %bitcast.core_ref, bf16[6,12,128,128]{3,2,1,0:T(8,128)(2,1)} %tiles_ref.15, f32[768,128]{1,0:T(8,128)} %broadcast_in_dim.55.weight_ref, f32[768,128]{1,0:T(8,128)} %get-tuple-element.13.anchor_ref, bf16[6,128,128]{2,1,0:T(8,128)(2,1)} %bitcast.32, ...), custom_call_target="tpu_custom_call" | custom-call | flops 301989888 | bytes 5242880 | tf_op jit(solution)/shard_map/spread/pallas_call | solution.py:171
  430.5 40.6 %all-to-all-done.4.refs_4_ = bf16[64,128,128]{2,1,0:T(8,128)(2,1)} async-done(((bf16[64,128,128]{2,1,0:T(8,128)(2,1)}), bf16[64,128,128]{2,1,0:T(8,128)(2,1)}, u32[]{:S(2)}, u32[]{:S(2)}) %all-to-all-start.4) | async-done | bytes 2097184 | tf_op jit(solution)/shard_map/all_to_all | solution.py:227
  471.1 5.7 %spread.15 = f32[768,256]{1,0:T(8,128)} custom-call(s32[72]{0:T(128)} %reshape.183.index_ref, s32[1]{0:T(128)} %bitcast.core_ref, bf16[6,12,128,128]{3,2,1,0:T(8,128)(2,1)} %tiles_ref.15, f32[768,128]{1,0:T(8,128)} %broadcast_in_dim.55.weight_ref, f32[768,128]{1,0:T(8,128)} %get-tuple-element.14.anchor_ref, bf16[6,128,128]{2,1,0:T(8,128)(2,1)} %bitcast.57, ...), custom_call_target="tpu_custom_call" | custom-call | flops 301989888 | bytes 5242880 | tf_op jit(solution)/shard_map/spread/pallas_call | solution.py:171
  (131 shorter events, 72.4 us)
Async XLA Ops:
  3.3 27.2 %collective-permute-start.16 = (bf16[6,128,128]{2,1,0:T(8,128)(2,1)}, bf16[6,128,128]{2,1,0:T(8,128)(2,1)S(1)}, u32[]{:S(2)}, u32[]{:S(2)}) collective-permute-start(bf16[6,128,128]{2,1,0:T(8,128)(2,1)} %bitcast.71), channel_id=1, source_target_pairs={{1,0},{2,1},{3,2},{0,3},{5,4},{6,5},{7,6},{4,7},{9,8},{10,9},{11,1... | collective-permute-start | bytes 589832 | tf_op jit(solution)/shard_map/ppermute | solution.py:222
  6.1 24.4 %collective-permute-start.17 = (bf16[6,128,128]{2,1,0:T(8,128)(2,1)}, bf16[6,128,128]{2,1,0:T(8,128)(2,1)S(1)}, u32[]{:S(2)}, u32[]{:S(2)}) collective-permute-start(bf16[6,128,128]{2,1,0:T(8,128)(2,1)} %bitcast.72), channel_id=1, source_target_pairs={{2,0},{3,1},{0,2},{1,3},{6,4},{7,5},{4,6},{5,7},{10,8},{11,9},{8,1... | collective-permute-start | bytes 589832 | tf_op jit(solution)/shard_map/ppermute | solution.py:222
  6.9 23.6 %collective-permute-start.18 = (bf16[6,128,128]{2,1,0:T(8,128)(2,1)}, bf16[6,128,128]{2,1,0:T(8,128)(2,1)S(1)}, u32[]{:S(2)}, u32[]{:S(2)}) collective-permute-start(bf16[6,128,128]{2,1,0:T(8,128)(2,1)} %bitcast.73), channel_id=1, source_target_pairs={{3,0},{0,1},{1,2},{2,3},{7,4},{4,5},{5,6},{6,7},{11,8},{8,9},{9,10... | collective-permute-start | bytes 589832 | tf_op jit(solution)/shard_map/ppermute | solution.py:222
  8.9 1.3 collective-permute-start.3
  34.8 5.3 %copy-start.6 = (bf16[768,128]{1,0:T(8,128)(2,1)S(1)}, bf16[768,128]{1,0:T(8,128)(2,1)}, u32[]{:S(2)}) copy-start(bf16[768,128]{1,0:T(8,128)(2,1)} %get-tuple-element.9) | copy-start | bytes 589828
  34.8 55.2 %all-to-all-start.5 = ((bf16[32,2,128,128]{3,2,1,0:T(8,128)(2,1)}), bf16[32,2,128,128]{3,2,1,0:T(8,128)(2,1)S(1)}, u32[]{:S(2)}, u32[]{:S(2)}) async-start(bf16[32,2,128,128]{3,2,1,0:T(8,128)(2,1)} %bitcast.27), calls=%async_computation.5 | async-start | bytes 4194304 | tf_op jit(solution)/shard_map/all_to_all | solution.py:230
  40.1 9.6 %collective-permute-start = (bf16[6,128,128]{2,1,0:T(8,128)(2,1)S(1)}, bf16[6,128,128]{2,1,0:T(8,128)(2,1)S(1)}, u32[]{:S(2)}, u32[]{:S(2)}) collective-permute-start(bf16[6,128,128]{2,1,0:T(8,128)(2,1)S(1)} %bitcast.68), channel_id=1, source_target_pairs={{1,0},{2,1},{3,2},{0,3},{5,4},{6,5},{7,6},{4,7},{9,8},{10,9},{11,1... | collective-permute-start | bytes 589832 | tf_op jit(solution)/shard_map/ppermute | solution.py:222
  42.5 8.7 %collective-permute-start.1 = (bf16[6,128,128]{2,1,0:T(8,128)(2,1)S(1)}, bf16[6,128,128]{2,1,0:T(8,128)(2,1)S(1)}, u32[]{:S(2)}, u32[]{:S(2)}) collective-permute-start(bf16[6,128,128]{2,1,0:T(8,128)(2,1)S(1)} %bitcast.69), channel_id=1, source_target_pairs={{2,0},{3,1},{0,2},{1,3},{6,4},{7,5},{4,6},{5,7},{10,8},{11,9},{8,1... | collective-permute-start | bytes 589832 | tf_op jit(solution)/shard_map/ppermute | solution.py:222
  44.0 9.3 %collective-permute-start.2 = (bf16[6,128,128]{2,1,0:T(8,128)(2,1)S(1)}, bf16[6,128,128]{2,1,0:T(8,128)(2,1)S(1)}, u32[]{:S(2)}, u32[]{:S(2)}) collective-permute-start(bf16[6,128,128]{2,1,0:T(8,128)(2,1)S(1)} %bitcast.70), channel_id=1, source_target_pairs={{3,0},{0,1},{1,2},{2,3},{7,4},{4,5},{5,6},{6,7},{11,8},{8,9},{9,10... | collective-permute-start | bytes 589832 | tf_op jit(solution)/shard_map/ppermute | solution.py:222
  49.7 3.7 copy-start.10
  91.4 6.4 %copy-start = (bf16[6,12,128,128]{3,2,1,0:T(8,128)(2,1)S(1)}, bf16[6,12,128,128]{3,2,1,0:T(8,128)(2,1)}, u32[]{:S(2)}) copy-start(bf16[6,12,128,128]{3,2,1,0:T(8,128)(2,1)} %tiles_ref.15) | copy-start | bytes 7077892
  91.4 54.8 %all-to-all-start.1 = ((bf16[32,2,128,128]{3,2,1,0:T(8,128)(2,1)}), bf16[32,2,128,128]{3,2,1,0:T(8,128)(2,1)}, u32[]{:S(2)}, u32[]{:S(2)}) async-start(bf16[32,2,128,128]{3,2,1,0:T(8,128)(2,1)} %bitcast.21), calls=%async_computation.1 | async-start | bytes 4194304 | tf_op jit(solution)/shard_map/all_to_all | solution.py:230
  97.2 4.6 collective-permute-start.19
  108.7 11.5 %collective-permute-start.20 = (bf16[6,128,128]{2,1,0:T(8,128)(2,1)}, bf16[6,128,128]{2,1,0:T(8,128)(2,1)S(1)}, u32[]{:S(2)}, u32[]{:S(2)}) collective-permute-start(bf16[6,128,128]{2,1,0:T(8,128)(2,1)} %bitcast.33), channel_id=1, source_target_pairs={{1,0},{2,1},{3,2},{0,3},{5,4},{6,5},{7,6},{4,7},{9,8},{10,9},{11,1... | collective-permute-start | bytes 589832 | tf_op jit(solution)/shard_map/ppermute | solution.py:222
  111.1 9.5 %collective-permute-start.21 = (bf16[6,128,128]{2,1,0:T(8,128)(2,1)}, bf16[6,128,128]{2,1,0:T(8,128)(2,1)S(1)}, u32[]{:S(2)}, u32[]{:S(2)}) collective-permute-start(bf16[6,128,128]{2,1,0:T(8,128)(2,1)} %bitcast.34), channel_id=1, source_target_pairs={{2,0},{3,1},{0,2},{1,3},{6,4},{7,5},{4,6},{5,7},{10,8},{11,9},{8,1... | collective-permute-start | bytes 589832 | tf_op jit(solution)/shard_map/ppermute | solution.py:222
  112.7 11.1 %collective-permute-start.22 = (bf16[6,128,128]{2,1,0:T(8,128)(2,1)}, bf16[6,128,128]{2,1,0:T(8,128)(2,1)S(1)}, u32[]{:S(2)}, u32[]{:S(2)}) collective-permute-start(bf16[6,128,128]{2,1,0:T(8,128)(2,1)} %bitcast.35), channel_id=1, source_target_pairs={{3,0},{0,1},{1,2},{2,3},{7,4},{4,5},{5,6},{6,7},{11,8},{8,9},{9,10... | collective-permute-start | bytes 589832 | tf_op jit(solution)/shard_map/ppermute | solution.py:222
  120.2 3.6 copy-start.16
  146.2 53.0 %all-to-all-start.6 = ((bf16[32,2,128,128]{3,2,1,0:T(8,128)(2,1)}), bf16[32,2,128,128]{3,2,1,0:T(8,128)(2,1)S(1)}, u32[]{:S(2)}, u32[]{:S(2)}) async-start(bf16[32,2,128,128]{3,2,1,0:T(8,128)(2,1)} %bitcast.22), calls=%async_computation.6 | async-start | bytes 4194304 | tf_op jit(solution)/shard_map/all_to_all | solution.py:230
  151.8 4.6 collective-permute-start.4
  162.4 11.6 %collective-permute-start.5 = (bf16[6,128,128]{2,1,0:T(8,128)(2,1)}, bf16[6,128,128]{2,1,0:T(8,128)(2,1)S(1)}, u32[]{:S(2)}, u32[]{:S(2)}) collective-permute-start(bf16[6,128,128]{2,1,0:T(8,128)(2,1)} %bitcast.38), channel_id=1, source_target_pairs={{1,0},{2,1},{3,2},{0,3},{5,4},{6,5},{7,6},{4,7},{9,8},{10,9},{11,1... | collective-permute-start | bytes 589832 | tf_op jit(solution)/shard_map/ppermute | solution.py:222
  165.0 9.5 %collective-permute-start.6 = (bf16[6,128,128]{2,1,0:T(8,128)(2,1)}, bf16[6,128,128]{2,1,0:T(8,128)(2,1)S(1)}, u32[]{:S(2)}, u32[]{:S(2)}) collective-permute-start(bf16[6,128,128]{2,1,0:T(8,128)(2,1)} %bitcast.39), channel_id=1, source_target_pairs={{2,0},{3,1},{0,2},{1,3},{6,4},{7,5},{4,6},{5,7},{10,8},{11,9},{8,1... | collective-permute-start | bytes 589832 | tf_op jit(solution)/shard_map/ppermute | solution.py:222
  166.6 11.1 %collective-permute-start.7 = (bf16[6,128,128]{2,1,0:T(8,128)(2,1)}, bf16[6,128,128]{2,1,0:T(8,128)(2,1)S(1)}, u32[]{:S(2)}, u32[]{:S(2)}) collective-permute-start(bf16[6,128,128]{2,1,0:T(8,128)(2,1)} %bitcast.40), channel_id=1, source_target_pairs={{3,0},{0,1},{1,2},{2,3},{7,4},{4,5},{5,6},{6,7},{11,8},{8,9},{9,10... | collective-permute-start | bytes 589832 | tf_op jit(solution)/shard_map/ppermute | solution.py:222
  199.2 6.3 %copy-start.3 = (bf16[32,2,128,128]{3,2,1,0:T(8,128)(2,1)}, bf16[32,2,128,128]{3,2,1,0:T(8,128)(2,1)S(1)}, u32[]{:S(2)}) copy-start(bf16[32,2,128,128]{3,2,1,0:T(8,128)(2,1)S(1)} %all-to-all-done.6.refs_4_) | copy-start | bytes 6291460
  199.2 53.5 %all-to-all-start.2 = ((bf16[32,2,128,128]{3,2,1,0:T(8,128)(2,1)}), bf16[32,2,128,128]{3,2,1,0:T(8,128)(2,1)}, u32[]{:S(2)}, u32[]{:S(2)}) async-start(bf16[32,2,128,128]{3,2,1,0:T(8,128)(2,1)} %bitcast.24), calls=%async_computation.2 | async-start | bytes 4194304 | tf_op jit(solution)/shard_map/all_to_all | solution.py:230
  205.5 4.4 collective-permute-start.23
  215.9 11.5 %collective-permute-start.24 = (bf16[6,128,128]{2,1,0:T(8,128)(2,1)}, bf16[6,128,128]{2,1,0:T(8,128)(2,1)S(1)}, u32[]{:S(2)}, u32[]{:S(2)}) collective-permute-start(bf16[6,128,128]{2,1,0:T(8,128)(2,1)} %bitcast.43), channel_id=1, source_target_pairs={{1,0},{2,1},{3,2},{0,3},{5,4},{6,5},{7,6},{4,7},{9,8},{10,9},{11,1... | collective-permute-start | bytes 589832 | tf_op jit(solution)/shard_map/ppermute | solution.py:222
  218.4 9.5 %collective-permute-start.25 = (bf16[6,128,128]{2,1,0:T(8,128)(2,1)}, bf16[6,128,128]{2,1,0:T(8,128)(2,1)S(1)}, u32[]{:S(2)}, u32[]{:S(2)}) collective-permute-start(bf16[6,128,128]{2,1,0:T(8,128)(2,1)} %bitcast.44), channel_id=1, source_target_pairs={{2,0},{3,1},{0,2},{1,3},{6,4},{7,5},{4,6},{5,7},{10,8},{11,9},{8,1... | collective-permute-start | bytes 589832 | tf_op jit(solution)/shard_map/ppermute | solution.py:222
  219.9 11.1 %collective-permute-start.26 = (bf16[6,128,128]{2,1,0:T(8,128)(2,1)}, bf16[6,128,128]{2,1,0:T(8,128)(2,1)S(1)}, u32[]{:S(2)}, u32[]{:S(2)}) collective-permute-start(bf16[6,128,128]{2,1,0:T(8,128)(2,1)} %bitcast.45), channel_id=1, source_target_pairs={{3,0},{0,1},{1,2},{2,3},{7,4},{4,5},{5,6},{6,7},{11,8},{8,9},{9,10... | collective-permute-start | bytes 589832 | tf_op jit(solution)/shard_map/ppermute | solution.py:222
  252.7 53.4 %all-to-all-start.7 = ((bf16[32,2,128,128]{3,2,1,0:T(8,128)(2,1)}), bf16[32,2,128,128]{3,2,1,0:T(8,128)(2,1)S(1)}, u32[]{:S(2)}, u32[]{:S(2)}) async-start(bf16[32,2,128,128]{3,2,1,0:T(8,128)(2,1)} %bitcast.25), calls=%async_computation.7 | async-start | bytes 4194304 | tf_op jit(solution)/shard_map/all_to_all | solution.py:230
  259.0 4.6 collective-permute-start.8
  269.6 9.6 %collective-permute-start.10 = (bf16[6,128,128]{2,1,0:T(8,128)(2,1)}, bf16[6,128,128]{2,1,0:T(8,128)(2,1)S(1)}, u32[]{:S(2)}, u32[]{:S(2)}) collective-permute-start(bf16[6,128,128]{2,1,0:T(8,128)(2,1)} %bitcast.48), channel_id=1, source_target_pairs={{2,0},{3,1},{0,2},{1,3},{6,4},{7,5},{4,6},{5,7},{10,8},{11,9},{8,1... | collective-permute-start | bytes 589832 | tf_op jit(solution)/shard_map/ppermute | solution.py:222
  271.5 11.0 %collective-permute-start.11 = (bf16[6,128,128]{2,1,0:T(8,128)(2,1)}, bf16[6,128,128]{2,1,0:T(8,128)(2,1)S(1)}, u32[]{:S(2)}, u32[]{:S(2)}) collective-permute-start(bf16[6,128,128]{2,1,0:T(8,128)(2,1)} %bitcast.49), channel_id=1, source_target_pairs={{3,0},{0,1},{1,2},{2,3},{7,4},{4,5},{5,6},{6,7},{11,8},{8,9},{9,10... | collective-permute-start | bytes 589832 | tf_op jit(solution)/shard_map/ppermute | solution.py:222
  272.9 9.7 %collective-permute-start.9 = (bf16[6,128,128]{2,1,0:T(8,128)(2,1)}, bf16[6,128,128]{2,1,0:T(8,128)(2,1)S(1)}, u32[]{:S(2)}, u32[]{:S(2)}) collective-permute-start(bf16[6,128,128]{2,1,0:T(8,128)(2,1)} %bitcast.50), channel_id=1, source_target_pairs={{1,0},{2,1},{3,2},{0,3},{5,4},{6,5},{7,6},{4,7},{9,8},{10,9},{11,1... | collective-permute-start | bytes 589832 | tf_op jit(solution)/shard_map/ppermute | solution.py:222
  306.1 6.3 %copy-start.4 = (bf16[32,2,128,128]{3,2,1,0:T(8,128)(2,1)}, bf16[32,2,128,128]{3,2,1,0:T(8,128)(2,1)S(1)}, u32[]{:S(2)}) copy-start(bf16[32,2,128,128]{3,2,1,0:T(8,128)(2,1)S(1)} %all-to-all-done.7.refs_4_) | copy-start | bytes 6291460
  306.2 53.5 %all-to-all-start.3 = ((bf16[32,2,128,128]{3,2,1,0:T(8,128)(2,1)}), bf16[32,2,128,128]{3,2,1,0:T(8,128)(2,1)}, u32[]{:S(2)}, u32[]{:S(2)}) async-start(bf16[32,2,128,128]{3,2,1,0:T(8,128)(2,1)} %bitcast.26), calls=%async_computation.3 | async-start | bytes 4194304 | tf_op jit(solution)/shard_map/all_to_all | solution.py:230
  312.5 4.4 collective-permute-start.27
  322.9 11.5 %collective-permute-start.28 = (bf16[6,128,128]{2,1,0:T(8,128)(2,1)}, bf16[6,128,128]{2,1,0:T(8,128)(2,1)S(1)}, u32[]{:S(2)}, u32[]{:S(2)}) collective-permute-start(bf16[6,128,128]{2,1,0:T(8,128)(2,1)} %bitcast.28), channel_id=1, source_target_pairs={{1,0},{2,1},{3,2},{0,3},{5,4},{6,5},{7,6},{4,7},{9,8},{10,9},{11,1... | collective-permute-start | bytes 589832 | tf_op jit(solution)/shard_map/ppermute | solution.py:222
  325.3 9.5 %collective-permute-start.29 = (bf16[6,128,128]{2,1,0:T(8,128)(2,1)}, bf16[6,128,128]{2,1,0:T(8,128)(2,1)S(1)}, u32[]{:S(2)}, u32[]{:S(2)}) collective-permute-start(bf16[6,128,128]{2,1,0:T(8,128)(2,1)} %bitcast.29), channel_id=1, source_target_pairs={{2,0},{3,1},{0,2},{1,3},{6,4},{7,5},{4,6},{5,7},{10,8},{11,9},{8,1... | collective-permute-start | bytes 589832 | tf_op jit(solution)/shard_map/ppermute | solution.py:222
  326.9 11.1 %collective-permute-start.30 = (bf16[6,128,128]{2,1,0:T(8,128)(2,1)}, bf16[6,128,128]{2,1,0:T(8,128)(2,1)S(1)}, u32[]{:S(2)}, u32[]{:S(2)}) collective-permute-start(bf16[6,128,128]{2,1,0:T(8,128)(2,1)} %bitcast.30), channel_id=1, source_target_pairs={{3,0},{0,1},{1,2},{2,3},{7,4},{4,5},{5,6},{6,7},{11,8},{8,9},{9,10... | collective-permute-start | bytes 589832 | tf_op jit(solution)/shard_map/ppermute | solution.py:222
  359.7 53.4 %all-to-all-start.8 = ((bf16[32,2,128,128]{3,2,1,0:T(8,128)(2,1)}), bf16[32,2,128,128]{3,2,1,0:T(8,128)(2,1)S(1)}, u32[]{:S(2)}, u32[]{:S(2)}) async-start(bf16[32,2,128,128]{3,2,1,0:T(8,128)(2,1)} %bitcast.23), calls=%async_computation.8 | async-start | bytes 4194304 | tf_op jit(solution)/shard_map/all_to_all | solution.py:230
  365.9 4.8 %collective-permute-start.12 = (bf16[32,2,128,128]{3,2,1,0:T(8,128)(2,1)}, bf16[32,2,128,128]{3,2,1,0:T(8,128)(2,1)}, u32[]{:S(2)}, u32[]{:S(2)}) collective-permute-start(bf16[32,2,128,128]{3,2,1,0:T(8,128)(2,1)} %all-to-all-done.3.refs_4_), channel_id=1, source_target_pairs={{0,4},{4,0},{1,5},{5,1},{2,6},{6,2},{3,7},{7,3},{8,12},{12,8},{9,1... | collective-permute-start | bytes 6291464 | tf_op jit(solution)/shard_map/ppermute | solution.py:231
  376.8 11.5 %collective-permute-start.13 = (bf16[6,128,128]{2,1,0:T(8,128)(2,1)}, bf16[6,128,128]{2,1,0:T(8,128)(2,1)S(1)}, u32[]{:S(2)}, u32[]{:S(2)}) collective-permute-start(bf16[6,128,128]{2,1,0:T(8,128)(2,1)} %bitcast.53), channel_id=1, source_target_pairs={{1,0},{2,1},{3,2},{0,3},{5,4},{6,5},{7,6},{4,7},{9,8},{10,9},{11,1... | collective-permute-start | bytes 589832 | tf_op jit(solution)/shard_map/ppermute | solution.py:222
  379.2 9.5 %collective-permute-start.14 = (bf16[6,128,128]{2,1,0:T(8,128)(2,1)}, bf16[6,128,128]{2,1,0:T(8,128)(2,1)S(1)}, u32[]{:S(2)}, u32[]{:S(2)}) collective-permute-start(bf16[6,128,128]{2,1,0:T(8,128)(2,1)} %bitcast.54), channel_id=1, source_target_pairs={{2,0},{3,1},{0,2},{1,3},{6,4},{7,5},{4,6},{5,7},{10,8},{11,9},{8,1... | collective-permute-start | bytes 589832 | tf_op jit(solution)/shard_map/ppermute | solution.py:222
  380.7 11.1 %collective-permute-start.15 = (bf16[6,128,128]{2,1,0:T(8,128)(2,1)}, bf16[6,128,128]{2,1,0:T(8,128)(2,1)S(1)}, u32[]{:S(2)}, u32[]{:S(2)}) collective-permute-start(bf16[6,128,128]{2,1,0:T(8,128)(2,1)} %bitcast.55), channel_id=1, source_target_pairs={{3,0},{0,1},{1,2},{2,3},{7,4},{4,5},{5,6},{6,7},{11,8},{8,9},{9,10... | collective-permute-start | bytes 589832 | tf_op jit(solution)/shard_map/ppermute | solution.py:222
  396.0 24.1 %copy-start.31 = (s32[6,12]{1,0:T(8,128)S(1)}, s32[6,12]{1,0:T(8,128)}, u32[]{:S(2)}) copy-start(s32[6,12]{1,0:T(8,128)} %param.6) | copy-start | bytes 868
  413.1 6.9 %copy-start.1 = (bf16[32,2,128,128]{3,2,1,0:T(8,128)(2,1)}, bf16[32,2,128,128]{3,2,1,0:T(8,128)(2,1)S(1)}, u32[]{:S(2)}) copy-start(bf16[32,2,128,128]{3,2,1,0:T(8,128)(2,1)S(1)} %all-to-all-done.8.refs_4_) | copy-start | bytes 6291460
  413.1 58.0 %all-to-all-start.4 = ((bf16[64,128,128]{2,1,0:T(8,128)(2,1)}), bf16[64,128,128]{2,1,0:T(8,128)(2,1)}, u32[]{:S(2)}, u32[]{:S(2)}) async-start(bf16[64,128,128]{2,1,0:T(8,128)(2,1)} %reply.11), calls=%async_computation.4 | async-start | bytes 4194304 | tf_op jit(solution)/shard_map/all_to_all | solution.py:227
  420.0 4.4 collective-permute-start.31
  (24 other events, 45.2 us)

commit v4 on v3

--- a/solution.py
+++ b/solution.py
@@ -9,6 +9,7 @@
 from jax.sharding import PartitionSpec as P
 
 HOPS = 4
+HOLD = {(0, 0): 2100, (1, 0): 700, (1, 1): 600, (2, 0): 700, (2, 1): 600, (3, 0): 700}
 PARTS = 2
 AXES = ("zy", "core", "x")
 GROUP = ("zy", "core")
@@ -120,6 +121,26 @@
         ),
         name="reply",
     )(asked, *parts)
+
+
+def hold_kernel(turns_ref, *refs):
+    spun = refs[-1]
+
+    @pl.loop(0, turns_ref[0])
+    def _(_):
+        spun[...] = spun[...] * 0.5 + 1.0
+
+
+def held(value, turns, after):
+    return pl.pallas_call(
+        hold_kernel,
+        out_shape=jax.ShapeDtypeStruct(value.shape, value.dtype),
+        in_specs=[SMEM, HBM] + [HBM] * len(after),
+        out_specs=HBM,
+        input_output_aliases={1: 0},
+        scratch_shapes=[pltpu.VMEM((8, LANES), jnp.float32)],
+        name="hold",
+    )(turns, value, *after)
 
 
 def spread_kernel(index_ref, core_ref, tiles_ref, weight_ref, anchor_ref, *refs, n_src, final):
@@ -214,6 +235,7 @@
 
     ranges = [slice(p * width, (p + 1) * width) for p in range(PARTS)]
     anchors = [(1.0 - ALPHA) * scale * anchor[:, r] for r in ranges]
+    before = []
     for hop in range(HOPS):
         last = hop == HOPS - 1
         for p in range(PARTS):
@@ -223,11 +245,14 @@
                 for d in range(1, n_cols)
             ]
             reply = reply_blocks(asked, pieces)
+            if (hop, p) in HOLD:
+                reply = held(reply, (own_core * HOLD[hop, p]).reshape(1), before)
             if last and p == PARTS - 1:
                 remote = [lax.all_to_all(reply, GROUP, 0, 0, tiled=True)]
             else:
                 reply = reply.reshape(n_chips, 2, block, width)
                 same = lax.all_to_all(reply, "zy", 0, 0, tiled=True)
+                before = [same]
                 remote = [same, lax.ppermute(same, "core", [(0, 1), (1, 0)])]
             blended[p] = spread_blocks(
                 index_last if len(remote) == 1 else index,

time: 480 us -> 461 us (0.960)
  waiting for transfers between devices: 281 us -> 179 us
  starting transfers between devices: 83.1 us -> 182 us
  blocking collectives: 20 us -> 0 us
    all_to_all x7, waiting for transfers between devices: 139 us -> 37 us  [local(): same = lax.all_to_all(reply, 'zy', 0, 0, tiled=True)]
    ppermute x7, starting transfers between devices: 0.99 us -> 70.1 us  [local(): remote = [same, lax.ppermute(same, 'core', [(0, 1), (1, 0)])]]
    all_to_all x1 -> x0, blocking collectives: 20 us -> none  [ask_blocks(): return lax.all_to_all(rows, 'zy', 0, 0, tiled=True)]
    all_to_all x0 -> x1, starting transfers between devices: none -> 11.7 us  [ask_blocks(): return lax.all_to_all(rows, 'zy', 0, 0, tiled=True)]
    all_to_all x1, starting transfers between devices: 6.85 us -> 16.8 us  [local(): remote = [lax.all_to_all(reply, GROUP, 0, 0, tiled=True)]]
    all_to_all x7, starting transfers between devices: 41.7 us -> 51 us  [local(): same = lax.all_to_all(reply, 'zy', 0, 0, tiled=True)]
    all_to_all x0 -> x1, waiting for transfers between devices: none -> 8.56 us  [ask_blocks(): return lax.all_to_all(rows, 'zy', 0, 0, tiled=True)]
    ppermute x24, waiting for transfers between devices: 72.4 us -> 66.3 us  [local(): lax.ppermute(own, 'x', [((x + d) % n_cols, x) for x in range(n_cols)])]
  transfers between devices with their start and end apart: 40 -> 41, of which waited for: 36 -> 29; matrix products, arithmetic and copies ran while one was open for 1% -> 1% of each run, Pallas kernels for 14% -> 15%
where the time goes in v4:
time: 461 us; the launch traced here: 459 us
  starting transfers between devices  182 us (39%)
  waiting for transfers between devices  179 us (39%)
  Pallas kernels  79.7 us (17%)
  local copies, waits for them, and re-layouts  13.8 us (3%)
    ppermute x7, starting transfers between devices, local(): remote = [same, lax.ppermute(same, 'core', [(0, 1), (1, 0)])]  70.1 us
    ppermute x24, waiting for transfers between devices, local(): lax.ppermute(own, 'x', [((x + d) % n_cols, x) for x in range(n_cols)])  66.3 us
    all_to_all x7, starting transfers between devices, local(): same = lax.all_to_all(reply, 'zy', 0, 0, tiled=True)  51 us
    pallas_call x8, Pallas kernels, spread_blocks(): pl.pallas_call(functools.partial(spread_kernel, n_src=n_src, final=final)...  48 us
    all_to_all x1, waiting for transfers between devices, local(): remote = [lax.all_to_all(reply, GROUP, 0, 0, tiled=True)]  40.6 us
    all_to_all x7, waiting for transfers between devices, local(): same = lax.all_to_all(reply, 'zy', 0, 0, tiled=True)  37 us
    ppermute x24, starting transfers between devices, local(): lax.ppermute(own, 'x', [((x + d) % n_cols, x) for x in range(n_cols)])  32.2 us
    pallas_call x8, Pallas kernels, reply_blocks(): pl.pallas_call(functools.partial(reply_kernel, n_cols=n_cols), out_shape=...  28.4 us
  transfers between devices with their start and end apart: 41, of which 29 were waited for; matrix products, arithmetic and copies ran while one was open for 1% of the time, Pallas kernels for 15%

profile of v4, /device:TPU:8, one launch (start us, length us, event | category | flops | bytes accessed | tf_op | source)
XLA Modules:
  0.0 458.7 jit_solution(13397290656232379165)
XLA Ops:
  12.3 11.7 %all-to-all-start = ((s32[32,1,128]{2,1,0:T(1,128)}), s32[32,1,128]{2,1,0:T(1,128)S(1)}, u32[]{:S(2)}, u32[]{:S(2)}) async-start(s32[32,1,128]{2,1,0:T(1,128)} %broadcast_select_fusion), calls=%async_computation | async-start | bytes 32768 | tf_op jit(solution)/shard_map/all_to_all | solution.py:39
  24.0 8.6 %all-to-all-done = s32[32,1,128]{2,1,0:T(1,128)S(1)} async-done(((s32[32,1,128]{2,1,0:T(1,128)}), s32[32,1,128]{2,1,0:T(1,128)S(1)}, u32[]{:S(2)}, u32[]{:S(2)}) %all-to-all-start) | async-done | bytes 16416 | tf_op jit(solution)/shard_map/all_to_all | solution.py:39
  36.9 5.2 %all-to-all-start.2 = ((bf16[32,2,128,128]{3,2,1,0:T(8,128)(2,1)}), bf16[32,2,128,128]{3,2,1,0:T(8,128)(2,1)S(1)}, u32[]{:S(2)}, u32[]{:S(2)}) async-start(bf16[32,2,128,128]{3,2,1,0:T(8,128)(2,1)} %bitcast.29), calls=%async_computation.2 | async-start | bytes 4194304 | tf_op jit(solution)/shard_map/all_to_all | solution.py:254
  45.6 5.6 %collective-permute-done.2.refs_3_ = bf16[6,128,128]{2,1,0:T(8,128)(2,1)S(1)} collective-permute-done((bf16[6,128,128]{2,1,0:T(8,128)(2,1)S(1)}, bf16[6,128,128]{2,1,0:T(8,128)(2,1)S(1)}, u32[]{:S(2)}, u32[]{:S(2)}) %collective-permute-start.2) | collective-permute-done | bytes 196640 | tf_op jit(solution)/shard_map/ppermute | solution.py:244
  52.8 3.5 reply.8
  56.4 25.7 %all-to-all-done.2.refs_4_ = bf16[32,2,128,128]{3,2,1,0:T(8,128)(2,1)S(1)} async-done(((bf16[32,2,128,128]{3,2,1,0:T(8,128)(2,1)}), bf16[32,2,128,128]{3,2,1,0:T(8,128)(2,1)S(1)}, u32[]{:S(2)}, u32[]{:S(2)}) %all-to-all-start.2) | async-done | bytes 2097184 | tf_op jit(solution)/shard_map/all_to_all | solution.py:254
  83.4 5.1 %all-to-all-start.1 = ((bf16[32,2,128,128]{3,2,1,0:T(8,128)(2,1)}), bf16[32,2,128,128]{3,2,1,0:T(8,128)(2,1)}, u32[]{:S(2)}, u32[]{:S(2)}) async-start(bf16[32,2,128,128]{3,2,1,0:T(8,128)(2,1)} %bitcast.30), calls=%async_computation.1 | async-start | bytes 4194304 | tf_op jit(solution)/shard_map/all_to_all | solution.py:254
  88.5 12.2 %collective-permute-start.11 = (bf16[32,2,128,128]{3,2,1,0:T(8,128)(2,1)}, bf16[32,2,128,128]{3,2,1,0:T(8,128)(2,1)}, u32[]{:S(2)}, u32[]{:S(2)}) collective-permute-start(bf16[32,2,128,128]{3,2,1,0:T(8,128)(2,1)} %copy-done.6), channel_id=1, source_target_pairs={{0,4},{4,0},{1,5},{5,1},{2,6},{6,2},{3,7},{7,3},{8,12},{12,8},{9,1... | collective-permute-start | bytes 6291464 | tf_op jit(solution)/shard_map/ppermute | solution.py:256
  105.7 6.0 %spread.9 = bf16[768,128]{1,0:T(8,128)(2,1)} custom-call(s32[72]{0:T(128)} %reshape.197.index_ref, s32[1]{0:T(128)} %bitcast.core_ref, bf16[6,12,128,128]{3,2,1,0:T(8,128)(2,1)} %tiles_ref.15, f32[768,128]{1,0:T(8,128)} %broadcast_in_dim.55.weight_ref, f32[768,128]{1,0:T(8,128)} %get-tuple-element.13.anchor_ref, bf16[6,128,128]{2,1,0:T(8,128)(2,1)} %bitcast.78, ...), custom_call_target="tpu_custom_call" | custom-call | flops 301989888 | bytes 5242880 | tf_op jit(solution)/shard_map/spread/pallas_call | solution.py:192
  115.2 9.5 %collective-permute-done.14.refs_3_ = bf16[6,128,128]{2,1,0:T(8,128)(2,1)S(1)} collective-permute-done((bf16[6,128,128]{2,1,0:T(8,128)(2,1)}, bf16[6,128,128]{2,1,0:T(8,128)(2,1)S(1)}, u32[]{:S(2)}, u32[]{:S(2)}) %collective-permute-start.14) | collective-permute-done | bytes 196640 | tf_op jit(solution)/shard_map/ppermute | solution.py:244
  130.0 9.4 %all-to-all-start.3 = ((bf16[32,2,128,128]{3,2,1,0:T(8,128)(2,1)}), bf16[32,2,128,128]{3,2,1,0:T(8,128)(2,1)S(1)}, u32[]{:S(2)}, u32[]{:S(2)}) async-start(bf16[32,2,128,128]{3,2,1,0:T(8,128)(2,1)} %bitcast.26), calls=%async_computation.3 | async-start | bytes 4194304 | tf_op jit(solution)/shard_map/all_to_all | solution.py:254
  139.4 11.0 %collective-permute-start.4 = (bf16[32,2,128,128]{3,2,1,0:T(8,128)(2,1)}, bf16[32,2,128,128]{3,2,1,0:T(8,128)(2,1)}, u32[]{:S(2)}, u32[]{:S(2)}) collective-permute-start(bf16[32,2,128,128]{3,2,1,0:T(8,128)(2,1)} %all-to-all-done.1.refs_4_.refs_1_), channel_id=1, source_target_pairs={{0,4},{4,0},{1,5},{5,1},{2,6},{6,2},{3,7},{7,3},{8,12},{12,8},{9,1... | collective-permute-start | bytes 6291464 | tf_op jit(solution)/shard_map/ppermute | solution.py:256
  150.4 4.1 collective-permute-done.4.refs_5_
  154.5 6.0 %spread.8 = bf16[768,128]{1,0:T(8,128)(2,1)} custom-call(s32[72]{0:T(128)} %reshape.197.index_ref, s32[1]{0:T(128)} %bitcast.core_ref, bf16[6,12,128,128]{3,2,1,0:T(8,128)(2,1)} %tiles_ref.15, f32[768,128]{1,0:T(8,128)} %broadcast_in_dim.55.weight_ref, f32[768,128]{1,0:T(8,128)} %get-tuple-element.14.anchor_ref, bf16[6,128,128]{2,1,0:T(8,128)(2,1)} %bitcast.70, ...), custom_call_target="tpu_custom_call" | custom-call | flops 301989888 | bytes 5242880 | tf_op jit(solution)/shard_map/spread/pallas_call | solution.py:192
  164.2 9.4 %collective-permute-done.7.refs_3_ = bf16[6,128,128]{2,1,0:T(8,128)(2,1)S(1)} collective-permute-done((bf16[6,128,128]{2,1,0:T(8,128)(2,1)}, bf16[6,128,128]{2,1,0:T(8,128)(2,1)S(1)}, u32[]{:S(2)}, u32[]{:S(2)}) %collective-permute-start.7) | collective-permute-done | bytes 196640 | tf_op jit(solution)/shard_map/ppermute | solution.py:244
  175.1 3.6 reply.9.refs_0_
  178.7 4.7 %all-to-all-done.3.refs_1_.refs_4_ = bf16[32,2,128,128]{3,2,1,0:T(8,128)(2,1)S(1)} async-done(((bf16[32,2,128,128]{3,2,1,0:T(8,128)(2,1)}), bf16[32,2,128,128]{3,2,1,0:T(8,128)(2,1)S(1)}, u32[]{:S(2)}, u32[]{:S(2)}) %all-to-all-start.3) | async-done | bytes 2097184 | tf_op jit(solution)/shard_map/all_to_all | solution.py:254
  184.7 5.3 %all-to-all-start.4 = ((bf16[32,2,128,128]{3,2,1,0:T(8,128)(2,1)}), bf16[32,2,128,128]{3,2,1,0:T(8,128)(2,1)}, u32[]{:S(2)}, u32[]{:S(2)}) async-start(bf16[32,2,128,128]{3,2,1,0:T(8,128)(2,1)} %bitcast.27), calls=%async_computation.4 | async-start | bytes 4194304 | tf_op jit(solution)/shard_map/all_to_all | solution.py:254
  190.0 12.6 %collective-permute-start.19 = (bf16[32,2,128,128]{3,2,1,0:T(8,128)(2,1)S(1)}, bf16[32,2,128,128]{3,2,1,0:T(8,128)(2,1)}, u32[]{:S(2)}, u32[]{:S(2)}) collective-permute-start(bf16[32,2,128,128]{3,2,1,0:T(8,128)(2,1)S(1)} %copy-done.2), channel_id=1, source_target_pairs={{0,4},{4,0},{1,5},{5,1},{2,6},{6,2},{3,7},{7,3},{8,12},{12,8},{9,1... | collective-permute-start | bytes 6291464 | tf_op jit(solution)/shard_map/ppermute | solution.py:256
  202.6 3.9 collective-permute-done.19.refs_5_
  206.5 6.0 %spread.11 = bf16[768,128]{1,0:T(8,128)(2,1)} custom-call(s32[72]{0:T(128)} %reshape.197.index_ref, s32[1]{0:T(128)} %bitcast.core_ref, bf16[6,12,128,128]{3,2,1,0:T(8,128)(2,1)} %tiles_ref.15, f32[768,128]{1,0:T(8,128)} %broadcast_in_dim.55.weight_ref, f32[768,128]{1,0:T(8,128)} %get-tuple-element.13.anchor_ref, bf16[6,128,128]{2,1,0:T(8,128)(2,1)} %bitcast.40, ...), custom_call_target="tpu_custom_call" | custom-call | flops 301989888 | bytes 5242880 | tf_op jit(solution)/shard_map/spread/pallas_call | solution.py:192
  212.9 3.6 collective-permute-start.21
  216.4 4.8 %collective-permute-done.22.refs_3_ = bf16[6,128,128]{2,1,0:T(8,128)(2,1)S(1)} collective-permute-done((bf16[6,128,128]{2,1,0:T(8,128)(2,1)}, bf16[6,128,128]{2,1,0:T(8,128)(2,1)S(1)}, u32[]{:S(2)}, u32[]{:S(2)}) %collective-permute-start.22) | collective-permute-done | bytes 196640 | tf_op jit(solution)/shard_map/ppermute | solution.py:244
  221.3 4.7 %collective-permute-done.21.refs_2_ = bf16[6,128,128]{2,1,0:T(8,128)(2,1)S(1)} collective-permute-done((bf16[6,128,128]{2,1,0:T(8,128)(2,1)}, bf16[6,128,128]{2,1,0:T(8,128)(2,1)S(1)}, u32[]{:S(2)}, u32[]{:S(2)}) %collective-permute-start.21) | collective-permute-done | bytes 196640 | tf_op jit(solution)/shard_map/ppermute | solution.py:244
  230.9 9.8 %all-to-all-start.5 = ((bf16[32,2,128,128]{3,2,1,0:T(8,128)(2,1)}), bf16[32,2,128,128]{3,2,1,0:T(8,128)(2,1)S(1)}, u32[]{:S(2)}, u32[]{:S(2)}) async-start(bf16[32,2,128,128]{3,2,1,0:T(8,128)(2,1)} %bitcast.28), calls=%async_computation.5 | async-start | bytes 4194304 | tf_op jit(solution)/shard_map/all_to_all | solution.py:254
  240.7 11.8 %collective-permute-start.15 = (bf16[32,2,128,128]{3,2,1,0:T(8,128)(2,1)}, bf16[32,2,128,128]{3,2,1,0:T(8,128)(2,1)}, u32[]{:S(2)}, u32[]{:S(2)}) collective-permute-start(bf16[32,2,128,128]{3,2,1,0:T(8,128)(2,1)} %all-to-all-done.4.refs_4_.refs_1_), channel_id=1, source_target_pairs={{0,4},{4,0},{1,5},{5,1},{2,6},{6,2},{3,7},{7,3},{8,12},{12,8},{9,1... | collective-permute-start | bytes 6291464 | tf_op jit(solution)/shard_map/ppermute | solution.py:256
  252.5 4.1 collective-permute-done.15.refs_5_
  256.6 6.0 %spread.10 = bf16[768,128]{1,0:T(8,128)(2,1)} custom-call(s32[72]{0:T(128)} %reshape.197.index_ref, s32[1]{0:T(128)} %bitcast.core_ref, bf16[6,12,128,128]{3,2,1,0:T(8,128)(2,1)} %tiles_ref.15, f32[768,128]{1,0:T(8,128)} %broadcast_in_dim.55.weight_ref, f32[768,128]{1,0:T(8,128)} %get-tuple-element.14.anchor_ref, bf16[6,128,128]{2,1,0:T(8,128)(2,1)} %bitcast.45, ...), custom_call_target="tpu_custom_call" | custom-call | flops 301989888 | bytes 5242880 | tf_op jit(solution)/shard_map/spread/pallas_call | solution.py:192
  262.9 5.3 %collective-permute-start.17 = (bf16[6,128,128]{2,1,0:T(8,128)(2,1)}, bf16[6,128,128]{2,1,0:T(8,128)(2,1)S(1)}, u32[]{:S(2)}, u32[]{:S(2)}) collective-permute-start(bf16[6,128,128]{2,1,0:T(8,128)(2,1)} %bitcast.47), channel_id=1, source_target_pairs={{2,0},{3,1},{0,2},{1,3},{6,4},{7,5},{4,6},{5,7},{10,8},{11,9},{8,1... | collective-permute-start | bytes 589832 | tf_op jit(solution)/shard_map/ppermute | solution.py:244
  268.2 4.2 collective-permute-done.18.refs_3_
  272.4 5.4 %collective-permute-done.17.refs_2_ = bf16[6,128,128]{2,1,0:T(8,128)(2,1)S(1)} collective-permute-done((bf16[6,128,128]{2,1,0:T(8,128)(2,1)}, bf16[6,128,128]{2,1,0:T(8,128)(2,1)S(1)}, u32[]{:S(2)}, u32[]{:S(2)}) %collective-permute-start.17) | collective-permute-done | bytes 196640 | tf_op jit(solution)/shard_map/ppermute | solution.py:244
  279.1 3.6 reply.12.refs_0_
  284.1 10.0 %all-to-all-start.6 = ((bf16[32,2,128,128]{3,2,1,0:T(8,128)(2,1)}), bf16[32,2,128,128]{3,2,1,0:T(8,128)(2,1)}, u32[]{:S(2)}, u32[]{:S(2)}) async-start(bf16[32,2,128,128]{3,2,1,0:T(8,128)(2,1)} %bitcast.24), calls=%async_computation.6 | async-start | bytes 4194304 | tf_op jit(solution)/shard_map/all_to_all | solution.py:254
  294.1 9.8 %collective-permute-start.27 = (bf16[32,2,128,128]{3,2,1,0:T(8,128)(2,1)S(1)}, bf16[32,2,128,128]{3,2,1,0:T(8,128)(2,1)}, u32[]{:S(2)}, u32[]{:S(2)}) collective-permute-start(bf16[32,2,128,128]{3,2,1,0:T(8,128)(2,1)S(1)} %copy-done.4), channel_id=1, source_target_pairs={{0,4},{4,0},{1,5},{5,1},{2,6},{6,2},{3,7},{7,3},{8,12},{12,8},{9,1... | collective-permute-start | bytes 6291464 | tf_op jit(solution)/shard_map/ppermute | solution.py:256
  303.9 3.9 collective-permute-done.27.refs_5_
  307.8 6.0 %spread.13 = bf16[768,128]{1,0:T(8,128)(2,1)} custom-call(s32[72]{0:T(128)} %reshape.197.index_ref, s32[1]{0:T(128)} %bitcast.core_ref, bf16[6,12,128,128]{3,2,1,0:T(8,128)(2,1)} %tiles_ref.15, f32[768,128]{1,0:T(8,128)} %broadcast_in_dim.55.weight_ref, f32[768,128]{1,0:T(8,128)} %get-tuple-element.13.anchor_ref, bf16[6,128,128]{2,1,0:T(8,128)(2,1)} %bitcast.55, ...), custom_call_target="tpu_custom_call" | custom-call | flops 301989888 | bytes 5242880 | tf_op jit(solution)/shard_map/spread/pallas_call | solution.py:192
  317.1 9.6 %collective-permute-done.30.refs_3_ = bf16[6,128,128]{2,1,0:T(8,128)(2,1)S(1)} collective-permute-done((bf16[6,128,128]{2,1,0:T(8,128)(2,1)}, bf16[6,128,128]{2,1,0:T(8,128)(2,1)S(1)}, u32[]{:S(2)}, u32[]{:S(2)}) %collective-permute-start.30) | collective-permute-done | bytes 196640 | tf_op jit(solution)/shard_map/ppermute | solution.py:244
  331.7 6.2 %all-to-all-done.6.refs_4_.refs_1_ = bf16[32,2,128,128]{3,2,1,0:T(8,128)(2,1)} async-done(((bf16[32,2,128,128]{3,2,1,0:T(8,128)(2,1)}), bf16[32,2,128,128]{3,2,1,0:T(8,128)(2,1)}, u32[]{:S(2)}, u32[]{:S(2)}) %all-to-all-start.6) | async-done | bytes 2097184 | tf_op jit(solution)/shard_map/all_to_all | solution.py:254
  337.9 6.2 %all-to-all-start.8 = ((bf16[32,2,128,128]{3,2,1,0:T(8,128)(2,1)}), bf16[32,2,128,128]{3,2,1,0:T(8,128)(2,1)S(1)}, u32[]{:S(2)}, u32[]{:S(2)}) async-start(bf16[32,2,128,128]{3,2,1,0:T(8,128)(2,1)} %bitcast.25), calls=%async_computation.8 | async-start | bytes 4194304 | tf_op jit(solution)/shard_map/all_to_all | solution.py:254
  344.1 12.6 %collective-permute-start.23 = (bf16[32,2,128,128]{3,2,1,0:T(8,128)(2,1)}, bf16[32,2,128,128]{3,2,1,0:T(8,128)(2,1)}, u32[]{:S(2)}, u32[]{:S(2)}) collective-permute-start(bf16[32,2,128,128]{3,2,1,0:T(8,128)(2,1)} %all-to-all-done.6.refs_4_.refs_1_), channel_id=1, source_target_pairs={{0,4},{4,0},{1,5},{5,1},{2,6},{6,2},{3,7},{7,3},{8,12},{12,8},{9,1... | collective-permute-start | bytes 6291464 | tf_op jit(solution)/shard_map/ppermute | solution.py:256
  356.8 4.1 collective-permute-done.23.refs_5_
  360.9 6.0 %spread.12 = bf16[768,128]{1,0:T(8,128)(2,1)} custom-call(s32[72]{0:T(128)} %reshape.197.index_ref, s32[1]{0:T(128)} %bitcast.core_ref, bf16[6,12,128,128]{3,2,1,0:T(8,128)(2,1)} %tiles_ref.15, f32[768,128]{1,0:T(8,128)} %broadcast_in_dim.55.weight_ref, f32[768,128]{1,0:T(8,128)} %get-tuple-element.14.anchor_ref, bf16[6,128,128]{2,1,0:T(8,128)(2,1)} %bitcast.50, ...), custom_call_target="tpu_custom_call" | custom-call | flops 301989888 | bytes 5242880 | tf_op jit(solution)/shard_map/spread/pallas_call | solution.py:192
  370.2 9.6 %collective-permute-done.26.refs_3_ = bf16[6,128,128]{2,1,0:T(8,128)(2,1)S(1)} collective-permute-done((bf16[6,128,128]{2,1,0:T(8,128)(2,1)}, bf16[6,128,128]{2,1,0:T(8,128)(2,1)S(1)}, u32[]{:S(2)}, u32[]{:S(2)}) %collective-permute-start.26) | collective-permute-done | bytes 196640 | tf_op jit(solution)/shard_map/ppermute | solution.py:244
  384.8 16.8 %all-to-all-start.7 = ((bf16[64,128,128]{2,1,0:T(8,128)(2,1)}), bf16[64,128,128]{2,1,0:T(8,128)(2,1)}, u32[]{:S(2)}, u32[]{:S(2)}) async-start(bf16[64,128,128]{2,1,0:T(8,128)(2,1)} %reply.14), calls=%async_computation.7 | async-start | bytes 4194304 | tf_op jit(solution)/shard_map/all_to_all | solution.py:251
  402.5 3.6 collective-permute-done.31.refs_5_
  406.0 6.1 %spread.14.refs_5_ = f32[768,128]{1,0:T(8,128)} custom-call(s32[72]{0:T(128)} %reshape.197.index_ref, s32[1]{0:T(128)} %bitcast.core_ref, bf16[6,12,128,128]{3,2,1,0:T(8,128)(2,1)} %tiles_ref.15, f32[768,128]{1,0:T(8,128)} %broadcast_in_dim.55.weight_ref, f32[768,128]{1,0:T(8,128)} %get-tuple-element.13.anchor_ref, bf16[6,128,128]{2,1,0:T(8,128)(2,1)} %bitcast.35, ...), custom_call_target="tpu_custom_call" | custom-call | flops 301989888 | bytes 5242880 | tf_op jit(solution)/shard_map/spread/pallas_call | solution.py:192
  412.2 40.6 %all-to-all-done.7.refs_4_ = bf16[64,128,128]{2,1,0:T(8,128)(2,1)} async-done(((bf16[64,128,128]{2,1,0:T(8,128)(2,1)}), bf16[64,128,128]{2,1,0:T(8,128)(2,1)}, u32[]{:S(2)}, u32[]{:S(2)}) %all-to-all-start.7) | async-done | bytes 2097184 | tf_op jit(solution)/shard_map/all_to_all | solution.py:251
  452.8 5.7 %spread.15 = f32[768,256]{1,0:T(8,128)} custom-call(s32[72]{0:T(128)} %reshape.195.index_ref, s32[1]{0:T(128)} %bitcast.core_ref, bf16[6,12,128,128]{3,2,1,0:T(8,128)(2,1)} %tiles_ref.15, f32[768,128]{1,0:T(8,128)} %broadcast_in_dim.55.weight_ref, f32[768,128]{1,0:T(8,128)} %get-tuple-element.14.anchor_ref, bf16[6,128,128]{2,1,0:T(8,128)(2,1)} %bitcast.60, ...), custom_call_target="tpu_custom_call" | custom-call | flops 301989888 | bytes 5242880 | tf_op jit(solution)/shard_map/spread/pallas_call | solution.py:192
  (144 shorter events, 68.7 us)
Async XLA Ops:
  3.3 29.2 %collective-permute-start.10 = (bf16[6,128,128]{2,1,0:T(8,128)(2,1)}, bf16[6,128,128]{2,1,0:T(8,128)(2,1)S(1)}, u32[]{:S(2)}, u32[]{:S(2)}) collective-permute-start(bf16[6,128,128]{2,1,0:T(8,128)(2,1)} %bitcast.74), channel_id=1, source_target_pairs={{3,0},{0,1},{1,2},{2,3},{7,4},{4,5},{5,6},{6,7},{11,8},{8,9},{9,10... | collective-permute-start | bytes 589832 | tf_op jit(solution)/shard_map/ppermute | solution.py:244
  4.8 27.8 %collective-permute-start.9 = (bf16[6,128,128]{2,1,0:T(8,128)(2,1)}, bf16[6,128,128]{2,1,0:T(8,128)(2,1)S(1)}, u32[]{:S(2)}, u32[]{:S(2)}) collective-permute-start(bf16[6,128,128]{2,1,0:T(8,128)(2,1)} %bitcast.75), channel_id=1, source_target_pairs={{2,0},{3,1},{0,2},{1,3},{6,4},{7,5},{4,6},{5,7},{10,8},{11,9},{8,1... | collective-permute-start | bytes 589832 | tf_op jit(solution)/shard_map/ppermute | solution.py:244
  7.5 25.0 %collective-permute-start.8 = (bf16[6,128,128]{2,1,0:T(8,128)(2,1)}, bf16[6,128,128]{2,1,0:T(8,128)(2,1)S(1)}, u32[]{:S(2)}, u32[]{:S(2)}) collective-permute-start(bf16[6,128,128]{2,1,0:T(8,128)(2,1)} %bitcast.76), channel_id=1, source_target_pairs={{1,0},{2,1},{3,2},{0,3},{5,4},{6,5},{7,6},{4,7},{9,8},{10,9},{11,1... | collective-permute-start | bytes 589832 | tf_op jit(solution)/shard_map/ppermute | solution.py:244
  10.1 1.3 collective-permute-start.3
  12.3 20.3 %all-to-all-start = ((s32[32,1,128]{2,1,0:T(1,128)}), s32[32,1,128]{2,1,0:T(1,128)S(1)}, u32[]{:S(2)}, u32[]{:S(2)}) async-start(s32[32,1,128]{2,1,0:T(1,128)} %broadcast_select_fusion), calls=%async_computation | async-start | bytes 32768 | tf_op jit(solution)/shard_map/all_to_all | solution.py:39
  36.9 5.3 %copy-start.9 = (bf16[768,128]{1,0:T(8,128)(2,1)S(1)}, bf16[768,128]{1,0:T(8,128)(2,1)}, u32[]{:S(2)}) copy-start(bf16[768,128]{1,0:T(8,128)(2,1)} %get-tuple-element.9) | copy-start | bytes 589828
  36.9 45.1 %all-to-all-start.2 = ((bf16[32,2,128,128]{3,2,1,0:T(8,128)(2,1)}), bf16[32,2,128,128]{3,2,1,0:T(8,128)(2,1)S(1)}, u32[]{:S(2)}, u32[]{:S(2)}) async-start(bf16[32,2,128,128]{3,2,1,0:T(8,128)(2,1)} %bitcast.29), calls=%async_computation.2 | async-start | bytes 4194304 | tf_op jit(solution)/shard_map/all_to_all | solution.py:254
  42.1 9.1 %collective-permute-start.2 = (bf16[6,128,128]{2,1,0:T(8,128)(2,1)S(1)}, bf16[6,128,128]{2,1,0:T(8,128)(2,1)S(1)}, u32[]{:S(2)}, u32[]{:S(2)}) collective-permute-start(bf16[6,128,128]{2,1,0:T(8,128)(2,1)S(1)} %bitcast.71), channel_id=1, source_target_pairs={{3,0},{0,1},{1,2},{2,3},{7,4},{4,5},{5,6},{6,7},{11,8},{8,9},{9,10... | collective-permute-start | bytes 589832 | tf_op jit(solution)/shard_map/ppermute | solution.py:244
  42.8 8.4 %collective-permute-start.1 = (bf16[6,128,128]{2,1,0:T(8,128)(2,1)S(1)}, bf16[6,128,128]{2,1,0:T(8,128)(2,1)S(1)}, u32[]{:S(2)}, u32[]{:S(2)}) collective-permute-start(bf16[6,128,128]{2,1,0:T(8,128)(2,1)S(1)} %bitcast.72), channel_id=1, source_target_pairs={{2,0},{3,1},{0,2},{1,3},{6,4},{7,5},{4,6},{5,7},{10,8},{11,9},{8,1... | collective-permute-start | bytes 589832 | tf_op jit(solution)/shard_map/ppermute | solution.py:244
  43.7 8.4 %collective-permute-start = (bf16[6,128,128]{2,1,0:T(8,128)(2,1)S(1)}, bf16[6,128,128]{2,1,0:T(8,128)(2,1)S(1)}, u32[]{:S(2)}, u32[]{:S(2)}) collective-permute-start(bf16[6,128,128]{2,1,0:T(8,128)(2,1)S(1)} %bitcast.73), channel_id=1, source_target_pairs={{1,0},{2,1},{3,2},{0,3},{5,4},{6,5},{7,6},{4,7},{9,8},{10,9},{11,1... | collective-permute-start | bytes 589832 | tf_op jit(solution)/shard_map/ppermute | solution.py:244
  83.4 17.9 %copy-start = (bf16[6,12,128,128]{3,2,1,0:T(8,128)(2,1)S(1)}, bf16[6,12,128,128]{3,2,1,0:T(8,128)(2,1)}, u32[]{:S(2)}) copy-start(bf16[6,12,128,128]{3,2,1,0:T(8,128)(2,1)} %tiles_ref.15) | copy-start | bytes 7077892
  83.4 46.6 %all-to-all-start.1 = ((bf16[32,2,128,128]{3,2,1,0:T(8,128)(2,1)}), bf16[32,2,128,128]{3,2,1,0:T(8,128)(2,1)}, u32[]{:S(2)}, u32[]{:S(2)}) async-start(bf16[32,2,128,128]{3,2,1,0:T(8,128)(2,1)} %bitcast.30), calls=%async_computation.1 | async-start | bytes 4194304 | tf_op jit(solution)/shard_map/all_to_all | solution.py:254
  88.5 13.2 %copy-start.8 = (f32[768,256]{1,0:T(8,128)S(1)}, f32[768,256]{1,0:T(8,128)}, u32[]{:S(2)}) copy-start(f32[768,256]{1,0:T(8,128)} %get-tuple-element.8) | copy-start | bytes 2359300
  88.5 16.3 %collective-permute-start.11 = (bf16[32,2,128,128]{3,2,1,0:T(8,128)(2,1)}, bf16[32,2,128,128]{3,2,1,0:T(8,128)(2,1)}, u32[]{:S(2)}, u32[]{:S(2)}) collective-permute-start(bf16[32,2,128,128]{3,2,1,0:T(8,128)(2,1)} %copy-done.6), channel_id=1, source_target_pairs={{0,4},{4,0},{1,5},{5,1},{2,6},{6,2},{3,7},{7,3},{8,12},{12,8},{9,1... | collective-permute-start | bytes 6291464 | tf_op jit(solution)/shard_map/ppermute | solution.py:256
  111.7 12.9 %collective-permute-start.14 = (bf16[6,128,128]{2,1,0:T(8,128)(2,1)}, bf16[6,128,128]{2,1,0:T(8,128)(2,1)S(1)}, u32[]{:S(2)}, u32[]{:S(2)}) collective-permute-start(bf16[6,128,128]{2,1,0:T(8,128)(2,1)} %bitcast.36), channel_id=1, source_target_pairs={{3,0},{0,1},{1,2},{2,3},{7,4},{4,5},{5,6},{6,7},{11,8},{8,9},{9,10... | collective-permute-start | bytes 589832 | tf_op jit(solution)/shard_map/ppermute | solution.py:244
  112.4 12.2 %collective-permute-start.13 = (bf16[6,128,128]{2,1,0:T(8,128)(2,1)}, bf16[6,128,128]{2,1,0:T(8,128)(2,1)S(1)}, u32[]{:S(2)}, u32[]{:S(2)}) collective-permute-start(bf16[6,128,128]{2,1,0:T(8,128)(2,1)} %bitcast.37), channel_id=1, source_target_pairs={{2,0},{3,1},{0,2},{1,3},{6,4},{7,5},{4,6},{5,7},{10,8},{11,9},{8,1... | collective-permute-start | bytes 589832 | tf_op jit(solution)/shard_map/ppermute | solution.py:244
  113.3 12.0 %collective-permute-start.12 = (bf16[6,128,128]{2,1,0:T(8,128)(2,1)}, bf16[6,128,128]{2,1,0:T(8,128)(2,1)S(1)}, u32[]{:S(2)}, u32[]{:S(2)}) collective-permute-start(bf16[6,128,128]{2,1,0:T(8,128)(2,1)} %bitcast.38), channel_id=1, source_target_pairs={{1,0},{2,1},{3,2},{0,3},{5,4},{6,5},{7,6},{4,7},{9,8},{10,9},{11,1... | collective-permute-start | bytes 589832 | tf_op jit(solution)/shard_map/ppermute | solution.py:244
  130.0 53.4 %all-to-all-start.3 = ((bf16[32,2,128,128]{3,2,1,0:T(8,128)(2,1)}), bf16[32,2,128,128]{3,2,1,0:T(8,128)(2,1)S(1)}, u32[]{:S(2)}, u32[]{:S(2)}) async-start(bf16[32,2,128,128]{3,2,1,0:T(8,128)(2,1)} %bitcast.26), calls=%async_computation.3 | async-start | bytes 4194304 | tf_op jit(solution)/shard_map/all_to_all | solution.py:254
  139.4 15.1 %collective-permute-start.4 = (bf16[32,2,128,128]{3,2,1,0:T(8,128)(2,1)}, bf16[32,2,128,128]{3,2,1,0:T(8,128)(2,1)}, u32[]{:S(2)}, u32[]{:S(2)}) collective-permute-start(bf16[32,2,128,128]{3,2,1,0:T(8,128)(2,1)} %all-to-all-done.1.refs_4_.refs_1_), channel_id=1, source_target_pairs={{0,4},{4,0},{1,5},{5,1},{2,6},{6,2},{3,7},{7,3},{8,12},{12,8},{9,1... | collective-permute-start | bytes 6291464 | tf_op jit(solution)/shard_map/ppermute | solution.py:256
  160.6 13.1 %collective-permute-start.7 = (bf16[6,128,128]{2,1,0:T(8,128)(2,1)}, bf16[6,128,128]{2,1,0:T(8,128)(2,1)S(1)}, u32[]{:S(2)}, u32[]{:S(2)}) collective-permute-start(bf16[6,128,128]{2,1,0:T(8,128)(2,1)} %bitcast.41), channel_id=1, source_target_pairs={{3,0},{0,1},{1,2},{2,3},{7,4},{4,5},{5,6},{6,7},{11,8},{8,9},{9,10... | collective-permute-start | bytes 589832 | tf_op jit(solution)/shard_map/ppermute | solution.py:244
  161.4 12.2 %collective-permute-start.6 = (bf16[6,128,128]{2,1,0:T(8,128)(2,1)}, bf16[6,128,128]{2,1,0:T(8,128)(2,1)S(1)}, u32[]{:S(2)}, u32[]{:S(2)}) collective-permute-start(bf16[6,128,128]{2,1,0:T(8,128)(2,1)} %bitcast.42), channel_id=1, source_target_pairs={{2,0},{3,1},{0,2},{1,3},{6,4},{7,5},{4,6},{5,7},{10,8},{11,9},{8,1... | collective-permute-start | bytes 589832 | tf_op jit(solution)/shard_map/ppermute | solution.py:244
  162.3 12.0 %collective-permute-start.5 = (bf16[6,128,128]{2,1,0:T(8,128)(2,1)}, bf16[6,128,128]{2,1,0:T(8,128)(2,1)S(1)}, u32[]{:S(2)}, u32[]{:S(2)}) collective-permute-start(bf16[6,128,128]{2,1,0:T(8,128)(2,1)} %bitcast.43), channel_id=1, source_target_pairs={{1,0},{2,1},{3,2},{0,3},{5,4},{6,5},{7,6},{4,7},{9,8},{10,9},{11,1... | collective-permute-start | bytes 589832 | tf_op jit(solution)/shard_map/ppermute | solution.py:244
  184.7 46.1 %all-to-all-start.4 = ((bf16[32,2,128,128]{3,2,1,0:T(8,128)(2,1)}), bf16[32,2,128,128]{3,2,1,0:T(8,128)(2,1)}, u32[]{:S(2)}, u32[]{:S(2)}) async-start(bf16[32,2,128,128]{3,2,1,0:T(8,128)(2,1)} %bitcast.27), calls=%async_computation.4 | async-start | bytes 4194304 | tf_op jit(solution)/shard_map/all_to_all | solution.py:254
  190.0 16.5 %collective-permute-start.19 = (bf16[32,2,128,128]{3,2,1,0:T(8,128)(2,1)S(1)}, bf16[32,2,128,128]{3,2,1,0:T(8,128)(2,1)}, u32[]{:S(2)}, u32[]{:S(2)}) collective-permute-start(bf16[32,2,128,128]{3,2,1,0:T(8,128)(2,1)S(1)} %copy-done.2), channel_id=1, source_target_pairs={{0,4},{4,0},{1,5},{5,1},{2,6},{6,2},{3,7},{7,3},{8,12},{12,8},{9,1... | collective-permute-start | bytes 6291464 | tf_op jit(solution)/shard_map/ppermute | solution.py:256
  212.6 8.7 %collective-permute-start.22 = (bf16[6,128,128]{2,1,0:T(8,128)(2,1)}, bf16[6,128,128]{2,1,0:T(8,128)(2,1)S(1)}, u32[]{:S(2)}, u32[]{:S(2)}) collective-permute-start(bf16[6,128,128]{2,1,0:T(8,128)(2,1)} %bitcast.51), channel_id=1, source_target_pairs={{3,0},{0,1},{1,2},{2,3},{7,4},{4,5},{5,6},{6,7},{11,8},{8,9},{9,10... | collective-permute-start | bytes 589832 | tf_op jit(solution)/shard_map/ppermute | solution.py:244
  212.9 13.1 %collective-permute-start.21 = (bf16[6,128,128]{2,1,0:T(8,128)(2,1)}, bf16[6,128,128]{2,1,0:T(8,128)(2,1)S(1)}, u32[]{:S(2)}, u32[]{:S(2)}) collective-permute-start(bf16[6,128,128]{2,1,0:T(8,128)(2,1)} %bitcast.52), channel_id=1, source_target_pairs={{2,0},{3,1},{0,2},{1,3},{6,4},{7,5},{4,6},{5,7},{10,8},{11,9},{8,1... | collective-permute-start | bytes 589832 | tf_op jit(solution)/shard_map/ppermute | solution.py:244
  216.4 9.6 %collective-permute-start.20 = (bf16[6,128,128]{2,1,0:T(8,128)(2,1)}, bf16[6,128,128]{2,1,0:T(8,128)(2,1)S(1)}, u32[]{:S(2)}, u32[]{:S(2)}) collective-permute-start(bf16[6,128,128]{2,1,0:T(8,128)(2,1)} %bitcast.53), channel_id=1, source_target_pairs={{1,0},{2,1},{3,2},{0,3},{5,4},{6,5},{7,6},{4,7},{9,8},{10,9},{11,1... | collective-permute-start | bytes 589832 | tf_op jit(solution)/shard_map/ppermute | solution.py:244
  230.9 51.8 %all-to-all-start.5 = ((bf16[32,2,128,128]{3,2,1,0:T(8,128)(2,1)}), bf16[32,2,128,128]{3,2,1,0:T(8,128)(2,1)S(1)}, u32[]{:S(2)}, u32[]{:S(2)}) async-start(bf16[32,2,128,128]{3,2,1,0:T(8,128)(2,1)} %bitcast.28), calls=%async_computation.5 | async-start | bytes 4194304 | tf_op jit(solution)/shard_map/all_to_all | solution.py:254
  240.7 15.9 %collective-permute-start.15 = (bf16[32,2,128,128]{3,2,1,0:T(8,128)(2,1)}, bf16[32,2,128,128]{3,2,1,0:T(8,128)(2,1)}, u32[]{:S(2)}, u32[]{:S(2)}) collective-permute-start(bf16[32,2,128,128]{3,2,1,0:T(8,128)(2,1)} %all-to-all-done.4.refs_4_.refs_1_), channel_id=1, source_target_pairs={{0,4},{4,0},{1,5},{5,1},{2,6},{6,2},{3,7},{7,3},{8,12},{12,8},{9,1... | collective-permute-start | bytes 6291464 | tf_op jit(solution)/shard_map/ppermute | solution.py:256
  262.6 9.8 %collective-permute-start.18 = (bf16[6,128,128]{2,1,0:T(8,128)(2,1)}, bf16[6,128,128]{2,1,0:T(8,128)(2,1)S(1)}, u32[]{:S(2)}, u32[]{:S(2)}) collective-permute-start(bf16[6,128,128]{2,1,0:T(8,128)(2,1)} %bitcast.46), channel_id=1, source_target_pairs={{3,0},{0,1},{1,2},{2,3},{7,4},{4,5},{5,6},{6,7},{11,8},{8,9},{9,10... | collective-permute-start | bytes 589832 | tf_op jit(solution)/shard_map/ppermute | solution.py:244
  262.9 14.9 %collective-permute-start.17 = (bf16[6,128,128]{2,1,0:T(8,128)(2,1)}, bf16[6,128,128]{2,1,0:T(8,128)(2,1)S(1)}, u32[]{:S(2)}, u32[]{:S(2)}) collective-permute-start(bf16[6,128,128]{2,1,0:T(8,128)(2,1)} %bitcast.47), channel_id=1, source_target_pairs={{2,0},{3,1},{0,2},{1,3},{6,4},{7,5},{4,6},{5,7},{10,8},{11,9},{8,1... | collective-permute-start | bytes 589832 | tf_op jit(solution)/shard_map/ppermute | solution.py:244
  268.2 9.6 %collective-permute-start.16 = (bf16[6,128,128]{2,1,0:T(8,128)(2,1)}, bf16[6,128,128]{2,1,0:T(8,128)(2,1)S(1)}, u32[]{:S(2)}, u32[]{:S(2)}) collective-permute-start(bf16[6,128,128]{2,1,0:T(8,128)(2,1)} %bitcast.48), channel_id=1, source_target_pairs={{1,0},{2,1},{3,2},{0,3},{5,4},{6,5},{7,6},{4,7},{9,8},{10,9},{11,1... | collective-permute-start | bytes 589832 | tf_op jit(solution)/shard_map/ppermute | solution.py:244
  272.4 5.4 %copy-start.21 = (bf16[6,128,128]{2,1,0:T(8,128)(2,1)}, bf16[6,128,128]{2,1,0:T(8,128)(2,1)S(1)}, u32[]{:S(2)}) copy-start(bf16[6,128,128]{2,1,0:T(8,128)(2,1)S(1)} %collective-permute-done.18.refs_3_) | copy-start | bytes 589828
  284.1 10.0 %copy-start.4 = (bf16[32,2,128,128]{3,2,1,0:T(8,128)(2,1)S(1)}, bf16[32,2,128,128]{3,2,1,0:T(8,128)(2,1)}, u32[]{:S(2)}) copy-start(bf16[32,2,128,128]{3,2,1,0:T(8,128)(2,1)} %copy-done.3) | copy-start | bytes 6291460
  284.1 53.8 %all-to-all-start.6 = ((bf16[32,2,128,128]{3,2,1,0:T(8,128)(2,1)}), bf16[32,2,128,128]{3,2,1,0:T(8,128)(2,1)}, u32[]{:S(2)}, u32[]{:S(2)}) async-start(bf16[32,2,128,128]{3,2,1,0:T(8,128)(2,1)} %bitcast.24), calls=%async_computation.6 | async-start | bytes 4194304 | tf_op jit(solution)/shard_map/all_to_all | solution.py:254
  294.1 13.7 %collective-permute-start.27 = (bf16[32,2,128,128]{3,2,1,0:T(8,128)(2,1)S(1)}, bf16[32,2,128,128]{3,2,1,0:T(8,128)(2,1)}, u32[]{:S(2)}, u32[]{:S(2)}) collective-permute-start(bf16[32,2,128,128]{3,2,1,0:T(8,128)(2,1)S(1)} %copy-done.4), channel_id=1, source_target_pairs={{0,4},{4,0},{1,5},{5,1},{2,6},{6,2},{3,7},{7,3},{8,12},{12,8},{9,1... | collective-permute-start | bytes 6291464 | tf_op jit(solution)/shard_map/ppermute | solution.py:256
  313.8 12.9 %collective-permute-start.30 = (bf16[6,128,128]{2,1,0:T(8,128)(2,1)}, bf16[6,128,128]{2,1,0:T(8,128)(2,1)S(1)}, u32[]{:S(2)}, u32[]{:S(2)}) collective-permute-start(bf16[6,128,128]{2,1,0:T(8,128)(2,1)} %bitcast.31), channel_id=1, source_target_pairs={{3,0},{0,1},{1,2},{2,3},{7,4},{4,5},{5,6},{6,7},{11,8},{8,9},{9,10... | collective-permute-start | bytes 589832 | tf_op jit(solution)/shard_map/ppermute | solution.py:244
  313.9 12.8 %collective-permute-start.29 = (bf16[6,128,128]{2,1,0:T(8,128)(2,1)}, bf16[6,128,128]{2,1,0:T(8,128)(2,1)S(1)}, u32[]{:S(2)}, u32[]{:S(2)}) collective-permute-start(bf16[6,128,128]{2,1,0:T(8,128)(2,1)} %bitcast.32), channel_id=1, source_target_pairs={{2,0},{3,1},{0,2},{1,3},{6,4},{7,5},{4,6},{5,7},{10,8},{11,9},{8,1... | collective-permute-start | bytes 589832 | tf_op jit(solution)/shard_map/ppermute | solution.py:244
  317.0 10.3 %collective-permute-start.28 = (bf16[6,128,128]{2,1,0:T(8,128)(2,1)}, bf16[6,128,128]{2,1,0:T(8,128)(2,1)S(1)}, u32[]{:S(2)}, u32[]{:S(2)}) collective-permute-start(bf16[6,128,128]{2,1,0:T(8,128)(2,1)} %bitcast.33), channel_id=1, source_target_pairs={{1,0},{2,1},{3,2},{0,3},{5,4},{6,5},{7,6},{4,7},{9,8},{10,9},{11,1... | collective-permute-start | bytes 589832 | tf_op jit(solution)/shard_map/ppermute | solution.py:244
  337.9 46.9 %all-to-all-start.8 = ((bf16[32,2,128,128]{3,2,1,0:T(8,128)(2,1)}), bf16[32,2,128,128]{3,2,1,0:T(8,128)(2,1)S(1)}, u32[]{:S(2)}, u32[]{:S(2)}) async-start(bf16[32,2,128,128]{3,2,1,0:T(8,128)(2,1)} %bitcast.25), calls=%async_computation.8 | async-start | bytes 4194304 | tf_op jit(solution)/shard_map/all_to_all | solution.py:254
  344.1 16.8 %collective-permute-start.23 = (bf16[32,2,128,128]{3,2,1,0:T(8,128)(2,1)}, bf16[32,2,128,128]{3,2,1,0:T(8,128)(2,1)}, u32[]{:S(2)}, u32[]{:S(2)}) collective-permute-start(bf16[32,2,128,128]{3,2,1,0:T(8,128)(2,1)} %all-to-all-done.6.refs_4_.refs_1_), channel_id=1, source_target_pairs={{0,4},{4,0},{1,5},{5,1},{2,6},{6,2},{3,7},{7,3},{8,12},{12,8},{9,1... | collective-permute-start | bytes 6291464 | tf_op jit(solution)/shard_map/ppermute | solution.py:256
  366.9 12.9 %collective-permute-start.26 = (bf16[6,128,128]{2,1,0:T(8,128)(2,1)}, bf16[6,128,128]{2,1,0:T(8,128)(2,1)S(1)}, u32[]{:S(2)}, u32[]{:S(2)}) collective-permute-start(bf16[6,128,128]{2,1,0:T(8,128)(2,1)} %bitcast.56), channel_id=1, source_target_pairs={{3,0},{0,1},{1,2},{2,3},{7,4},{4,5},{5,6},{6,7},{11,8},{8,9},{9,10... | collective-permute-start | bytes 589832 | tf_op jit(solution)/shard_map/ppermute | solution.py:244
  367.0 12.8 %collective-permute-start.25 = (bf16[6,128,128]{2,1,0:T(8,128)(2,1)}, bf16[6,128,128]{2,1,0:T(8,128)(2,1)S(1)}, u32[]{:S(2)}, u32[]{:S(2)}) collective-permute-start(bf16[6,128,128]{2,1,0:T(8,128)(2,1)} %bitcast.57), channel_id=1, source_target_pairs={{2,0},{3,1},{0,2},{1,3},{6,4},{7,5},{4,6},{5,7},{10,8},{11,9},{8,1... | collective-permute-start | bytes 589832 | tf_op jit(solution)/shard_map/ppermute | solution.py:244
  370.0 10.5 %collective-permute-start.24 = (bf16[6,128,128]{2,1,0:T(8,128)(2,1)}, bf16[6,128,128]{2,1,0:T(8,128)(2,1)S(1)}, u32[]{:S(2)}, u32[]{:S(2)}) collective-permute-start(bf16[6,128,128]{2,1,0:T(8,128)(2,1)} %bitcast.58), channel_id=1, source_target_pairs={{1,0},{2,1},{3,2},{0,3},{5,4},{6,5},{7,6},{4,7},{9,8},{10,9},{11,1... | collective-permute-start | bytes 589832 | tf_op jit(solution)/shard_map/ppermute | solution.py:244
  384.8 17.1 %copy-start.34 = (s32[6,12]{1,0:T(8,128)S(1)}, s32[6,12]{1,0:T(8,128)}, u32[]{:S(2)}) copy-start(s32[6,12]{1,0:T(8,128)} %param.6) | copy-start | bytes 868
  384.8 16.8 %copy-start.5 = (bf16[32,2,128,128]{3,2,1,0:T(8,128)(2,1)}, bf16[32,2,128,128]{3,2,1,0:T(8,128)(2,1)S(1)}, u32[]{:S(2)}) copy-start(bf16[32,2,128,128]{3,2,1,0:T(8,128)(2,1)S(1)} %all-to-all-done.8.refs_4_) | copy-start | bytes 6291460
  384.8 68.0 %all-to-all-start.7 = ((bf16[64,128,128]{2,1,0:T(8,128)(2,1)}), bf16[64,128,128]{2,1,0:T(8,128)(2,1)}, u32[]{:S(2)}, u32[]{:S(2)}) async-start(bf16[64,128,128]{2,1,0:T(8,128)(2,1)} %reply.14), calls=%async_computation.7 | async-start | bytes 4194304 | tf_op jit(solution)/shard_map/all_to_all | solution.py:251
  401.7 4.4 collective-permute-start.31
  (28 other events, 30.5 us)

commit v5 on v4

--- a/solution.py
+++ b/solution.py
@@ -225,7 +225,6 @@
     chip, core = owner_group // 2, owner_group % 2
     slot = group_size + chip + jnp.where(core == own_core, 0, n_chips)
     index = jnp.where(owner_group == own_group, place, slot).reshape(-1)
-    index_last = jnp.where(owner_group == own_group, place, group_size + owner_group).reshape(-1)
     asked = ask_blocks(owner_group, place, own_group, n_rows)
     anchor, blended = prepare(label_prior, seed_label, seed_mask)
 
@@ -247,15 +246,12 @@
             reply = reply_blocks(asked, pieces)
             if (hop, p) in HOLD:
                 reply = held(reply, (own_core * HOLD[hop, p]).reshape(1), before)
-            if last and p == PARTS - 1:
-                remote = [lax.all_to_all(reply, GROUP, 0, 0, tiled=True)]
-            else:
-                reply = reply.reshape(n_chips, 2, block, width)
-                same = lax.all_to_all(reply, "zy", 0, 0, tiled=True)
-                before = [same]
-                remote = [same, lax.ppermute(same, "core", [(0, 1), (1, 0)])]
+            reply = reply.reshape(n_chips, 2, block, width)
+            same = lax.all_to_all(reply, "zy", 0, 0, tiled=True)
+            before = [same]
+            remote = [same, lax.ppermute(same, "core", [(0, 1), (1, 0)])]
             blended[p] = spread_blocks(
-                index_last if len(remote) == 1 else index,
+                index,
                 own_core.reshape(1), adjacency_tiles, weight, anchors[p], pieces + remote,
                 jnp.float32 if last else jnp.bfloat16,
                 blended[0] if last and p == PARTS - 1 else None,

time: 461 us -> 460 us (level)
    all_to_all x1 -> x0, waiting for transfers between devices: 40.6 us -> none  [local(): remote = [lax.all_to_all(reply, GROUP, 0, 0, tiled=True)]]
    all_to_all x7 -> x8, waiting for transfers between devices: 37 us -> 76.5 us  [local(): same = lax.all_to_all(reply, 'zy', 0, 0, tiled=True)]
    all_to_all x1 -> x0, starting transfers between devices: 16.8 us -> none  [local(): remote = [lax.all_to_all(reply, GROUP, 0, 0, tiled=True)]]
    all_to_all x7 -> x8, starting transfers between devices: 51 us -> 62.1 us  [local(): same = lax.all_to_all(reply, 'zy', 0, 0, tiled=True)]
    ppermute x7 -> x8, starting transfers between devices: 70.1 us -> 79.5 us  [local(): remote = [same, lax.ppermute(same, 'core', [(0, 1), (1, 0)])]]
    ppermute x24, waiting for transfers between devices: 66.3 us -> 73.6 us  [local(): lax.ppermute(own, 'x', [((x + d) % n_cols, x) for x in range(n_cols)])]
    ppermute x24, starting transfers between devices: 32.2 us -> 25.7 us  [local(): lax.ppermute(own, 'x', [((x + d) % n_cols, x) for x in range(n_cols)])]
    ppermute x7 -> x8, waiting for transfers between devices: 25.9 us -> 22.3 us  [local(): remote = [same, lax.ppermute(same, 'core', [(0, 1), (1, 0)])]]
  transfers between devices with their start and end apart: 41 -> 42, of which waited for: 29 -> 34; matrix products, arithmetic and copies ran while one was open for 1% -> 1% of each run, Pallas kernels for 15% -> 15%
where the time goes in v5:
time: 460 us; the launch traced here: 456 us
  waiting for transfers between devices  182 us (40%)
  starting transfers between devices  179 us (39%)
  Pallas kernels  79.7 us (17%)
  local copies, waits for them, and re-layouts  11.4 us (2%)
    ppermute x8, starting transfers between devices, local(): remote = [same, lax.ppermute(same, 'core', [(0, 1), (1, 0)])]  79.5 us
    all_to_all x8, waiting for transfers between devices, local(): same = lax.all_to_all(reply, 'zy', 0, 0, tiled=True)  76.5 us
    ppermute x24, waiting for transfers between devices, local(): lax.ppermute(own, 'x', [((x + d) % n_cols, x) for x in range(n_cols)])  73.6 us
    all_to_all x8, starting transfers between devices, local(): same = lax.all_to_all(reply, 'zy', 0, 0, tiled=True)  62.1 us
    pallas_call x8, Pallas kernels, spread_blocks(): pl.pallas_call(functools.partial(spread_kernel, n_src=n_src, final=final)...  48 us
    pallas_call x8, Pallas kernels, reply_blocks(): pl.pallas_call(functools.partial(reply_kernel, n_cols=n_cols), out_shape=...  28.4 us
    ppermute x24, starting transfers between devices, local(): lax.ppermute(own, 'x', [((x + d) % n_cols, x) for x in range(n_cols)])  25.7 us
    ppermute x8, waiting for transfers between devices, local(): remote = [same, lax.ppermute(same, 'core', [(0, 1), (1, 0)])]  22.3 us
  transfers between devices with their start and end apart: 42, of which 34 were waited for; matrix products, arithmetic and copies ran while one was open for 1% of the time, Pallas kernels for 15%

profile of v5, /device:TPU:8, one launch (start us, length us, event | category | flops | bytes accessed | tf_op | source)
XLA Modules:
  0.0 456.2 jit_solution(4318374550260788246)
XLA Ops:
  0.0 3.3 prepare.1
  11.7 11.7 %all-to-all-start = ((s32[32,1,128]{2,1,0:T(1,128)}), s32[32,1,128]{2,1,0:T(1,128)S(1)}, u32[]{:S(2)}, u32[]{:S(2)}) async-start(s32[32,1,128]{2,1,0:T(1,128)} %broadcast_select_fusion), calls=%async_computation | async-start | bytes 32768 | tf_op jit(solution)/shard_map/all_to_all | solution.py:39
  23.4 8.6 %all-to-all-done = s32[32,1,128]{2,1,0:T(1,128)S(1)} async-done(((s32[32,1,128]{2,1,0:T(1,128)}), s32[32,1,128]{2,1,0:T(1,128)S(1)}, u32[]{:S(2)}, u32[]{:S(2)}) %all-to-all-start) | async-done | bytes 16416 | tf_op jit(solution)/shard_map/all_to_all | solution.py:39
  32.7 3.5 reply.10.refs_0_
  36.3 5.2 %all-to-all-start.2 = ((bf16[32,2,128,128]{3,2,1,0:T(8,128)(2,1)}), bf16[32,2,128,128]{3,2,1,0:T(8,128)(2,1)S(1)}, u32[]{:S(2)}, u32[]{:S(2)}) async-start(bf16[32,2,128,128]{3,2,1,0:T(8,128)(2,1)} %bitcast.30), calls=%async_computation.2 | async-start | bytes 4194304 | tf_op jit(solution)/shard_map/all_to_all | solution.py:250
  52.7 3.5 reply.8
  56.3 25.2 %all-to-all-done.2.refs_4_ = bf16[32,2,128,128]{3,2,1,0:T(8,128)(2,1)S(1)} async-done(((bf16[32,2,128,128]{3,2,1,0:T(8,128)(2,1)}), bf16[32,2,128,128]{3,2,1,0:T(8,128)(2,1)S(1)}, u32[]{:S(2)}, u32[]{:S(2)}) %all-to-all-start.2) | async-done | bytes 2097184 | tf_op jit(solution)/shard_map/all_to_all | solution.py:250
  82.8 5.1 %all-to-all-start.1 = ((bf16[32,2,128,128]{3,2,1,0:T(8,128)(2,1)}), bf16[32,2,128,128]{3,2,1,0:T(8,128)(2,1)}, u32[]{:S(2)}, u32[]{:S(2)}) async-start(bf16[32,2,128,128]{3,2,1,0:T(8,128)(2,1)} %bitcast.31), calls=%async_computation.1 | async-start | bytes 4194304 | tf_op jit(solution)/shard_map/all_to_all | solution.py:250
  87.9 12.2 %collective-permute-start.11 = (bf16[32,2,128,128]{3,2,1,0:T(8,128)(2,1)}, bf16[32,2,128,128]{3,2,1,0:T(8,128)(2,1)}, u32[]{:S(2)}, u32[]{:S(2)}) collective-permute-start(bf16[32,2,128,128]{3,2,1,0:T(8,128)(2,1)} %copy-done.6), channel_id=1, source_target_pairs={{0,4},{4,0},{1,5},{5,1},{2,6},{6,2},{3,7},{7,3},{8,12},{12,8},{9,1... | collective-permute-start | bytes 6291464 | tf_op jit(solution)/shard_map/ppermute | solution.py:252
  105.1 6.0 %spread.9 = bf16[768,128]{1,0:T(8,128)(2,1)} custom-call(s32[72]{0:T(128)} %reshape.195.index_ref, s32[1]{0:T(128)} %bitcast.core_ref, bf16[6,12,128,128]{3,2,1,0:T(8,128)(2,1)} %tiles_ref.15, f32[768,128]{1,0:T(8,128)} %broadcast_in_dim.56.weight_ref, f32[768,128]{1,0:T(8,128)} %get-tuple-element.13.anchor_ref, bf16[6,128,128]{2,1,0:T(8,128)(2,1)} %bitcast.80, ...), custom_call_target="tpu_custom_call" | custom-call | flops 301989888 | bytes 5242880 | tf_op jit(solution)/shard_map/spread/pallas_call | solution.py:192
  114.3 4.8 %collective-permute-done.12.refs_1_ = bf16[6,128,128]{2,1,0:T(8,128)(2,1)S(1)} collective-permute-done((bf16[6,128,128]{2,1,0:T(8,128)(2,1)}, bf16[6,128,128]{2,1,0:T(8,128)(2,1)S(1)}, u32[]{:S(2)}, u32[]{:S(2)}) %collective-permute-start.12) | collective-permute-done | bytes 196640 | tf_op jit(solution)/shard_map/ppermute | solution.py:243
  125.8 3.5 reply.11.refs_0_
  129.4 9.8 %all-to-all-start.3 = ((bf16[32,2,128,128]{3,2,1,0:T(8,128)(2,1)}), bf16[32,2,128,128]{3,2,1,0:T(8,128)(2,1)S(1)}, u32[]{:S(2)}, u32[]{:S(2)}) async-start(bf16[32,2,128,128]{3,2,1,0:T(8,128)(2,1)} %bitcast.27), calls=%async_computation.3 | async-start | bytes 4194304 | tf_op jit(solution)/shard_map/all_to_all | solution.py:250
  139.2 10.6 %collective-permute-start.4 = (bf16[32,2,128,128]{3,2,1,0:T(8,128)(2,1)}, bf16[32,2,128,128]{3,2,1,0:T(8,128)(2,1)}, u32[]{:S(2)}, u32[]{:S(2)}) collective-permute-start(bf16[32,2,128,128]{3,2,1,0:T(8,128)(2,1)} %all-to-all-done.1.refs_4_.refs_1_), channel_id=1, source_target_pairs={{0,4},{4,0},{1,5},{5,1},{2,6},{6,2},{3,7},{7,3},{8,12},{12,8},{9,1... | collective-permute-start | bytes 6291464 | tf_op jit(solution)/shard_map/ppermute | solution.py:252
  149.8 4.1 collective-permute-done.4.refs_5_
  153.9 6.0 %spread.8 = bf16[768,128]{1,0:T(8,128)(2,1)} custom-call(s32[72]{0:T(128)} %reshape.195.index_ref, s32[1]{0:T(128)} %bitcast.core_ref, bf16[6,12,128,128]{3,2,1,0:T(8,128)(2,1)} %tiles_ref.15, f32[768,128]{1,0:T(8,128)} %broadcast_in_dim.56.weight_ref, f32[768,128]{1,0:T(8,128)} %get-tuple-element.14.anchor_ref, bf16[6,128,128]{2,1,0:T(8,128)(2,1)} %bitcast.72, ...), custom_call_target="tpu_custom_call" | custom-call | flops 301989888 | bytes 5242880 | tf_op jit(solution)/shard_map/spread/pallas_call | solution.py:192
  163.4 4.8 %collective-permute-done.5.refs_1_ = bf16[6,128,128]{2,1,0:T(8,128)(2,1)S(1)} collective-permute-done((bf16[6,128,128]{2,1,0:T(8,128)(2,1)}, bf16[6,128,128]{2,1,0:T(8,128)(2,1)S(1)}, u32[]{:S(2)}, u32[]{:S(2)}) %collective-permute-start.5) | collective-permute-done | bytes 196640 | tf_op jit(solution)/shard_map/ppermute | solution.py:243
  174.9 3.6 reply.9.refs_0_
  178.5 4.8 %all-to-all-done.3.refs_1_.refs_4_ = bf16[32,2,128,128]{3,2,1,0:T(8,128)(2,1)S(1)} async-done(((bf16[32,2,128,128]{3,2,1,0:T(8,128)(2,1)}), bf16[32,2,128,128]{3,2,1,0:T(8,128)(2,1)S(1)}, u32[]{:S(2)}, u32[]{:S(2)}) %all-to-all-start.3) | async-done | bytes 2097184 | tf_op jit(solution)/shard_map/all_to_all | solution.py:250
  184.6 5.6 %all-to-all-start.4 = ((bf16[32,2,128,128]{3,2,1,0:T(8,128)(2,1)}), bf16[32,2,128,128]{3,2,1,0:T(8,128)(2,1)}, u32[]{:S(2)}, u32[]{:S(2)}) async-start(bf16[32,2,128,128]{3,2,1,0:T(8,128)(2,1)} %bitcast.28), calls=%async_computation.4 | async-start | bytes 4194304 | tf_op jit(solution)/shard_map/all_to_all | solution.py:250
  190.3 12.1 %collective-permute-start.19 = (bf16[32,2,128,128]{3,2,1,0:T(8,128)(2,1)S(1)}, bf16[32,2,128,128]{3,2,1,0:T(8,128)(2,1)}, u32[]{:S(2)}, u32[]{:S(2)}) collective-permute-start(bf16[32,2,128,128]{3,2,1,0:T(8,128)(2,1)S(1)} %copy-done.2), channel_id=1, source_target_pairs={{0,4},{4,0},{1,5},{5,1},{2,6},{6,2},{3,7},{7,3},{8,12},{12,8},{9,1... | collective-permute-start | bytes 6291464 | tf_op jit(solution)/shard_map/ppermute | solution.py:252
  202.4 3.9 collective-permute-done.19.refs_5_
  206.3 6.0 %spread.11 = bf16[768,128]{1,0:T(8,128)(2,1)} custom-call(s32[72]{0:T(128)} %reshape.195.index_ref, s32[1]{0:T(128)} %bitcast.core_ref, bf16[6,12,128,128]{3,2,1,0:T(8,128)(2,1)} %tiles_ref.15, f32[768,128]{1,0:T(8,128)} %broadcast_in_dim.56.weight_ref, f32[768,128]{1,0:T(8,128)} %get-tuple-element.13.anchor_ref, bf16[6,128,128]{2,1,0:T(8,128)(2,1)} %bitcast.42, ...), custom_call_target="tpu_custom_call" | custom-call | flops 301989888 | bytes 5242880 | tf_op jit(solution)/shard_map/spread/pallas_call | solution.py:192
  215.4 5.0 %collective-permute-done.20.refs_1_ = bf16[6,128,128]{2,1,0:T(8,128)(2,1)S(1)} collective-permute-done((bf16[6,128,128]{2,1,0:T(8,128)(2,1)}, bf16[6,128,128]{2,1,0:T(8,128)(2,1)S(1)}, u32[]{:S(2)}, u32[]{:S(2)}) %collective-permute-start.20) | collective-permute-done | bytes 196640 | tf_op jit(solution)/shard_map/ppermute | solution.py:243
  226.9 3.5 reply.13.refs_0_
  231.4 8.9 %all-to-all-start.5 = ((bf16[32,2,128,128]{3,2,1,0:T(8,128)(2,1)}), bf16[32,2,128,128]{3,2,1,0:T(8,128)(2,1)S(1)}, u32[]{:S(2)}, u32[]{:S(2)}) async-start(bf16[32,2,128,128]{3,2,1,0:T(8,128)(2,1)} %bitcast.29), calls=%async_computation.5 | async-start | bytes 4194304 | tf_op jit(solution)/shard_map/all_to_all | solution.py:250
  240.3 12.4 %collective-permute-start.15 = (bf16[32,2,128,128]{3,2,1,0:T(8,128)(2,1)}, bf16[32,2,128,128]{3,2,1,0:T(8,128)(2,1)}, u32[]{:S(2)}, u32[]{:S(2)}) collective-permute-start(bf16[32,2,128,128]{3,2,1,0:T(8,128)(2,1)} %all-to-all-done.4.refs_4_.refs_1_), channel_id=1, source_target_pairs={{0,4},{4,0},{1,5},{5,1},{2,6},{6,2},{3,7},{7,3},{8,12},{12,8},{9,1... | collective-permute-start | bytes 6291464 | tf_op jit(solution)/shard_map/ppermute | solution.py:252
  252.7 4.1 collective-permute-done.15.refs_5_
  256.8 6.0 %spread.10 = bf16[768,128]{1,0:T(8,128)(2,1)} custom-call(s32[72]{0:T(128)} %reshape.195.index_ref, s32[1]{0:T(128)} %bitcast.core_ref, bf16[6,12,128,128]{3,2,1,0:T(8,128)(2,1)} %tiles_ref.15, f32[768,128]{1,0:T(8,128)} %broadcast_in_dim.56.weight_ref, f32[768,128]{1,0:T(8,128)} %get-tuple-element.14.anchor_ref, bf16[6,128,128]{2,1,0:T(8,128)(2,1)} %bitcast.47, ...), custom_call_target="tpu_custom_call" | custom-call | flops 301989888 | bytes 5242880 | tf_op jit(solution)/shard_map/spread/pallas_call | solution.py:192
  265.4 5.5 %collective-permute-done.16.refs_1_ = bf16[6,128,128]{2,1,0:T(8,128)(2,1)S(1)} collective-permute-done((bf16[6,128,128]{2,1,0:T(8,128)(2,1)}, bf16[6,128,128]{2,1,0:T(8,128)(2,1)S(1)}, u32[]{:S(2)}, u32[]{:S(2)}) %collective-permute-start.16) | collective-permute-done | bytes 196640 | tf_op jit(solution)/shard_map/ppermute | solution.py:243
  277.0 3.6 reply.12.refs_0_
  281.9 10.0 %all-to-all-start.6 = ((bf16[32,2,128,128]{3,2,1,0:T(8,128)(2,1)}), bf16[32,2,128,128]{3,2,1,0:T(8,128)(2,1)}, u32[]{:S(2)}, u32[]{:S(2)}) async-start(bf16[32,2,128,128]{3,2,1,0:T(8,128)(2,1)} %bitcast.25), calls=%async_computation.6 | async-start | bytes 4194304 | tf_op jit(solution)/shard_map/all_to_all | solution.py:250
  291.9 11.5 %collective-permute-start.28 = (bf16[32,2,128,128]{3,2,1,0:T(8,128)(2,1)S(1)}, bf16[32,2,128,128]{3,2,1,0:T(8,128)(2,1)}, u32[]{:S(2)}, u32[]{:S(2)}) collective-permute-start(bf16[32,2,128,128]{3,2,1,0:T(8,128)(2,1)S(1)} %copy-done.4), channel_id=1, source_target_pairs={{0,4},{4,0},{1,5},{5,1},{2,6},{6,2},{3,7},{7,3},{8,12},{12,8},{9,1... | collective-permute-start | bytes 6291464 | tf_op jit(solution)/shard_map/ppermute | solution.py:252
  303.4 3.9 collective-permute-done.28.refs_5_
  307.4 6.0 %spread.13 = bf16[768,128]{1,0:T(8,128)(2,1)} custom-call(s32[72]{0:T(128)} %reshape.195.index_ref, s32[1]{0:T(128)} %bitcast.core_ref, bf16[6,12,128,128]{3,2,1,0:T(8,128)(2,1)} %tiles_ref.15, f32[768,128]{1,0:T(8,128)} %broadcast_in_dim.56.weight_ref, f32[768,128]{1,0:T(8,128)} %get-tuple-element.13.anchor_ref, bf16[6,128,128]{2,1,0:T(8,128)(2,1)} %bitcast.57, ...), custom_call_target="tpu_custom_call" | custom-call | flops 301989888 | bytes 5242880 | tf_op jit(solution)/shard_map/spread/pallas_call | solution.py:192
  316.1 5.4 %collective-permute-done.29.refs_1_ = bf16[6,128,128]{2,1,0:T(8,128)(2,1)S(1)} collective-permute-done((bf16[6,128,128]{2,1,0:T(8,128)(2,1)}, bf16[6,128,128]{2,1,0:T(8,128)(2,1)S(1)}, u32[]{:S(2)}, u32[]{:S(2)}) %collective-permute-start.29) | collective-permute-done | bytes 196640 | tf_op jit(solution)/shard_map/ppermute | solution.py:243
  328.1 3.5 reply.15.refs_0_
  333.8 7.7 %all-to-all-start.8 = ((bf16[32,2,128,128]{3,2,1,0:T(8,128)(2,1)}), bf16[32,2,128,128]{3,2,1,0:T(8,128)(2,1)S(1)}, u32[]{:S(2)}, u32[]{:S(2)}) async-start(bf16[32,2,128,128]{3,2,1,0:T(8,128)(2,1)} %bitcast.26), calls=%async_computation.8 | async-start | bytes 4194304 | tf_op jit(solution)/shard_map/all_to_all | solution.py:250
  341.5 13.1 %collective-permute-start.23 = (bf16[32,2,128,128]{3,2,1,0:T(8,128)(2,1)}, bf16[32,2,128,128]{3,2,1,0:T(8,128)(2,1)}, u32[]{:S(2)}, u32[]{:S(2)}) collective-permute-start(bf16[32,2,128,128]{3,2,1,0:T(8,128)(2,1)} %all-to-all-done.6.refs_4_.refs_1_), channel_id=1, source_target_pairs={{0,4},{4,0},{1,5},{5,1},{2,6},{6,2},{3,7},{7,3},{8,12},{12,8},{9,1... | collective-permute-start | bytes 6291464 | tf_op jit(solution)/shard_map/ppermute | solution.py:252
  354.6 4.1 collective-permute-done.23.refs_5_
  358.7 6.0 %spread.12 = bf16[768,128]{1,0:T(8,128)(2,1)} custom-call(s32[72]{0:T(128)} %reshape.195.index_ref, s32[1]{0:T(128)} %bitcast.core_ref, bf16[6,12,128,128]{3,2,1,0:T(8,128)(2,1)} %tiles_ref.15, f32[768,128]{1,0:T(8,128)} %broadcast_in_dim.56.weight_ref, f32[768,128]{1,0:T(8,128)} %get-tuple-element.14.anchor_ref, bf16[6,128,128]{2,1,0:T(8,128)(2,1)} %bitcast.52, ...), custom_call_target="tpu_custom_call" | custom-call | flops 301989888 | bytes 5242880 | tf_op jit(solution)/shard_map/spread/pallas_call | solution.py:192
  367.4 5.4 %collective-permute-done.24.refs_1_ = bf16[6,128,128]{2,1,0:T(8,128)(2,1)S(1)} collective-permute-done((bf16[6,128,128]{2,1,0:T(8,128)(2,1)}, bf16[6,128,128]{2,1,0:T(8,128)(2,1)S(1)}, u32[]{:S(2)}, u32[]{:S(2)}) %collective-permute-start.24) | collective-permute-done | bytes 196640 | tf_op jit(solution)/shard_map/ppermute | solution.py:243
  379.7 3.5 reply.14
  383.2 9.8 %all-to-all-start.7 = ((bf16[32,2,128,128]{3,2,1,0:T(8,128)(2,1)}), bf16[32,2,128,128]{3,2,1,0:T(8,128)(2,1)}, u32[]{:S(2)}, u32[]{:S(2)}) async-start(bf16[32,2,128,128]{3,2,1,0:T(8,128)(2,1)} %bitcast.32), calls=%async_computation.7 | async-start | bytes 4194304 | tf_op jit(solution)/shard_map/all_to_all | solution.py:250
  393.1 5.3 %collective-permute-start.32 = (bf16[32,2,128,128]{3,2,1,0:T(8,128)(2,1)S(1)}, bf16[32,2,128,128]{3,2,1,0:T(8,128)(2,1)}, u32[]{:S(2)}, u32[]{:S(2)}) collective-permute-start(bf16[32,2,128,128]{3,2,1,0:T(8,128)(2,1)S(1)} %all-to-all-done.8.refs_4_), channel_id=1, source_target_pairs={{0,4},{4,0},{1,5},{5,1},{2,6},{6,2},{3,7},{7,3},{8,12},{12,8},{9,1... | collective-permute-start | bytes 6291464 | tf_op jit(solution)/shard_map/ppermute | solution.py:252
  398.4 43.5 %all-to-all-done.7.refs_4_ = bf16[32,2,128,128]{3,2,1,0:T(8,128)(2,1)} async-done(((bf16[32,2,128,128]{3,2,1,0:T(8,128)(2,1)}), bf16[32,2,128,128]{3,2,1,0:T(8,128)(2,1)}, u32[]{:S(2)}, u32[]{:S(2)}) %all-to-all-start.7) | async-done | bytes 2097184 | tf_op jit(solution)/shard_map/all_to_all | solution.py:250
  444.2 6.1 %spread.14.refs_6_ = f32[768,128]{1,0:T(8,128)} custom-call(s32[72]{0:T(128)} %reshape.195.index_ref, s32[1]{0:T(128)} %bitcast.core_ref, bf16[6,12,128,128]{3,2,1,0:T(8,128)(2,1)} %tiles_ref.15, f32[768,128]{1,0:T(8,128)} %broadcast_in_dim.56.weight_ref, f32[768,128]{1,0:T(8,128)} %get-tuple-element.13.anchor_ref, bf16[6,128,128]{2,1,0:T(8,128)(2,1)} %bitcast.37, ...), custom_call_target="tpu_custom_call" | custom-call | flops 301989888 | bytes 5242880 | tf_op jit(solution)/shard_map/spread/pallas_call | solution.py:192
  450.4 5.7 %spread.15 = f32[768,256]{1,0:T(8,128)} custom-call(s32[72]{0:T(128)} %reshape.195.index_ref, s32[1]{0:T(128)} %bitcast.core_ref, bf16[6,12,128,128]{3,2,1,0:T(8,128)(2,1)} %tiles_ref.15, f32[768,128]{1,0:T(8,128)} %broadcast_in_dim.56.weight_ref, f32[768,128]{1,0:T(8,128)} %get-tuple-element.14.anchor_ref, bf16[6,128,128]{2,1,0:T(8,128)(2,1)} %bitcast.62, ...), custom_call_target="tpu_custom_call" | custom-call | flops 301989888 | bytes 5242880 | tf_op jit(solution)/shard_map/spread/pallas_call | solution.py:192
  (142 shorter events, 91.6 us)
Async XLA Ops:
  3.3 28.6 %collective-permute-start.10 = (bf16[6,128,128]{2,1,0:T(8,128)(2,1)}, bf16[6,128,128]{2,1,0:T(8,128)(2,1)S(1)}, u32[]{:S(2)}, u32[]{:S(2)}) collective-permute-start(bf16[6,128,128]{2,1,0:T(8,128)(2,1)} %bitcast.76), channel_id=1, source_target_pairs={{3,0},{0,1},{1,2},{2,3},{7,4},{4,5},{5,6},{6,7},{11,8},{8,9},{9,10... | collective-permute-start | bytes 589832 | tf_op jit(solution)/shard_map/ppermute | solution.py:243
  4.8 27.2 %collective-permute-start.8 = (bf16[6,128,128]{2,1,0:T(8,128)(2,1)}, bf16[6,128,128]{2,1,0:T(8,128)(2,1)S(1)}, u32[]{:S(2)}, u32[]{:S(2)}) collective-permute-start(bf16[6,128,128]{2,1,0:T(8,128)(2,1)} %bitcast.77), channel_id=1, source_target_pairs={{1,0},{2,1},{3,2},{0,3},{5,4},{6,5},{7,6},{4,7},{9,8},{10,9},{11,1... | collective-permute-start | bytes 589832 | tf_op jit(solution)/shard_map/ppermute | solution.py:243
  6.5 25.4 %collective-permute-start.9 = (bf16[6,128,128]{2,1,0:T(8,128)(2,1)}, bf16[6,128,128]{2,1,0:T(8,128)(2,1)S(1)}, u32[]{:S(2)}, u32[]{:S(2)}) collective-permute-start(bf16[6,128,128]{2,1,0:T(8,128)(2,1)} %bitcast.78), channel_id=1, source_target_pairs={{2,0},{3,1},{0,2},{1,3},{6,4},{7,5},{4,6},{5,7},{10,8},{11,9},{8,1... | collective-permute-start | bytes 589832 | tf_op jit(solution)/shard_map/ppermute | solution.py:243
  9.5 1.3 collective-permute-start.3
  11.7 20.3 %all-to-all-start = ((s32[32,1,128]{2,1,0:T(1,128)}), s32[32,1,128]{2,1,0:T(1,128)S(1)}, u32[]{:S(2)}, u32[]{:S(2)}) async-start(s32[32,1,128]{2,1,0:T(1,128)} %broadcast_select_fusion), calls=%async_computation | async-start | bytes 32768 | tf_op jit(solution)/shard_map/all_to_all | solution.py:39
  36.3 45.1 %all-to-all-start.2 = ((bf16[32,2,128,128]{3,2,1,0:T(8,128)(2,1)}), bf16[32,2,128,128]{3,2,1,0:T(8,128)(2,1)S(1)}, u32[]{:S(2)}, u32[]{:S(2)}) async-start(bf16[32,2,128,128]{3,2,1,0:T(8,128)(2,1)} %bitcast.30), calls=%async_computation.2 | async-start | bytes 4194304 | tf_op jit(solution)/shard_map/all_to_all | solution.py:250
  41.5 5.7 %collective-permute-start = (bf16[6,128,128]{2,1,0:T(8,128)(2,1)S(1)}, bf16[6,128,128]{2,1,0:T(8,128)(2,1)S(1)}, u32[]{:S(2)}, u32[]{:S(2)}) collective-permute-start(bf16[6,128,128]{2,1,0:T(8,128)(2,1)S(1)} %bitcast.73), channel_id=1, source_target_pairs={{1,0},{2,1},{3,2},{0,3},{5,4},{6,5},{7,6},{4,7},{9,8},{10,9},{11,1... | collective-permute-start | bytes 589832 | tf_op jit(solution)/shard_map/ppermute | solution.py:243
  42.8 7.3 %collective-permute-start.1 = (bf16[6,128,128]{2,1,0:T(8,128)(2,1)S(1)}, bf16[6,128,128]{2,1,0:T(8,128)(2,1)S(1)}, u32[]{:S(2)}, u32[]{:S(2)}) collective-permute-start(bf16[6,128,128]{2,1,0:T(8,128)(2,1)S(1)} %bitcast.74), channel_id=1, source_target_pairs={{2,0},{3,1},{0,2},{1,3},{6,4},{7,5},{4,6},{5,7},{10,8},{11,9},{8,1... | collective-permute-start | bytes 589832 | tf_op jit(solution)/shard_map/ppermute | solution.py:243
  44.3 7.8 %collective-permute-start.2 = (bf16[6,128,128]{2,1,0:T(8,128)(2,1)S(1)}, bf16[6,128,128]{2,1,0:T(8,128)(2,1)S(1)}, u32[]{:S(2)}, u32[]{:S(2)}) collective-permute-start(bf16[6,128,128]{2,1,0:T(8,128)(2,1)S(1)} %bitcast.75), channel_id=1, source_target_pairs={{3,0},{0,1},{1,2},{2,3},{7,4},{4,5},{5,6},{6,7},{11,8},{8,9},{9,10... | collective-permute-start | bytes 589832 | tf_op jit(solution)/shard_map/ppermute | solution.py:243
  82.8 17.9 %copy-start = (bf16[6,12,128,128]{3,2,1,0:T(8,128)(2,1)S(1)}, bf16[6,12,128,128]{3,2,1,0:T(8,128)(2,1)}, u32[]{:S(2)}) copy-start(bf16[6,12,128,128]{3,2,1,0:T(8,128)(2,1)} %tiles_ref.15) | copy-start | bytes 7077892
  82.8 46.6 %all-to-all-start.1 = ((bf16[32,2,128,128]{3,2,1,0:T(8,128)(2,1)}), bf16[32,2,128,128]{3,2,1,0:T(8,128)(2,1)}, u32[]{:S(2)}, u32[]{:S(2)}) async-start(bf16[32,2,128,128]{3,2,1,0:T(8,128)(2,1)} %bitcast.31), calls=%async_computation.1 | async-start | bytes 4194304 | tf_op jit(solution)/shard_map/all_to_all | solution.py:250
  87.9 13.2 %copy-start.8 = (f32[768,256]{1,0:T(8,128)S(1)}, f32[768,256]{1,0:T(8,128)}, u32[]{:S(2)}) copy-start(f32[768,256]{1,0:T(8,128)} %get-tuple-element.8) | copy-start | bytes 2359300
  87.9 16.3 %collective-permute-start.11 = (bf16[32,2,128,128]{3,2,1,0:T(8,128)(2,1)}, bf16[32,2,128,128]{3,2,1,0:T(8,128)(2,1)}, u32[]{:S(2)}, u32[]{:S(2)}) collective-permute-start(bf16[32,2,128,128]{3,2,1,0:T(8,128)(2,1)} %copy-done.6), channel_id=1, source_target_pairs={{0,4},{4,0},{1,5},{5,1},{2,6},{6,2},{3,7},{7,3},{8,12},{12,8},{9,1... | collective-permute-start | bytes 6291464 | tf_op jit(solution)/shard_map/ppermute | solution.py:252
  111.1 8.1 %collective-permute-start.12 = (bf16[6,128,128]{2,1,0:T(8,128)(2,1)}, bf16[6,128,128]{2,1,0:T(8,128)(2,1)S(1)}, u32[]{:S(2)}, u32[]{:S(2)}) collective-permute-start(bf16[6,128,128]{2,1,0:T(8,128)(2,1)} %bitcast.38), channel_id=1, source_target_pairs={{1,0},{2,1},{3,2},{0,3},{5,4},{6,5},{7,6},{4,7},{9,8},{10,9},{11,1... | collective-permute-start | bytes 589832 | tf_op jit(solution)/shard_map/ppermute | solution.py:243
  112.3 9.5 %collective-permute-start.13 = (bf16[6,128,128]{2,1,0:T(8,128)(2,1)}, bf16[6,128,128]{2,1,0:T(8,128)(2,1)S(1)}, u32[]{:S(2)}, u32[]{:S(2)}) collective-permute-start(bf16[6,128,128]{2,1,0:T(8,128)(2,1)} %bitcast.39), channel_id=1, source_target_pairs={{2,0},{3,1},{0,2},{1,3},{6,4},{7,5},{4,6},{5,7},{10,8},{11,9},{8,1... | collective-permute-start | bytes 589832 | tf_op jit(solution)/shard_map/ppermute | solution.py:243
  113.9 11.3 %collective-permute-start.14 = (bf16[6,128,128]{2,1,0:T(8,128)(2,1)}, bf16[6,128,128]{2,1,0:T(8,128)(2,1)S(1)}, u32[]{:S(2)}, u32[]{:S(2)}) collective-permute-start(bf16[6,128,128]{2,1,0:T(8,128)(2,1)} %bitcast.40), channel_id=1, source_target_pairs={{3,0},{0,1},{1,2},{2,3},{7,4},{4,5},{5,6},{6,7},{11,8},{8,9},{9,10... | collective-permute-start | bytes 589832 | tf_op jit(solution)/shard_map/ppermute | solution.py:243
  129.4 53.8 %all-to-all-start.3 = ((bf16[32,2,128,128]{3,2,1,0:T(8,128)(2,1)}), bf16[32,2,128,128]{3,2,1,0:T(8,128)(2,1)S(1)}, u32[]{:S(2)}, u32[]{:S(2)}) async-start(bf16[32,2,128,128]{3,2,1,0:T(8,128)(2,1)} %bitcast.27), calls=%async_computation.3 | async-start | bytes 4194304 | tf_op jit(solution)/shard_map/all_to_all | solution.py:250
  139.2 14.7 %collective-permute-start.4 = (bf16[32,2,128,128]{3,2,1,0:T(8,128)(2,1)}, bf16[32,2,128,128]{3,2,1,0:T(8,128)(2,1)}, u32[]{:S(2)}, u32[]{:S(2)}) collective-permute-start(bf16[32,2,128,128]{3,2,1,0:T(8,128)(2,1)} %all-to-all-done.1.refs_4_.refs_1_), channel_id=1, source_target_pairs={{0,4},{4,0},{1,5},{5,1},{2,6},{6,2},{3,7},{7,3},{8,12},{12,8},{9,1... | collective-permute-start | bytes 6291464 | tf_op jit(solution)/shard_map/ppermute | solution.py:252
  160.0 8.2 %collective-permute-start.5 = (bf16[6,128,128]{2,1,0:T(8,128)(2,1)}, bf16[6,128,128]{2,1,0:T(8,128)(2,1)S(1)}, u32[]{:S(2)}, u32[]{:S(2)}) collective-permute-start(bf16[6,128,128]{2,1,0:T(8,128)(2,1)} %bitcast.43), channel_id=1, source_target_pairs={{1,0},{2,1},{3,2},{0,3},{5,4},{6,5},{7,6},{4,7},{9,8},{10,9},{11,1... | collective-permute-start | bytes 589832 | tf_op jit(solution)/shard_map/ppermute | solution.py:243
  161.4 9.5 %collective-permute-start.6 = (bf16[6,128,128]{2,1,0:T(8,128)(2,1)}, bf16[6,128,128]{2,1,0:T(8,128)(2,1)S(1)}, u32[]{:S(2)}, u32[]{:S(2)}) collective-permute-start(bf16[6,128,128]{2,1,0:T(8,128)(2,1)} %bitcast.44), channel_id=1, source_target_pairs={{2,0},{3,1},{0,2},{1,3},{6,4},{7,5},{4,6},{5,7},{10,8},{11,9},{8,1... | collective-permute-start | bytes 589832 | tf_op jit(solution)/shard_map/ppermute | solution.py:243
  162.9 11.3 %collective-permute-start.7 = (bf16[6,128,128]{2,1,0:T(8,128)(2,1)}, bf16[6,128,128]{2,1,0:T(8,128)(2,1)S(1)}, u32[]{:S(2)}, u32[]{:S(2)}) collective-permute-start(bf16[6,128,128]{2,1,0:T(8,128)(2,1)} %bitcast.45), channel_id=1, source_target_pairs={{3,0},{0,1},{1,2},{2,3},{7,4},{4,5},{5,6},{6,7},{11,8},{8,9},{9,10... | collective-permute-start | bytes 589832 | tf_op jit(solution)/shard_map/ppermute | solution.py:243
  168.2 6.0 %copy-start.21 = (bf16[6,128,128]{2,1,0:T(8,128)(2,1)}, bf16[6,128,128]{2,1,0:T(8,128)(2,1)S(1)}, u32[]{:S(2)}) copy-start(bf16[6,128,128]{2,1,0:T(8,128)(2,1)S(1)} %collective-permute-done.5.refs_1_) | copy-start | bytes 589828
  184.6 46.7 %all-to-all-start.4 = ((bf16[32,2,128,128]{3,2,1,0:T(8,128)(2,1)}), bf16[32,2,128,128]{3,2,1,0:T(8,128)(2,1)}, u32[]{:S(2)}, u32[]{:S(2)}) async-start(bf16[32,2,128,128]{3,2,1,0:T(8,128)(2,1)} %bitcast.28), calls=%async_computation.4 | async-start | bytes 4194304 | tf_op jit(solution)/shard_map/all_to_all | solution.py:250
  190.3 16.0 %collective-permute-start.19 = (bf16[32,2,128,128]{3,2,1,0:T(8,128)(2,1)S(1)}, bf16[32,2,128,128]{3,2,1,0:T(8,128)(2,1)}, u32[]{:S(2)}, u32[]{:S(2)}) collective-permute-start(bf16[32,2,128,128]{3,2,1,0:T(8,128)(2,1)S(1)} %copy-done.2), channel_id=1, source_target_pairs={{0,4},{4,0},{1,5},{5,1},{2,6},{6,2},{3,7},{7,3},{8,12},{12,8},{9,1... | collective-permute-start | bytes 6291464 | tf_op jit(solution)/shard_map/ppermute | solution.py:252
  212.3 8.1 %collective-permute-start.20 = (bf16[6,128,128]{2,1,0:T(8,128)(2,1)}, bf16[6,128,128]{2,1,0:T(8,128)(2,1)S(1)}, u32[]{:S(2)}, u32[]{:S(2)}) collective-permute-start(bf16[6,128,128]{2,1,0:T(8,128)(2,1)} %bitcast.53), channel_id=1, source_target_pairs={{1,0},{2,1},{3,2},{0,3},{5,4},{6,5},{7,6},{4,7},{9,8},{10,9},{11,1... | collective-permute-start | bytes 589832 | tf_op jit(solution)/shard_map/ppermute | solution.py:243
  213.4 9.5 %collective-permute-start.21 = (bf16[6,128,128]{2,1,0:T(8,128)(2,1)}, bf16[6,128,128]{2,1,0:T(8,128)(2,1)S(1)}, u32[]{:S(2)}, u32[]{:S(2)}) collective-permute-start(bf16[6,128,128]{2,1,0:T(8,128)(2,1)} %bitcast.54), channel_id=1, source_target_pairs={{2,0},{3,1},{0,2},{1,3},{6,4},{7,5},{4,6},{5,7},{10,8},{11,9},{8,1... | collective-permute-start | bytes 589832 | tf_op jit(solution)/shard_map/ppermute | solution.py:243
  214.6 11.7 %collective-permute-start.22 = (bf16[6,128,128]{2,1,0:T(8,128)(2,1)}, bf16[6,128,128]{2,1,0:T(8,128)(2,1)S(1)}, u32[]{:S(2)}, u32[]{:S(2)}) collective-permute-start(bf16[6,128,128]{2,1,0:T(8,128)(2,1)} %bitcast.55), channel_id=1, source_target_pairs={{3,0},{0,1},{1,2},{2,3},{7,4},{4,5},{5,6},{6,7},{11,8},{8,9},{9,10... | collective-permute-start | bytes 589832 | tf_op jit(solution)/shard_map/ppermute | solution.py:243
  231.4 49.2 %all-to-all-start.5 = ((bf16[32,2,128,128]{3,2,1,0:T(8,128)(2,1)}), bf16[32,2,128,128]{3,2,1,0:T(8,128)(2,1)S(1)}, u32[]{:S(2)}, u32[]{:S(2)}) async-start(bf16[32,2,128,128]{3,2,1,0:T(8,128)(2,1)} %bitcast.29), calls=%async_computation.5 | async-start | bytes 4194304 | tf_op jit(solution)/shard_map/all_to_all | solution.py:250
  240.3 16.6 %collective-permute-start.15 = (bf16[32,2,128,128]{3,2,1,0:T(8,128)(2,1)}, bf16[32,2,128,128]{3,2,1,0:T(8,128)(2,1)}, u32[]{:S(2)}, u32[]{:S(2)}) collective-permute-start(bf16[32,2,128,128]{3,2,1,0:T(8,128)(2,1)} %all-to-all-done.4.refs_4_.refs_1_), channel_id=1, source_target_pairs={{0,4},{4,0},{1,5},{5,1},{2,6},{6,2},{3,7},{7,3},{8,12},{12,8},{9,1... | collective-permute-start | bytes 6291464 | tf_op jit(solution)/shard_map/ppermute | solution.py:252
  262.9 8.1 %collective-permute-start.16 = (bf16[6,128,128]{2,1,0:T(8,128)(2,1)}, bf16[6,128,128]{2,1,0:T(8,128)(2,1)S(1)}, u32[]{:S(2)}, u32[]{:S(2)}) collective-permute-start(bf16[6,128,128]{2,1,0:T(8,128)(2,1)} %bitcast.48), channel_id=1, source_target_pairs={{1,0},{2,1},{3,2},{0,3},{5,4},{6,5},{7,6},{4,7},{9,8},{10,9},{11,1... | collective-permute-start | bytes 589832 | tf_op jit(solution)/shard_map/ppermute | solution.py:243
  263.5 9.5 %collective-permute-start.17 = (bf16[6,128,128]{2,1,0:T(8,128)(2,1)}, bf16[6,128,128]{2,1,0:T(8,128)(2,1)S(1)}, u32[]{:S(2)}, u32[]{:S(2)}) collective-permute-start(bf16[6,128,128]{2,1,0:T(8,128)(2,1)} %bitcast.49), channel_id=1, source_target_pairs={{2,0},{3,1},{0,2},{1,3},{6,4},{7,5},{4,6},{5,7},{10,8},{11,9},{8,1... | collective-permute-start | bytes 589832 | tf_op jit(solution)/shard_map/ppermute | solution.py:243
  264.6 11.7 %collective-permute-start.18 = (bf16[6,128,128]{2,1,0:T(8,128)(2,1)}, bf16[6,128,128]{2,1,0:T(8,128)(2,1)S(1)}, u32[]{:S(2)}, u32[]{:S(2)}) collective-permute-start(bf16[6,128,128]{2,1,0:T(8,128)(2,1)} %bitcast.50), channel_id=1, source_target_pairs={{3,0},{0,1},{1,2},{2,3},{7,4},{4,5},{5,6},{6,7},{11,8},{8,9},{9,10... | collective-permute-start | bytes 589832 | tf_op jit(solution)/shard_map/ppermute | solution.py:243
  281.9 10.0 %copy-start.4 = (bf16[32,2,128,128]{3,2,1,0:T(8,128)(2,1)S(1)}, bf16[32,2,128,128]{3,2,1,0:T(8,128)(2,1)}, u32[]{:S(2)}) copy-start(bf16[32,2,128,128]{3,2,1,0:T(8,128)(2,1)} %copy-done.3) | copy-start | bytes 6291460
  281.9 51.9 %all-to-all-start.6 = ((bf16[32,2,128,128]{3,2,1,0:T(8,128)(2,1)}), bf16[32,2,128,128]{3,2,1,0:T(8,128)(2,1)}, u32[]{:S(2)}, u32[]{:S(2)}) async-start(bf16[32,2,128,128]{3,2,1,0:T(8,128)(2,1)} %bitcast.25), calls=%async_computation.6 | async-start | bytes 4194304 | tf_op jit(solution)/shard_map/all_to_all | solution.py:250
  291.9 15.4 %collective-permute-start.28 = (bf16[32,2,128,128]{3,2,1,0:T(8,128)(2,1)S(1)}, bf16[32,2,128,128]{3,2,1,0:T(8,128)(2,1)}, u32[]{:S(2)}, u32[]{:S(2)}) collective-permute-start(bf16[32,2,128,128]{3,2,1,0:T(8,128)(2,1)S(1)} %copy-done.4), channel_id=1, source_target_pairs={{0,4},{4,0},{1,5},{5,1},{2,6},{6,2},{3,7},{7,3},{8,12},{12,8},{9,1... | collective-permute-start | bytes 6291464 | tf_op jit(solution)/shard_map/ppermute | solution.py:252
  313.4 8.1 %collective-permute-start.29 = (bf16[6,128,128]{2,1,0:T(8,128)(2,1)}, bf16[6,128,128]{2,1,0:T(8,128)(2,1)S(1)}, u32[]{:S(2)}, u32[]{:S(2)}) collective-permute-start(bf16[6,128,128]{2,1,0:T(8,128)(2,1)} %bitcast.33), channel_id=1, source_target_pairs={{1,0},{2,1},{3,2},{0,3},{5,4},{6,5},{7,6},{4,7},{9,8},{10,9},{11,1... | collective-permute-start | bytes 589832 | tf_op jit(solution)/shard_map/ppermute | solution.py:243
  314.6 9.5 %collective-permute-start.30 = (bf16[6,128,128]{2,1,0:T(8,128)(2,1)}, bf16[6,128,128]{2,1,0:T(8,128)(2,1)S(1)}, u32[]{:S(2)}, u32[]{:S(2)}) collective-permute-start(bf16[6,128,128]{2,1,0:T(8,128)(2,1)} %bitcast.34), channel_id=1, source_target_pairs={{2,0},{3,1},{0,2},{1,3},{6,4},{7,5},{4,6},{5,7},{10,8},{11,9},{8,1... | collective-permute-start | bytes 589832 | tf_op jit(solution)/shard_map/ppermute | solution.py:243
  315.2 12.2 %collective-permute-start.31 = (bf16[6,128,128]{2,1,0:T(8,128)(2,1)}, bf16[6,128,128]{2,1,0:T(8,128)(2,1)S(1)}, u32[]{:S(2)}, u32[]{:S(2)}) collective-permute-start(bf16[6,128,128]{2,1,0:T(8,128)(2,1)} %bitcast.35), channel_id=1, source_target_pairs={{3,0},{0,1},{1,2},{2,3},{7,4},{4,5},{5,6},{6,7},{11,8},{8,9},{9,10... | collective-permute-start | bytes 589832 | tf_op jit(solution)/shard_map/ppermute | solution.py:243
  333.8 49.4 %all-to-all-start.8 = ((bf16[32,2,128,128]{3,2,1,0:T(8,128)(2,1)}), bf16[32,2,128,128]{3,2,1,0:T(8,128)(2,1)S(1)}, u32[]{:S(2)}, u32[]{:S(2)}) async-start(bf16[32,2,128,128]{3,2,1,0:T(8,128)(2,1)} %bitcast.26), calls=%async_computation.8 | async-start | bytes 4194304 | tf_op jit(solution)/shard_map/all_to_all | solution.py:250
  341.5 17.2 %collective-permute-start.23 = (bf16[32,2,128,128]{3,2,1,0:T(8,128)(2,1)}, bf16[32,2,128,128]{3,2,1,0:T(8,128)(2,1)}, u32[]{:S(2)}, u32[]{:S(2)}) collective-permute-start(bf16[32,2,128,128]{3,2,1,0:T(8,128)(2,1)} %all-to-all-done.6.refs_4_.refs_1_), channel_id=1, source_target_pairs={{0,4},{4,0},{1,5},{5,1},{2,6},{6,2},{3,7},{7,3},{8,12},{12,8},{9,1... | collective-permute-start | bytes 6291464 | tf_op jit(solution)/shard_map/ppermute | solution.py:252
  364.8 8.1 %collective-permute-start.24 = (bf16[6,128,128]{2,1,0:T(8,128)(2,1)}, bf16[6,128,128]{2,1,0:T(8,128)(2,1)S(1)}, u32[]{:S(2)}, u32[]{:S(2)}) collective-permute-start(bf16[6,128,128]{2,1,0:T(8,128)(2,1)} %bitcast.58), channel_id=1, source_target_pairs={{1,0},{2,1},{3,2},{0,3},{5,4},{6,5},{7,6},{4,7},{9,8},{10,9},{11,1... | collective-permute-start | bytes 589832 | tf_op jit(solution)/shard_map/ppermute | solution.py:243
  366.4 9.5 %collective-permute-start.25 = (bf16[6,128,128]{2,1,0:T(8,128)(2,1)}, bf16[6,128,128]{2,1,0:T(8,128)(2,1)S(1)}, u32[]{:S(2)}, u32[]{:S(2)}) collective-permute-start(bf16[6,128,128]{2,1,0:T(8,128)(2,1)} %bitcast.59), channel_id=1, source_target_pairs={{2,0},{3,1},{0,2},{1,3},{6,4},{7,5},{4,6},{5,7},{10,8},{11,9},{8,1... | collective-permute-start | bytes 589832 | tf_op jit(solution)/shard_map/ppermute | solution.py:243
  366.6 12.4 %collective-permute-start.26 = (bf16[6,128,128]{2,1,0:T(8,128)(2,1)}, bf16[6,128,128]{2,1,0:T(8,128)(2,1)S(1)}, u32[]{:S(2)}, u32[]{:S(2)}) collective-permute-start(bf16[6,128,128]{2,1,0:T(8,128)(2,1)} %bitcast.60), channel_id=1, source_target_pairs={{3,0},{0,1},{1,2},{2,3},{7,4},{4,5},{5,6},{6,7},{11,8},{8,9},{9,10... | collective-permute-start | bytes 589832 | tf_op jit(solution)/shard_map/ppermute | solution.py:243
  372.8 6.2 %copy-start.31 = (bf16[6,128,128]{2,1,0:T(8,128)(2,1)}, bf16[6,128,128]{2,1,0:T(8,128)(2,1)S(1)}, u32[]{:S(2)}) copy-start(bf16[6,128,128]{2,1,0:T(8,128)(2,1)S(1)} %collective-permute-done.24.refs_1_) | copy-start | bytes 589828
  383.2 9.9 %copy-start.5 = (bf16[32,2,128,128]{3,2,1,0:T(8,128)(2,1)}, bf16[32,2,128,128]{3,2,1,0:T(8,128)(2,1)S(1)}, u32[]{:S(2)}) copy-start(bf16[32,2,128,128]{3,2,1,0:T(8,128)(2,1)S(1)} %all-to-all-done.8.refs_4_) | copy-start | bytes 6291460
  383.2 58.7 %all-to-all-start.7 = ((bf16[32,2,128,128]{3,2,1,0:T(8,128)(2,1)}), bf16[32,2,128,128]{3,2,1,0:T(8,128)(2,1)}, u32[]{:S(2)}, u32[]{:S(2)}) async-start(bf16[32,2,128,128]{3,2,1,0:T(8,128)(2,1)} %bitcast.32), calls=%async_computation.7 | async-start | bytes 4194304 | tf_op jit(solution)/shard_map/all_to_all | solution.py:250
  393.1 51.1 %collective-permute-start.32 = (bf16[32,2,128,128]{3,2,1,0:T(8,128)(2,1)S(1)}, bf16[32,2,128,128]{3,2,1,0:T(8,128)(2,1)}, u32[]{:S(2)}, u32[]{:S(2)}) collective-permute-start(bf16[32,2,128,128]{3,2,1,0:T(8,128)(2,1)S(1)} %all-to-all-done.8.refs_4_), channel_id=1, source_target_pairs={{0,4},{4,0},{1,5},{5,1},{2,6},{6,2},{3,7},{7,3},{8,12},{12,8},{9,1... | collective-permute-start | bytes 6291464 | tf_op jit(solution)/shard_map/ppermute | solution.py:252
  441.9 8.4 %collective-permute-start.27 = (bf16[32,2,128,128]{3,2,1,0:T(8,128)(2,1)}, bf16[32,2,128,128]{3,2,1,0:T(8,128)(2,1)}, u32[]{:S(2)}, u32[]{:S(2)}) collective-permute-start(bf16[32,2,128,128]{3,2,1,0:T(8,128)(2,1)} %all-to-all-done.7.refs_4_), channel_id=1, source_target_pairs={{0,4},{4,0},{1,5},{5,1},{2,6},{6,2},{3,7},{7,3},{8,12},{12,8},{9,1... | collective-permute-start | bytes 6291464 | tf_op jit(solution)/shard_map/ppermute | solution.py:252
  (28 other events, 71.9 us)
